TPU v7x, 32 devices: a whole 2x2x4 slice. The times are simulated.
32 devices in a mesh: gx: 2 (over x), gy: 2 (over core), gz: 8 (over z, y).
Axes of the slice: x: 2, y: 2, z: 4, core: 2. Of those that a mesh axis runs over, the one named last changes fastest.
Arguments:
- state_re: float32 [33554432], P(('gx', 'gy', 'gz')), may hold values from -6 to 6
- state_im: float32 [33554432], P(('gx', 'gy', 'gz')), may hold values from -6 to 6
Outputs:
- out_re: float32 [33554432], P(('gx', 'gy', 'gz'))
- out_im: float32 [33554432], P(('gx', 'gy', 'gz'))
- probability: float32 [33554432], P(('gx', 'gy', 'gz'))
All inputs are finite; a program needn't handle non-finite values.
Results may differ from a plain program's by a relative error of at most 0.000071.
Values sent between devices are 32-bit elements; how exact they have to be, the bound alone decides.
No kernel may reach another device: no remote copies, remote signals or barrier semaphores. Data moves between devices by JAX's collectives and lax.ppermute only.
A program may use at most 128 MiB of HBM per device.

v0:
```python
import math

import jax
import jax.numpy as jnp
from jax import lax
from jax.sharding import PartitionSpec as P


def bit_reverse(values, bits):
    result = values * 0
    for place in range(bits):
        result = result + (values >> place & 1) * (1 << bits - 1 - place)
    return result


def phases(product, modulus):
    reduced = product % modulus
    upper = (reduced // 4096).astype(jnp.float32)
    lower = (reduced % 4096).astype(jnp.float32)
    angle = upper * (2.0 * math.pi * 4096.0 / modulus) + lower * (2.0 * math.pi / modulus)
    return (jnp.cos(angle), jnp.sin(angle))


def table(count, bits):
    across = jnp.arange(count, dtype=jnp.int32)
    return phases(bit_reverse(across, bits)[:, None] * across[None, :], count)


def complex_mix(spec, tab, pair):
    cosine, sine = tab
    real_part, imag_part = pair

    def contract(left, right):
        return jnp.einsum(spec, left, right, precision=lax.Precision.HIGHEST)

    return (
        contract(cosine, real_part) - contract(sine, imag_part),
        contract(sine, real_part) + contract(cosine, imag_part),
    )


def twist(pair, turn):
    real_part, imag_part = pair
    cosine, sine = turn
    return (real_part * cosine - imag_part * sine, real_part * sine + imag_part * cosine)


def on_device(state_re, state_im):
    devices_all = lax.axis_size(("gx", "gy", "gz"))
    device_bits = devices_all.bit_length() - 1
    local_count = state_re.shape[0]
    columns = local_count // devices_all
    total = local_count * devices_all
    mixing = table(devices_all, device_bits)
    spread = jnp.stack(
        (state_re.reshape(devices_all, columns), state_im.reshape(devices_all, columns)), axis=0
    )
    stacked = lax.all_to_all(spread, ("gx", "gy", "gz"), split_axis=1, concat_axis=1, tiled=True)
    mixed = complex_mix("ed,dm->em", mixing, (stacked[0], stacked[1]))
    moved = jnp.stack(mixed, axis=0)
    returned = lax.all_to_all(moved, ("gx", "gy", "gz"), split_axis=1, concat_axis=1, tiled=True)
    back = (returned[0], returned[1])
    line = (back[0].reshape(local_count), back[1].reshape(local_count))
    owner = bit_reverse(lax.axis_index(("gx", "gy", "gz")), device_bits)
    positions = jnp.arange(local_count, dtype=jnp.int32)
    line = twist(line, phases(positions * owner, total))
    local_bits = local_count.bit_length() - 1
    first_bits = min(7, local_bits)
    third_bits = min(7, local_bits - first_bits)
    middle_bits = local_bits - first_bits - third_bits
    first_n = 1 << first_bits
    middle_n = 1 << middle_bits
    third_n = 1 << third_bits
    cube = (
        line[0].reshape(first_n, middle_n, third_n),
        line[1].reshape(first_n, middle_n, third_n),
    )
    cube = complex_mix("ra,abc->rbc", table(first_n, first_bits), cube)
    first_rev = bit_reverse(jnp.arange(first_n, dtype=jnp.int32), first_bits)[:, None, None]
    rest_index = (
        jnp.arange(middle_n, dtype=jnp.int32)[None, :, None] * third_n
        + jnp.arange(third_n, dtype=jnp.int32)[None, None, :]
    )
    cube = twist(cube, phases(first_rev * rest_index, local_count))
    cube = complex_mix("rb,abc->arc", table(middle_n, middle_bits), cube)
    middle_rev = bit_reverse(jnp.arange(middle_n, dtype=jnp.int32), middle_bits)[None, :, None]
    inner_index = jnp.arange(third_n, dtype=jnp.int32)[None, None, :]
    cube = twist(cube, phases(middle_rev * inner_index, middle_n * third_n))
    cube = complex_mix("rc,abc->abr", table(third_n, third_bits), cube)
    factor = 1.0 / math.sqrt(total)
    out_re = cube[0].reshape(local_count) * factor
    out_im = cube[1].reshape(local_count) * factor
    probability = out_re * out_re + out_im * out_im
    return (out_re, out_im, probability)


def solution(mesh):
    return jax.shard_map(
        on_device,
        mesh=mesh,
        in_specs=(P(("gx", "gy", "gz")), P(("gx", "gy", "gz"))),
        out_specs=(P(("gx", "gy", "gz")), P(("gx", "gy", "gz")), P(("gx", "gy", "gz"))),
        check_vma=False,
    )
```

profile of v0, /device:TPU:0, one launch (start us, length us, event | category | flops | bytes accessed | tf_op | source)
XLA Modules:
  0.0 652.8 jit_solution(14103493779315260491)
XLA Ops:
  0.6 10.0 %pad_maximum_fusion = f32[2,32,32768]{2,0,1:T(2,128)} fusion(f32[1,32,32768]{2,0,1:T(1,128)} %bitcast.73, f32[1,32,32768]{2,0,1:T(1,128)} %bitcast.74), kind=kLoop, calls=%fused_computation.4 | loop fusion | flops 2097152 | bytes 16777216 | tf_op jit(solution)/shard_map/stack | solution.py:55
  10.6 7.5 %all-to-all-start = ((f32[2,32,32768]{2,0,1:T(2,128)}), f32[2,32,32768]{2,0,1:T(2,128)}, u32[]{:S(2)}, u32[]{:S(2)}) async-start(f32[2,32,32768]{2,0,1:T(2,128)} %pad_maximum_fusion), calls=%async_computation | async-start | bytes 16777216 | tf_op jit(solution)/shard_map/all_to_all | solution.py:58
  18.1 189.8 %all-to-all-done = f32[2,32,32768]{2,0,1:T(2,128)} async-done(((f32[2,32,32768]{2,0,1:T(2,128)}), f32[2,32,32768]{2,0,1:T(2,128)}, u32[]{:S(2)}, u32[]{:S(2)}) %all-to-all-start) | async-done | bytes 8388640 | tf_op jit(solution)/shard_map/all_to_all | solution.py:58
  207.9 10.0 %fusion.383 = (f32[1,32,32768]{2,0,1:T(1,128)S(1)}, f32[1,32,32768]{2,0,1:T(1,128)S(1)}) fusion(f32[2,32,32768]{2,0,1:T(2,128)} %all-to-all-done), kind=kLoop, calls=%fused_computation.452 | loop fusion | bytes 16777216 | tf_op jit(solution)/shard_map/slice | solution.py:59
  217.9 6.0 fusion.18
  223.9 6.0 fusion.16
  229.9 6.8 %fusion.1 = f32[1,32,32768]{2,1,0:T(8,128)S(1)} fusion(f32[32,32768]{1,0:T(8,128)S(1)} %fusion.18, f32[1,32,32768]{2,0,1:T(1,128)S(1)} %get-tuple-element.9, s32[32]{0:T(128)S(1)} %fusion.161), kind=kOutput, calls=%fused_computation.3 | convolution fusion | flops 403738624 | bytes 12583040 | tf_op jit(solution)/shard_map/ed,dm->em/dot_general | solution.py:34
  236.7 6.4 fusion
  243.1 0.5 pad_maximum_fusion.1
  243.6 7.8 %copy.42 = f32[2,32,32768]{2,0,1:T(2,128)} copy(f32[2,32,32768]{2,1,0:T(8,128)S(1)} %pad_maximum_fusion.1) | data formatting | bytes 16777216 | tf_op jit(solution)/shard_map/stack | solution.py:60
  251.5 3.7 all-to-all-start.1
  255.2 0.1 iota_add_fusion
  255.3 0.2 fusion.134
  255.6 189.2 %all-to-all-done.1 = f32[2,32,32768]{2,0,1:T(2,128)} async-done(((f32[2,32,32768]{2,0,1:T(2,128)}), f32[2,32,32768]{2,0,1:T(2,128)}, u32[]{:S(2)}, u32[]{:S(2)}) %all-to-all-start.1) | async-done | bytes 8388640 | tf_op jit(solution)/shard_map/all_to_all | solution.py:61
  444.8 9.8 %fusion.382 = (f32[1,32,32768]{2,0,1:T(1,128)S(1)}, f32[1,32,32768]{2,0,1:T(1,128)S(1)}) fusion(f32[2,32,32768]{2,0,1:T(2,128)} %all-to-all-done.1), kind=kLoop, calls=%fused_computation.451 | loop fusion | bytes 16777216 | tf_op jit(solution)/shard_map/slice | solution.py:62
  454.6 27.3 %fusion.64 = f32[128,64,128]{2,0,1:T(8,128)S(1)} fusion(f32[128,64,128]{2,1,0:T(8,128)S(1)} %bitcast.79, f32[128,64,128]{2,1,0:T(8,128)S(1)} %bitcast.75, s32[]{:T(128)S(6)} %add.751, s32[128]{0:T(128)S(1)} %fusion.196), kind=kOutput, calls=%fused_computation.93 | convolution fusion | flops 1656291328 | bytes 12583428 | tf_op jit(solution)/shard_map/ra,abc->rbc/dot_general | solution.py:34
  482.0 27.6 %fusion.65 = f32[128,64,128]{2,0,1:T(8,128)S(1)} fusion(f32[128,64,128]{2,1,0:T(8,128)S(1)} %bitcast.80, f32[128,64,128]{2,1,0:T(8,128)S(1)} %bitcast.76, s32[]{:T(128)S(6)} %add.751, s32[128]{0:T(128)S(1)} %fusion.196), kind=kOutput, calls=%fused_computation.94 | convolution fusion | flops 1656291328 | bytes 12583428 | tf_op jit(solution)/shard_map/ra,abc->rbc/dot_general | solution.py:34
  509.5 27.8 %convolution_subtract_fusion.1 = f32[128,64,128]{2,0,1:T(8,128)S(1)} fusion(f32[128,64,128]{2,0,1:T(8,128)S(1)} %fusion.65, f32[128,64,128]{2,1,0:T(8,128)S(1)} %bitcast.81, f32[128,64,128]{2,1,0:T(8,128)S(1)} %bitcast.77, s32[]{:T(128)S(6)} %add.751, s32[128]{0:T(128)S(1)} %fusion.196), kind=kOutput, calls=%fused_computation.88 | convolution fusion | flops 1657339904 | bytes 16777732 | tf_op jit(solution)/shard_map/ra,abc->rbc/dot_general | solution.py:34
  537.3 49.0 %multiply_subtract_fusion = (f32[128,64,128]{2,0,1:T(8,128)S(1)}, f32[128,64,128]{2,0,1:T(8,128)S(1)}) fusion(f32[128,64,128]{2,0,1:T(8,128)S(1)} %convolution_subtract_fusion.1, s32[64,128]{1,0:T(8,128)S(1)} %iota_add_fusion, s32[128]{0:T(128)S(1)} %fusion.196, f32[128,64,128]{2,0,1:T(8,128)S(1)} %fusion.64, f32[128,64,128]{2,1,0:T(8,128)S(1)} %bitcast.82, ...), kind=kOutput, calls=%fused_computation.52 | convolution fusion | flops 1701380096 | bytes 25199108 | tf_op jit(solution)/shard_map/ra,abc->rbc/dot_general | solution.py:34
  586.3 6.8 %fusion.44 = f32[128,128,64]{1,2,0:T(8,128)S(1)} fusion(f32[128,64,128]{2,0,1:T(8,128)S(1)} %get-tuple-element.6, s32[64]{0:T(128)S(1)} %fusion.177), kind=kOutput, calls=%fused_computation.79 | convolution fusion | flops 805453824 | bytes 8388864 | tf_op jit(solution)/shard_map/rb,abc->arc/dot_general | solution.py:34
  593.2 7.0 %fusion.42 = f32[128,128,64]{1,2,0:T(8,128)S(1)} fusion(f32[128,64,128]{2,0,1:T(8,128)S(1)} %get-tuple-element.6, s32[64]{0:T(128)S(1)} %fusion.177), kind=kOutput, calls=%fused_computation.77 | convolution fusion | flops 805453824 | bytes 8388864 | tf_op jit(solution)/shard_map/rb,abc->arc/dot_general | solution.py:34
  600.2 7.0 %fusion.50 = f32[128,128,64]{1,2,0:T(8,128)S(1)} fusion(f32[128,128,64]{1,2,0:T(8,128)S(1)} %fusion.44, f32[128,64,128]{2,0,1:T(8,128)S(1)} %get-tuple-element.5, s32[64]{0:T(128)S(1)} %fusion.177), kind=kOutput, calls=%fused_computation.85 | convolution fusion | flops 806502400 | bytes 12583168 | tf_op jit(solution)/shard_map/rb,abc->arc/dot_general | solution.py:34
  607.2 8.4 %fusion.20 = (f32[128,64,128]{2,1,0:T(8,128)S(1)}, f32[128,64,128]{2,1,0:T(8,128)S(1)}) fusion(f32[128,128,64]{1,2,0:T(8,128)S(1)} %fusion.50, f32[64,128]{1,0:T(8,128)S(1)} %get-tuple-element.12, f32[64,128]{1,0:T(8,128)S(1)} %get-tuple-element.11, f32[128,128,64]{1,2,0:T(8,128)S(1)} %fusion.42, s32[64]{0:T(128)S(1)} %fusion.177, ...), kind=kOutput, calls=%fused_computation.44 | convolution fusion | flops 812793856 | bytes 21037312 | tf_op jit(solution)/shard_map/rb,abc->arc/dot_general | solution.py:34
  615.5 7.1 %fusion.34 = f32[128,64,128]{2,0,1:T(8,128)S(1)} fusion(f32[128,64,128]{2,1,0:T(8,128)S(1)} %get-tuple-element.4, s32[128]{0:T(128)S(1)} %fusion.196), kind=kOutput, calls=%fused_computation.69 | convolution fusion | flops 1611202560 | bytes 8389120 | tf_op jit(solution)/shard_map/rc,abc->abr/dot_general | solution.py:34
  622.7 7.1 %fusion.36 = f32[128,64,128]{2,0,1:T(8,128)S(1)} fusion(f32[128,64,128]{2,1,0:T(8,128)S(1)} %get-tuple-element.4, s32[128]{0:T(128)S(1)} %fusion.196), kind=kOutput, calls=%fused_computation.71 | convolution fusion | flops 1611202560 | bytes 8389120 | tf_op jit(solution)/shard_map/rc,abc->abr/dot_general | solution.py:34
  629.8 7.4 %add_multiply_fusion = f32[128,64,128]{2,0,1:T(8,128)S(1)} fusion(f32[128,64,128]{2,0,1:T(8,128)S(1)} %fusion.34, f32[128,64,128]{2,1,0:T(8,128)S(1)} %get-tuple-element.3, s32[128]{0:T(128)S(1)} %fusion.196), kind=kOutput, calls=%fused_computation.49 | convolution fusion | flops 1613299712 | bytes 12583424 | tf_op jit(solution)/shard_map/rc,abc->abr/dot_general | solution.py:34
  637.2 2.4 copy.56
  639.6 0.0 copy-start
  639.7 7.2 %subtract_multiply_fusion = f32[128,64,128]{2,0,1:T(8,128)S(1)} fusion(f32[128,64,128]{2,0,1:T(8,128)S(1)} %fusion.36, f32[128,64,128]{2,1,0:T(8,128)S(1)} %get-tuple-element.3, s32[128]{0:T(128)S(1)} %fusion.196), kind=kOutput, calls=%fused_computation.50 | convolution fusion | flops 1613299712 | bytes 12583424 | tf_op jit(solution)/shard_map/rc,abc->abr/dot_general | solution.py:34
  646.8 2.4 copy.53
  649.3 0.0 copy-start.1
  649.3 0.0 copy-done
  649.3 2.7 multiply_add_fusion
  652.0 0.5 copy-done.1
  (4 shorter events, 0.0 us)
Async XLA Ops:
  10.6 197.3 %all-to-all-start = ((f32[2,32,32768]{2,0,1:T(2,128)}), f32[2,32,32768]{2,0,1:T(2,128)}, u32[]{:S(2)}, u32[]{:S(2)}) async-start(f32[2,32,32768]{2,0,1:T(2,128)} %pad_maximum_fusion), calls=%async_computation | async-start | bytes 16777216 | tf_op jit(solution)/shard_map/all_to_all | solution.py:58
  251.5 193.3 %all-to-all-start.1 = ((f32[2,32,32768]{2,0,1:T(2,128)}), f32[2,32,32768]{2,0,1:T(2,128)}, u32[]{:S(2)}, u32[]{:S(2)}) async-start(f32[2,32,32768]{2,0,1:T(2,128)} %copy.42), calls=%async_computation.1 | async-start | bytes 16777216 | tf_op jit(solution)/shard_map/all_to_all | solution.py:61
  639.6 9.6 %copy-start = (f32[128,64,128]{2,1,0:T(8,128)}, f32[128,64,128]{2,1,0:T(8,128)S(1)}, u32[]{:S(2)}) copy-start(f32[128,64,128]{2,1,0:T(8,128)S(1)} %copy.56) | copy-start | bytes 12582916
  649.3 3.3 copy-start.1
where the time goes:
time: 655 us; the launch traced here: 653 us
  waiting for transfers between devices  379 us (58%)
  matrix products  215 us (33%)
  local copies, waits for them, and re-layouts  33.1 us (5%)
  other arithmetic  13.6 us (2%)
  starting transfers between devices  11.1 us (2%)
    dot_general x16, matrix products, contract(): return jnp.einsum(spec, left, right, precision=lax.Precision.HIGHEST)  215 us
    all_to_all x1, waiting for transfers between devices, on_device(): lax.all_to_all(spread, ('gx', 'gy', 'gz'), split_axis=1, concat_axis=1, t...  190 us
    all_to_all x1, waiting for transfers between devices, on_device(): lax.all_to_all(moved, ('gx', 'gy', 'gz'), split_axis=1, concat_axis=1, ti...  189 us
  transfers between devices with their start and end apart: 2, of which 2 were waited for; matrix products, arithmetic and copies ran while one was open for 0% of the time, Pallas kernels for 0%

commit v1 on v0

v1 whole, which is shorter than its diff:
```python
import functools
import math

import jax
import jax.numpy as jnp
import numpy as np
from jax import lax
from jax.experimental import pallas as pl
from jax.experimental.pallas import tpu as pltpu
from jax.sharding import PartitionSpec as P

AXES = ("gx", "gy", "gz")
LANES = 128
CHUNKS = 2


def reversed_bits(count):
    bits = count.bit_length() - 1
    values = np.arange(count)
    result = np.zeros(count, np.int32)
    for place in range(bits):
        result += ((values >> place) & 1) << (bits - 1 - place)
    return result.astype(np.int32)


def phases(product, modulus):
    angle = (product % modulus).astype(jnp.float32) * (2.0 * math.pi / modulus)
    return jnp.cos(angle), jnp.sin(angle)


def halves(values):
    high = values.astype(jnp.bfloat16)
    low = (values - high.astype(jnp.float32)).astype(jnp.bfloat16)
    return high, low


def table_halves(values):
    high = lax.reduce_precision(values, 8, 7)
    return high.astype(jnp.bfloat16), (values - high).astype(jnp.bfloat16)


def fourier(reals, imags):
    count = len(reals)
    span = count // 2
    reals, imags = list(reals), list(imags)
    while span >= 1:
        for start in range(0, count, 2 * span):
            for offset in range(span):
                top, bottom = start + offset, start + offset + span
                ar, ai, br, bi = reals[top], imags[top], reals[bottom], imags[bottom]
                reals[top], imags[top] = ar + br, ai + bi
                dr, di = ar - br, ai - bi
                if offset == 0:
                    reals[bottom], imags[bottom] = dr, di
                elif 2 * offset == span:
                    reals[bottom], imags[bottom] = -di, dr
                else:
                    angle = math.pi * offset / span
                    c, s = math.cos(angle), math.sin(angle)
                    if 4 * offset == span:
                        reals[bottom], imags[bottom] = (dr - di) * c, (dr + di) * c
                    elif 4 * offset == 3 * span:
                        reals[bottom], imags[bottom] = -(dr + di) * s, (dr - di) * s
                    else:
                        reals[bottom], imags[bottom] = dr * c - di * s, dr * s + di * c
        span //= 2
    return reals, imags


def device_kernel(re_ref, im_ref, cos_ref, sin_ref, high_ref, low_ref):
    count = re_ref.shape[0]
    reals, imags = fourier([re_ref[d] for d in range(count)], [im_ref[d] for d in range(count)])
    for e in range(count):
        c, s = cos_ref[:, e : e + 1], sin_ref[:, e : e + 1]
        yr = reals[e] * c - imags[e] * s
        yi = reals[e] * s + imags[e] * c
        high, low = halves(yr)
        high_ref[e, :, :LANES], low_ref[e, :, :LANES] = high, low
        high, low = halves(yi)
        high_ref[e, :, LANES:], low_ref[e, :, LANES:] = high, low


def device_stage(re, im, cosine, sine):
    devices, rows, lanes = re.shape
    block = 16
    spec = pl.BlockSpec((devices, block, lanes), lambda i: (0, i, 0))
    table = pl.BlockSpec((block, devices), lambda i: (i, 0))
    out = pl.BlockSpec((devices, block, 2 * lanes), lambda i: (0, i, 0))
    shape = jax.ShapeDtypeStruct((devices, rows, 2 * lanes), jnp.bfloat16)
    return pl.pallas_call(
        device_kernel,
        grid=(rows // block,),
        in_specs=[spec, spec, table, table],
        out_specs=[out, out],
        out_shape=[shape, shape],
        cost_estimate=pl.CostEstimate(
            flops=80 * devices * rows * lanes, bytes_accessed=16 * devices * rows * lanes, transcendentals=0
        ),
        name="device_stage",
    )(re, im, cosine, sine)


def row_kernel(high_ref, low_ref, table_ref, out_ref):
    rows = table_ref.shape[1] // 2
    dot = functools.partial(jnp.dot, preferred_element_type=jnp.float32)
    high, low = high_ref[0], low_ref[0]
    mixed = dot(table_ref[0], high) + dot(table_ref[1], high) + dot(table_ref[0], low)
    out_ref[0, :rows] = mixed[:rows, :LANES] - mixed[rows:, LANES:]
    out_ref[0, rows:] = mixed[rows:, :LANES] + mixed[:rows, LANES:]


def row_stage(high, low, table):
    devices, rows, wide = high.shape
    part = table.shape[1]
    spec = pl.BlockSpec((1, rows, wide), lambda e: (e, 0, 0))
    return pl.pallas_call(
        row_kernel,
        grid=(devices,),
        in_specs=[spec, spec, pl.BlockSpec((2, part, rows), lambda e: (0, 0, 0))],
        out_specs=pl.BlockSpec((1, part, LANES), lambda e: (e, 0, 0)),
        out_shape=jax.ShapeDtypeStruct((devices, part, LANES), jnp.float32),
        cost_estimate=pl.CostEstimate(
            flops=6 * devices * part * rows * wide, bytes_accessed=8 * devices * rows * wide, transcendentals=0
        ),
        name="row_stage",
    )(high, low, table)


def lane_kernel(block, x_ref, mc_ref, ms_ref, jc_ref, js_ref, table_ref, *refs):
    re_ref, im_ref, prob_ref = refs[-3:]
    count = x_ref.shape[0]
    reals, imags = fourier([x_ref[j, 0] for j in range(count)], [x_ref[j, 1] for j in range(count)])
    mc, ms = mc_ref[...], ms_ref[...]
    highs, lows = [], []
    for j in range(count):
        jc, js = jc_ref[j : j + 1, :], js_ref[j : j + 1, :]
        c = mc * jc - ms * js
        s = mc * js + ms * jc
        rh, rl = halves(reals[j] * c - imags[j] * s)
        ih, il = halves(reals[j] * s + imags[j] * c)
        highs.append(jnp.concatenate([rh, ih], axis=1))
        lows.append(jnp.concatenate([rl, il], axis=1))
    high, low = jnp.concatenate(highs, axis=0), jnp.concatenate(lows, axis=0)
    dot = functools.partial(jnp.dot, preferred_element_type=jnp.float32)
    mixed = dot(high, table_ref[0]) + dot(high, table_ref[1]) + dot(low, table_ref[0])
    cube = jnp.swapaxes(mixed.reshape(count, block, 2 * LANES), 0, 1)
    re, im = cube[:, :, :LANES], cube[:, :, LANES:]
    re_ref[...] = re
    im_ref[...] = im
    prob_ref[...] = re * re + im * im


def lane_stage(x, previous, index, rows, mid, inner, table):
    count, _, part, lanes = x.shape
    block = 16
    first = index * (part // block)
    mspec = pl.BlockSpec((block, lanes), lambda i: (first + i, 0))
    jspec = pl.BlockSpec((count, lanes), lambda i: (0, 0))
    out = pl.BlockSpec((block, count, lanes), lambda i: (first + i, 0, 0))
    shape = jax.ShapeDtypeStruct((rows, count, lanes), jnp.float32)
    arguments = [x, *mid, *inner, table]
    specs = [
        pl.BlockSpec((count, 2, block, lanes), lambda i: (0, 0, i, 0)),
        mspec, mspec, jspec, jspec,
        pl.BlockSpec((2, 2 * lanes, 2 * lanes), lambda i: (0, 0, 0)),
    ]
    aliases = {}
    if previous is not None:
        aliases = {len(arguments) + k: k for k in range(3)}
        arguments += previous
        specs += [pl.BlockSpec(memory_space=pl.ANY)] * 3
    return pl.pallas_call(
        functools.partial(lane_kernel, block),
        grid=(part // block,),
        in_specs=specs,
        out_specs=[out, out, out],
        out_shape=[shape, shape, shape],
        input_output_aliases=aliases,
        cost_estimate=pl.CostEstimate(
            flops=20 * count * part * lanes * lanes, bytes_accessed=20 * count * part * lanes, transcendentals=0
        ),
        name="lane_stage",
    )(*arguments)


def exchange(x):
    return lax.all_to_all(x, AXES, split_axis=0, concat_axis=0, tiled=True)


def on_device(state_re, state_im):
    devices = lax.axis_size(AXES)
    local = state_re.shape[0]
    total = devices * local
    rows = local // (devices * LANES)
    me = lax.axis_index(AXES).astype(jnp.int32)
    rev_d, rev_a, rev_l = reversed_bits(devices), reversed_bits(rows), reversed_bits(LANES)

    def outgoing(values):
        return jnp.swapaxes(values.reshape(rows, devices, LANES), 0, 1)

    got_re, got_im = exchange(outgoing(state_re)), exchange(outgoing(state_im))

    a_index = jnp.arange(rows, dtype=jnp.int32)
    turn = phases((a_index[:, None] * (devices * LANES) + me * LANES) * rev_d[None, :], total)
    high, low = device_stage(got_re, got_im, *turn)

    def row_table(part):
        c, s = phases(part[:, None] * (a_index[None, :] * devices + me), rows * devices)
        return jnp.stack(table_halves(jnp.concatenate([c, s], axis=0)))

    k_here = jnp.sum(jnp.where(jnp.arange(devices) == me, rev_d, 0))
    lane = np.arange(LANES, dtype=np.int32)
    mid = phases((k_here + devices * rev_a)[:, None] * lane[None, :], total)
    angle = (rev_d[:, None] * lane[None, :] % (devices * LANES)) * (2.0 * math.pi / (devices * LANES))
    inner = (jnp.asarray(np.cos(angle), jnp.float32), jnp.asarray(np.sin(angle), jnp.float32))
    angle = (lane[:, None] * rev_l[None, :] % LANES) * (2.0 * math.pi / LANES)
    c, s = np.cos(angle) / math.sqrt(total), np.sin(angle) / math.sqrt(total)
    table = jnp.stack(table_halves(jnp.asarray(np.block([[c, s], [-s, c]]), jnp.float32)))

    part = rows // CHUNKS
    arrived = []
    for index in range(CHUNKS):
        sent = row_stage(high, low, row_table(rev_a[index * part : (index + 1) * part]))
        arrived.append(exchange(sent))
    outs = None
    for index in range(CHUNKS):
        x = arrived[index].reshape(devices, 2, part, LANES)
        outs = lane_stage(x, outs, index, rows, mid, inner, table)
    return tuple(values.reshape(local) for values in outs)


def solution(mesh):
    spec = P(AXES)
    return jax.shard_map(
        on_device, mesh=mesh, in_specs=(spec, spec), out_specs=(spec, spec, spec), check_vma=False
    )
```

time: 655 us -> 457 us (0.70)
  matrix products: 215 us -> 0 us
  Pallas kernels: 0 us -> 77.7 us
  waiting for transfers between devices: 379 us -> 338 us
  local copies, waits for them, and re-layouts: 33.1 us -> 13.4 us
  starting transfers between devices: 11.1 us -> 18.3 us
  other arithmetic: 13.6 us -> 6.52 us
    dot_general x16 -> x0, matrix products: 215 us -> none  [contract(): return jnp.einsum(spec, left, right, precision=lax.Precision.HIGHEST)]
    pallas_call x0 -> x5, Pallas kernels: none -> 77.7 us  [the longest x2 45.2 us: row_stage(): pl.pallas_call(row_kernel, grid=(devices,), in_specs=[spec, spec, pl.Bloc...]
    all_to_all x2 -> x4, waiting for transfers between devices: 379 us -> 338 us  [exchange(): return lax.all_to_all(x, AXES, split_axis=0, concat_axis=0, tiled=True)]
    slice x2 -> x0, local copies, waits for them, and re-layouts: 19.9 us -> none  [the longest x1 10 us: on_device(): mixed = complex_mix('ed,dm->em', mixing, (stacked[0], stacked[1]))]
    reshape x0 -> x2, local copies, waits for them, and re-layouts: none -> 13.3 us  [outgoing(): return jnp.swapaxes(values.reshape(rows, devices, LANES), 0, 1)]
    another operation x2, other arithmetic: 10.5 us -> 1.47 us  [row_table(): return jnp.stack(table_halves(jnp.concatenate([c, s], axis=0)))]
    another operation x1 -> x0, local copies, waits for them, and re-layouts: 7.83 us -> none  [on_device(): moved = jnp.stack(mixed, axis=0)]
    all_to_all x2 -> x4, starting transfers between devices: 11.1 us -> 18.3 us  [exchange(): return lax.all_to_all(x, AXES, split_axis=0, concat_axis=0, tiled=True)]
  transfers between devices with their start and end apart: 2 -> 4, of which waited for: 2 -> 4; matrix products, arithmetic and copies ran while one was open for 0% -> 3% of each run, Pallas kernels for 0% -> 7%
where the time goes in v1:
time: 457 us; the launch traced here: 454 us
  waiting for transfers between devices  338 us (74%)
  Pallas kernels  77.7 us (17%)
  starting transfers between devices  18.3 us (4%)
  local copies, waits for them, and re-layouts  13.4 us (3%)
  other arithmetic  6.52 us (1%)
    all_to_all x4, waiting for transfers between devices, exchange(): return lax.all_to_all(x, AXES, split_axis=0, concat_axis=0, tiled=True)  338 us
    pallas_call x2, Pallas kernels, row_stage(): pl.pallas_call(row_kernel, grid=(devices,), in_specs=[spec, spec, pl.Bloc...  45.2 us
    pallas_call x2, Pallas kernels, lane_stage(): pl.pallas_call(functools.partial(lane_kernel, block), grid=(part // block...  18.7 us
    all_to_all x4, starting transfers between devices, exchange(): return lax.all_to_all(x, AXES, split_axis=0, concat_axis=0, tiled=True)  18.3 us
    pallas_call x1, Pallas kernels, device_stage(): pl.pallas_call(device_kernel, grid=(rows // block,), in_specs=[spec, spec...  13.8 us
    reshape x2, local copies, waits for them, and re-layouts, outgoing(): return jnp.swapaxes(values.reshape(rows, devices, LANES), 0, 1)  13.3 us
  transfers between devices with their start and end apart: 4, of which 4 were waited for; matrix products, arithmetic and copies ran while one was open for 3% of the time, Pallas kernels for 7%

profile of v1, /device:TPU:0, one launch (start us, length us, event | category | flops | bytes accessed | tf_op | source)
XLA Modules:
  0.0 454.4 jit_solution(5592237112347967892)
XLA Ops:
  0.6 6.6 %copy.25 = f32[256,32,128]{2,0,1:T(8,128)} copy(f32[256,32,128]{2,1,0:T(8,128)} %bitcast.23) | data formatting | bytes 8388608 | tf_op jit(solution)/shard_map/reshape | solution.py:199
  7.3 7.5 %all-to-all-start = ((f32[32,256,128]{2,1,0:T(8,128)}), f32[32,256,128]{2,1,0:T(8,128)}, u32[]{:S(2)}, u32[]{:S(2)}) async-start(f32[32,256,128]{2,1,0:T(8,128)} %bitcast.22), calls=%async_computation | async-start | bytes 8388608 | tf_op jit(solution)/shard_map/all_to_all | solution.py:187
  14.7 6.6 %copy.24 = f32[256,32,128]{2,0,1:T(8,128)} copy(f32[256,32,128]{2,1,0:T(8,128)} %bitcast.24) | data formatting | bytes 8388608 | tf_op jit(solution)/shard_map/reshape | solution.py:199
  21.4 89.1 %all-to-all-done.re_ref = f32[32,256,128]{2,1,0:T(8,128)} async-done(((f32[32,256,128]{2,1,0:T(8,128)}), f32[32,256,128]{2,1,0:T(8,128)}, u32[]{:S(2)}, u32[]{:S(2)}) %all-to-all-start) | async-done | bytes 4194336 | tf_op jit(solution)/shard_map/all_to_all | solution.py:187
  110.5 0.0 copy-start.1
  110.5 0.0 copy-start.2
  110.5 0.0 copy-start.3
  110.5 3.7 all-to-all-start.1
  114.2 0.0 copy-done.1
  114.2 0.1 fusion.16
  114.3 0.1 copy.21
  114.4 0.0 copy-done.2
  114.4 0.0 copy-done.3
  114.5 1.1 cosine_bitcast_fusion
  115.6 0.1 reduce-precision_convert_fusion
  115.7 0.7 pad_maximum_fusion.3.table_ref
  116.4 1.2 multiply_sine_fusion
  117.6 92.4 %all-to-all-done.1.im_ref = f32[32,256,128]{2,1,0:T(8,128)} async-done(((f32[32,256,128]{2,1,0:T(8,128)}), f32[32,256,128]{2,1,0:T(8,128)}, u32[]{:S(2)}, u32[]{:S(2)}) %all-to-all-start.1) | async-done | bytes 4194336 | tf_op jit(solution)/shard_map/all_to_all | solution.py:187
  210.0 13.8 %device_stage.1 = (bf16[32,256,256]{2,1,0:T(8,128)(2,1)}, bf16[32,256,256]{2,1,0:T(8,128)(2,1)}) custom-call(f32[32,256,128]{2,1,0:T(8,128)} %all-to-all-done.re_ref, f32[32,256,128]{2,1,0:T(8,128)} %all-to-all-done.1.im_ref, f32[256,32]{1,0:T(8,128)} %get-tuple-element.24.cos_ref, f32[256,32]{1,0:T(8,128)} %get-tuple-element.23.sin_ref), custom_call_target="tpu_custom_call" | custom-call | flops 83886080 | bytes 16777216 | tf_op jit(solution)/shard_map/device_stage/pallas_call | solution.py:90
  223.8 22.6 %row_stage.3 = f32[32,256,128]{2,1,0:T(8,128)} custom-call(bf16[32,256,256]{2,1,0:T(8,128)(2,1)} %get-tuple-element.11.high_ref, bf16[32,256,256]{2,1,0:T(8,128)(2,1)} %get-tuple-element.12.low_ref, bf16[2,256,256]{2,1,0:T(8,128)(2,1)} %pad_maximum_fusion.3.table_ref), custom_call_target="tpu_custom_call" | custom-call | flops 3221225472 | bytes 16777216 | tf_op jit(solution)/shard_map/row_stage/pallas_call | solution.py:116
  246.4 3.6 all-to-all-start.3
  250.0 0.7 pad_maximum_fusion.1.table_ref
  250.7 22.6 %row_stage.2 = f32[32,256,128]{2,1,0:T(8,128)} custom-call(bf16[32,256,256]{2,1,0:T(8,128)(2,1)} %get-tuple-element.11.high_ref, bf16[32,256,256]{2,1,0:T(8,128)(2,1)} %get-tuple-element.12.low_ref, bf16[2,256,256]{2,1,0:T(8,128)(2,1)} %pad_maximum_fusion.1.table_ref), custom_call_target="tpu_custom_call" | custom-call | flops 3221225472 | bytes 16777216 | tf_op jit(solution)/shard_map/row_stage/pallas_call | solution.py:116
  273.3 0.0 copy-start
  273.3 72.4 %all-to-all-done.3 = f32[32,256,128]{2,1,0:T(8,128)} async-done(((f32[32,256,128]{2,1,0:T(8,128)}), f32[32,256,128]{2,1,0:T(8,128)}, u32[]{:S(2)}, u32[]{:S(2)}) %all-to-all-start.3) | async-done | bytes 4194336 | tf_op jit(solution)/shard_map/all_to_all | solution.py:187
  345.7 3.6 all-to-all-start.2
  349.3 0.6 fusion.18
  349.9 0.0 copy-done
  349.9 0.6 broadcast_add_fusion
  350.6 1.3 fusion.14
  351.9 9.4 %lane_stage.2 = (f32[256,32,128]{2,1,0:T(8,128)}, f32[256,32,128]{2,1,0:T(8,128)}, f32[256,32,128]{2,1,0:T(8,128)}) custom-call(f32[32,2,128,128]{3,2,1,0:T(8,128)} %bitcast.9.x_ref, f32[256,128]{1,0:T(8,128)} %get-tuple-element.32.mc_ref, f32[256,128]{1,0:T(8,128)} %get-tuple-element.31.ms_ref, f32[32,128]{1,0:T(8,128)} %constant.93.clone.jc_ref, ...), custom_call_target="tpu_custom_call" | custom-call | flops 1342177280 | bytes 10485760 | tf_op jit(solution)/shard_map/lane_stage/pallas_call | solution.py:172
  361.3 83.8 %all-to-all-done.2 = f32[32,256,128]{2,1,0:T(8,128)} async-done(((f32[32,256,128]{2,1,0:T(8,128)}), f32[32,256,128]{2,1,0:T(8,128)}, u32[]{:S(2)}, u32[]{:S(2)}) %all-to-all-start.2) | async-done | bytes 4194336 | tf_op jit(solution)/shard_map/all_to_all | solution.py:187
  445.1 9.4 %lane_stage.3 = (f32[256,32,128]{2,1,0:T(8,128)}, f32[256,32,128]{2,1,0:T(8,128)}, f32[256,32,128]{2,1,0:T(8,128)}) custom-call(f32[32,2,128,128]{3,2,1,0:T(8,128)} %bitcast.6.x_ref, f32[256,128]{1,0:T(8,128)} %get-tuple-element.32.mc_ref, f32[256,128]{1,0:T(8,128)} %get-tuple-element.31.ms_ref, ...), custom_call_target="tpu_custom_call", output_to_operand_aliasing={{0}: (6, {}), {1}: (7, {}), {2}: (8, {})} | custom-call | flops 1342177280 | bytes 10485760 | tf_op jit(solution)/shard_map/lane_stage/pallas_call | solution.py:172
  (2 shorter events, 0.0 us)
Async XLA Ops:
  7.3 103.2 %all-to-all-start = ((f32[32,256,128]{2,1,0:T(8,128)}), f32[32,256,128]{2,1,0:T(8,128)}, u32[]{:S(2)}, u32[]{:S(2)}) async-start(f32[32,256,128]{2,1,0:T(8,128)} %bitcast.22), calls=%async_computation | async-start | bytes 8388608 | tf_op jit(solution)/shard_map/all_to_all | solution.py:187
  110.5 3.8 copy-start.1
  110.5 4.0 copy-start.2
  110.5 4.0 copy-start.3
  110.5 99.5 %all-to-all-start.1 = ((f32[32,256,128]{2,1,0:T(8,128)}), f32[32,256,128]{2,1,0:T(8,128)}, u32[]{:S(2)}, u32[]{:S(2)}) async-start(f32[32,256,128]{2,1,0:T(8,128)} %bitcast.21), calls=%async_computation.1 | async-start | bytes 8388608 | tf_op jit(solution)/shard_map/all_to_all | solution.py:187
  246.4 99.4 %all-to-all-start.3 = ((f32[32,256,128]{2,1,0:T(8,128)}), f32[32,256,128]{2,1,0:T(8,128)}, u32[]{:S(2)}, u32[]{:S(2)}) async-start(f32[32,256,128]{2,1,0:T(8,128)} %row_stage.3), calls=%async_computation.3 | async-start | bytes 8388608 | tf_op jit(solution)/shard_map/all_to_all | solution.py:187
  273.3 76.6 %copy-start = (s32[256]{0:T(256)S(1)}, s32[256]{0:T(256)}, u32[]{:S(2)}) copy-start(s32[256]{0:T(256)} %constant.91.clone) | copy-start | bytes 3076
  345.7 99.3 %all-to-all-start.2 = ((f32[32,256,128]{2,1,0:T(8,128)}), f32[32,256,128]{2,1,0:T(8,128)}, u32[]{:S(2)}, u32[]{:S(2)}) async-start(f32[32,256,128]{2,1,0:T(8,128)} %row_stage.2), calls=%async_computation.2 | async-start | bytes 8388608 | tf_op jit(solution)/shard_map/all_to_all | solution.py:187

commit v2 on v1

v2 whole, which is shorter than its diff:
```python
import functools
import math

import jax
import jax.numpy as jnp
import numpy as np
from jax import lax
from jax.experimental import pallas as pl
from jax.experimental.pallas import tpu as pltpu
from jax.sharding import PartitionSpec as P


AXES = ("gx", "gy", "gz")
LANES = 128
SLICES = 4
SWAP = 4
TILE = 128
GROUPS = ((2, 3), (1, 0))

SCALAR = pl.BlockSpec(memory_space=pltpu.SMEM)
ANYWHERE = pl.BlockSpec(memory_space=pl.ANY)
WHOLE = pl.BlockSpec(memory_space=pltpu.VMEM)


def reversed_bits(count):
    bits = count.bit_length() - 1
    values = np.arange(count)
    result = np.zeros(count, np.int32)
    for place in range(bits):
        result += ((values >> place) & 1) << (bits - 1 - place)
    return result.astype(np.int32)


def phases(product, modulus):
    angle = (product % modulus).astype(jnp.float32) * (2.0 * math.pi / modulus)
    return jnp.cos(angle), jnp.sin(angle)


def halves(values):
    high = values.astype(jnp.bfloat16)
    low = (values - high.astype(jnp.float32)).astype(jnp.bfloat16)
    return high, low


def table_halves(values):
    high = lax.reduce_precision(values, 8, 7)
    return high.astype(jnp.bfloat16), (values - high).astype(jnp.bfloat16)


def fourier(reals, imags):
    count = len(reals)
    span = count // 2
    reals, imags = list(reals), list(imags)
    while span >= 1:
        for start in range(0, count, 2 * span):
            for offset in range(span):
                top, bottom = start + offset, start + offset + span
                ar, ai, br, bi = reals[top], imags[top], reals[bottom], imags[bottom]
                reals[top], imags[top] = ar + br, ai + bi
                dr, di = ar - br, ai - bi
                if offset == 0:
                    reals[bottom], imags[bottom] = dr, di
                elif 2 * offset == span:
                    reals[bottom], imags[bottom] = -di, dr
                else:
                    angle = math.pi * offset / span
                    c, s = math.cos(angle), math.sin(angle)
                    if 4 * offset == span:
                        reals[bottom], imags[bottom] = (dr - di) * c, (dr + di) * c
                    elif 4 * offset == 3 * span:
                        reals[bottom], imags[bottom] = -(dr + di) * s, (dr - di) * s
                    else:
                        reals[bottom], imags[bottom] = dr * c - di * s, dr * s + di * c
        span //= 2
    return reals, imags


def pack_kernel(first, z_ref, re_ref, im_ref, *refs):
    outs = refs[-SWAP:]
    block, tile, lanes = re_ref.shape
    for side, ref in enumerate((re_ref, im_ref)):
        flat = ref.reshape(block * tile, lanes)
        for slot, out_ref in enumerate(outs):
            place = first + jnp.bitwise_xor(z_ref[0], slot)
            out_ref[side] = flat[pl.ds(place, block, stride=tile), :]


def pack_stage(z, re, im, c, after):
    rows, _, lanes = re.shape
    block, tile = 128, 8
    spec = pl.BlockSpec((block, tile, lanes), lambda i: (i, c * SWAP // tile, 0))
    out = pl.BlockSpec((2, block, lanes), lambda i: (0, i, 0))
    return pl.pallas_call(
        functools.partial(pack_kernel, c * SWAP % tile),
        grid=(rows // block,),
        in_specs=[SCALAR, spec, spec] + [ANYWHERE] * len(after),
        out_specs=[out] * SWAP,
        out_shape=[jax.ShapeDtypeStruct((2, rows, lanes), jnp.float32)] * SWAP,
        cost_estimate=pl.CostEstimate(flops=40 << 20, bytes_accessed=8 << 20, transcendentals=0),
        name="pack_stage",
    )(z, re, im, *after)


def butterfly(mine, theirs, sign, cosine, sine):
    r, i = theirs[0] + sign * mine[0], theirs[1] + sign * mine[1]
    return r * cosine - i * sine, r * sine + i * cosine


def per_slot(refs):
    return [refs[0].at[s] for s in range(SWAP)] if len(refs) == 1 else refs


def slot_spec(listed, block):
    if listed:
        return [pl.BlockSpec((2, block, LANES), lambda i: (0, i, 0))] * SWAP
    return [pl.BlockSpec((SWAP, 2, block, LANES), lambda i: (0, 0, i, 0))]


def slot_shape(listed, rows):
    shape = (2, rows, LANES) if listed else (SWAP, 2, rows, LANES)
    return [jax.ShapeDtypeStruct(shape, jnp.float32)] * (SWAP if listed else 1)


def mix_kernel(inputs, coef_ref, after_ref, *refs):
    mine, theirs, outs = (
        per_slot(part) for part in (refs[:inputs], refs[inputs : 2 * inputs], refs[2 * inputs :])
    )
    for s in range(SWAP):
        r, i = butterfly(mine[s], theirs[s], coef_ref[2 * SWAP], coef_ref[s], coef_ref[SWAP + s])
        outs[s][0], outs[s][1] = r, i


def mix_stage(coef, mine, theirs, listed, after):
    rows = mine[0].shape[-2]
    block = 128
    return pl.pallas_call(
        functools.partial(mix_kernel, len(mine)),
        grid=(rows // block,),
        in_specs=[SCALAR, ANYWHERE] + slot_spec(len(mine) > 1, block) * 2,
        out_specs=slot_spec(listed, block),
        out_shape=slot_shape(listed, rows),
        cost_estimate=pl.CostEstimate(flops=20 << 20, bytes_accessed=6 << 20, transcendentals=0),
        name="mix_stage",
    )(coef, after, *mine, *theirs)


def swap_kernel(z_ref, coef_ref, turn_ref, after_ref, mine_ref, theirs_ref, *refs):
    outs, scratch = per_slot(refs[:-1]), refs[-1]
    reals, imags = [], []
    for place in range(SWAP):
        slot = jnp.bitwise_xor(z_ref[0], place)
        r, i = butterfly(
            mine_ref.at[slot], theirs_ref.at[slot], coef_ref[2 * SWAP], coef_ref[place], coef_ref[SWAP + place]
        )
        reals.append(r)
        imags.append(i)
    reals, imags = fourier(reals, imags)
    for place in range(SWAP):
        c, s = turn_ref[place], turn_ref[SWAP + place]
        scratch[place, 0] = reals[place] * c - imags[place] * s
        scratch[place, 1] = reals[place] * s + imags[place] * c
    for slot in range(SWAP):
        outs[slot][...] = scratch[jnp.bitwise_xor(z_ref[0], slot)]


def swap_stage(z, coef, turn, mine, theirs, listed, after):
    rows = mine.shape[-2]
    block = 128
    full = slot_spec(False, block)
    return pl.pallas_call(
        swap_kernel,
        grid=(rows // block,),
        in_specs=[SCALAR, SCALAR, SCALAR, ANYWHERE] + full * 2,
        out_specs=slot_spec(listed, block),
        out_shape=slot_shape(listed, rows),
        scratch_shapes=[pltpu.VMEM((SWAP, 2, block, LANES), jnp.float32)],
        cost_estimate=pl.CostEstimate(flops=30 << 20, bytes_accessed=6 << 20, transcendentals=0),
        name="swap_stage",
    )(z, coef, turn, after, mine, theirs)


def row_kernel(c, slots, sizes, coef_ref, after_ref, tc_ref, ts_ref, rc_ref, rs_ref, table_ref, *refs):
    refs, (high_ref, low_ref) = refs[:-2], refs[-2:]
    inputs = len(slots) if len(slots) < SWAP else 1
    mine, theirs, outs = refs[:inputs], refs[inputs : 2 * inputs], refs[2 * inputs :]
    if len(slots) == SWAP:
        mine, theirs = per_slot(mine), per_slot(theirs)
    dot = functools.partial(jnp.dot, preferred_element_type=jnp.float32)
    for n, s in enumerate(slots):
        r, i = butterfly(mine[n], theirs[n], coef_ref[2 * SWAP], coef_ref[0], coef_ref[SWAP])
        cosine, sine = tc_ref[:, s : s + 1], ts_ref[:, s : s + 1]
        high_ref[:, :LANES], low_ref[:, :LANES] = halves(r * cosine - i * sine)
        high_ref[:, LANES:], low_ref[:, LANES:] = halves(r * sine + i * cosine)
        base = 0
        for part, size in enumerate(sizes):
            out_ref = outs[part * len(slots) + n]

            def tile(m, carry, out_ref=out_ref, base=base):
                high = high_ref[...]
                mixed = dot(table_ref[base + m, 0], high) + dot(table_ref[base + m, 1], high)
                mixed += dot(table_ref[base + m, 0], low_ref[...])
                yr = mixed[:TILE, :LANES] - mixed[TILE:, LANES:]
                yi = mixed[TILE:, :LANES] + mixed[:TILE, LANES:]
                here = pl.ds(pl.multiple_of((base + m) * TILE, TILE), TILE)
                cosine, sine = rc_ref[here, c : c + 1], rs_ref[here, c : c + 1]
                there = pl.ds(pl.multiple_of(m * TILE, TILE), TILE)
                out_ref[0, there, :] = yr * cosine - yi * sine
                out_ref[1, there, :] = yr * sine + yi * cosine
                return carry

            lax.fori_loop(0, size // TILE, tile, 0)
            base += size // TILE


def row_stage(coef, turn, scale, table, mine, theirs, c, slots, sizes, after):
    rows = mine[0].shape[-2]
    shapes = [jax.ShapeDtypeStruct((2, size, LANES), jnp.float32) for size in sizes for _ in slots]
    outs = pl.pallas_call(
        functools.partial(row_kernel, c, slots, sizes),
        in_specs=[SCALAR, ANYWHERE] + [WHOLE] * (5 + 2 * len(mine)),
        out_specs=[WHOLE] * len(shapes),
        out_shape=shapes,
        scratch_shapes=[pltpu.VMEM((rows, 2 * LANES), jnp.bfloat16)] * 2,
        cost_estimate=pl.CostEstimate(flops=len(slots) * (100 << 20), bytes_accessed=8 << 20, transcendentals=0),
        name="row_stage",
    )(coef, after, *turn, *scale, table, *mine, *theirs)
    return [outs[k * len(slots) : (k + 1) * len(slots)] for k in range(len(sizes))]


def lane_kernel(block, z_ref, mc_ref, ms_ref, jc_ref, js_ref, table_ref, *refs):
    count = jc_ref.shape[0]
    scratch = refs[-1]
    re_ref, im_ref, prob_ref = refs[-4:-1]
    for n in range(count):
        scratch[(n // SWAP) * SWAP + jnp.bitwise_xor(z_ref[0], n % SWAP)] = refs[n][...]
    reals, imags = fourier([scratch[n, 0] for n in range(count)], [scratch[n, 1] for n in range(count)])
    mc, ms = mc_ref[...], ms_ref[...]
    highs, lows = [], []
    for j in range(count):
        jc, js = jc_ref[j : j + 1, :], js_ref[j : j + 1, :]
        c = mc * jc - ms * js
        s = mc * js + ms * jc
        rh, rl = halves(reals[j] * c - imags[j] * s)
        ih, il = halves(reals[j] * s + imags[j] * c)
        highs.append(jnp.concatenate([rh, ih], axis=1))
        lows.append(jnp.concatenate([rl, il], axis=1))
    high, low = jnp.concatenate(highs, axis=0), jnp.concatenate(lows, axis=0)
    dot = functools.partial(jnp.dot, preferred_element_type=jnp.float32)
    mixed = dot(high, table_ref[0]) + dot(high, table_ref[1]) + dot(low, table_ref[0])
    cube = jnp.swapaxes(mixed.reshape(count, block, 2 * LANES), 0, 1)
    re, im = cube[:, :, :LANES], cube[:, :, LANES:]
    re_ref[...] = re
    im_ref[...] = im
    prob_ref[...] = re * re + im * im


def lane_stage(z, sources, previous, start, part, rows, mid, inner, table):
    count = inner[0].shape[0]
    block = 32
    first = start // block
    mspec = pl.BlockSpec((block, LANES), lambda i: (first + i, 0))
    jspec = pl.BlockSpec((count, LANES), lambda i: (0, 0))
    out = pl.BlockSpec((block, count, LANES), lambda i: (first + i, 0, 0))
    shape = jax.ShapeDtypeStruct((rows, count, LANES), jnp.float32)
    arguments = [z, *mid, *inner, table]
    specs = [SCALAR, mspec, mspec, jspec, jspec, pl.BlockSpec((2, 2 * LANES, 2 * LANES), lambda i: (0, 0, 0))]
    for source, base in sources:
        offset = (start - base) // block
        arguments += source
        specs += [pl.BlockSpec((2, block, LANES), lambda i, offset=offset: (0, offset + i, 0))] * SWAP
    aliases = {}
    kernel = functools.partial(lane_kernel, block)
    if previous is not None:
        aliases = {len(arguments) + k: k for k in range(3)}
        arguments += previous
        specs += [ANYWHERE] * 3
    return pl.pallas_call(
        kernel,
        grid=(part // block,),
        in_specs=specs,
        out_specs=[out, out, out],
        out_shape=[shape, shape, shape],
        scratch_shapes=[pltpu.VMEM((count, 2, block, LANES), jnp.float32)],
        input_output_aliases=aliases,
        cost_estimate=pl.CostEstimate(
            flops=20 * count * part * LANES * LANES, bytes_accessed=20 * count * part * LANES, transcendentals=0
        ),
        name="lane_stage",
    )(*arguments)


def on_device(state_re, state_im):
    devices = lax.axis_size(AXES)
    sizes = [lax.axis_size(axis) for axis in AXES]
    assert sizes[0] == 2 and sizes[1] == 2 and sizes[2] % SWAP == 0
    weights = sizes[2] // SWAP
    local = state_re.shape[0]
    total = devices * local
    inside = SLICES * SWAP
    rows = local // (inside * LANES)
    x, core, g = (lax.axis_index(axis).astype(jnp.int32) for axis in AXES)
    z, w = g // weights, g % weights
    zs = z.reshape(1)
    rev_a, rev_l, rev_z = reversed_bits(rows), reversed_bits(LANES), reversed_bits(SWAP)
    places = jnp.arange(SWAP, dtype=jnp.int32)
    slots = jnp.bitwise_xor(places, z)
    a_index = jnp.arange(rows, dtype=jnp.int32)
    w_bits = weights.bit_length() - 1
    rev_w = sum(((w >> t) & 1) << (w_bits - 1 - t) for t in range(w_bits))

    def flip(values, distance):
        return lax.ppermute(values, AXES, [(i, i ^ distance) for i in range(devices)])

    def coefficients(bit, exponents, modulus):
        c, s = phases(bit * exponents, modulus)
        sign = (1 - 2 * bit).astype(jnp.float32).reshape(1)
        return jnp.concatenate([c, s, sign])

    x_coef = coefficients(x, core * (devices // 4) + slots * weights + w, devices)
    core_coef = coefficients(core, places * weights + w, devices // 2)
    z_turn = jnp.concatenate(phases(rev_z * w, SWAP * weights))
    w_coef = {t: coefficients((w >> t) & 1, 0 * places + w % (1 << t), 2 << t) for t in range(w_bits)}
    low_k = x + 2 * core + 16 * rev_w
    k_slot = low_k + 4 * (2 * (slots & 1) + (slots >> 1))
    k_here = low_k + 4 * (2 * (z & 1) + (z >> 1))

    cosine, sine = phases(rev_a[:, None] * a_index[None, :], rows)
    tiles = (rows // TILE, TILE, rows)
    table = jnp.concatenate([cosine.reshape(tiles), sine.reshape(tiles)], axis=1)
    row_table = jnp.stack(table_halves(table), axis=1)
    offsets = jnp.arange(SLICES, dtype=jnp.int32) * SWAP + z
    scale = phases(rev_a[:, None] * offsets[None, :], rows * inside)
    turns = [
        phases((a_index[:, None] * (inside * LANES) + offsets[c] * LANES) * k_slot[None, :], total)
        for c in range(SLICES)
    ]

    lane = np.arange(LANES, dtype=np.int32)
    mid = phases((k_here + devices * rev_a)[:, None] * lane[None, :], total)
    angle = (reversed_bits(inside)[:, None] * lane[None, :] % (inside * LANES)) * (2.0 * math.pi / (inside * LANES))
    inner = (jnp.asarray(np.cos(angle), jnp.float32), jnp.asarray(np.sin(angle), jnp.float32))
    angle = (lane[:, None] * rev_l[None, :] % LANES) * (2.0 * math.pi / LANES)
    c, s = np.cos(angle) / math.sqrt(total), np.sin(angle) / math.sqrt(total)
    lane_table = jnp.stack(table_halves(jnp.asarray(np.block([[c, s], [-s, c]]), jnp.float32)))

    re, im = (v.reshape(rows, inside, LANES) for v in (state_re, state_im))
    chain = [zs]

    def kernel(function, *arguments):
        result = function(*arguments, chain[0])
        leaf = jax.tree.leaves(result)[0]
        chain[0] = leaf
        return result

    def swap_out(arrays):
        return [arrays[0]] + [flip(arrays[s], s * weights) for s in range(1, SWAP)]

    packed, inward, across, mixed, spread = {}, {}, {}, {}, {}
    parts = {k: (rows,) for k in range(SLICES)}
    parts[SLICES - 1] = (TILE,) * (rows // TILE)
    outward = {k: [[None] * SWAP for _ in sizes] for k, sizes in parts.items()}

    def pack(k, *after):
        packed[k] = pack_stage(zs, re, im, k, [chain[0], *after])
        chain[0] = packed[k][0]
        inward[k] = swap_out(packed[k])
        across[k] = [flip(packed[k][0], devices // 2)]

    def cross(k):
        across[k] += [flip(v, devices // 2) for v in inward[k][1:]]

    def mixing(k):
        (mixed[k],) = kernel(mix_stage, x_coef, inward[k], across[k], False)
        spread[k] = flip(mixed[k], devices // 4)

    def swapping(k):
        mixed[k] = kernel(swap_stage, zs, core_coef, z_turn, mixed[k], spread[k], True)
        for t in range(w_bits - 1, -1, -1):
            spread[k] = [None] * SWAP
            for s in sum(GROUPS, ()):
                spread[k][s] = flip(mixed[k][s], 1 << t)
            if t:
                mixed[k] = kernel(mix_stage, w_coef[t], mixed[k], spread[k], True)

    def finish(k, n):
        mine, theirs = ([v[k][s] for s in GROUPS[n]] for v in (mixed, spread))
        shared = (w_coef[0], turns[k], scale, row_table)
        pieces = kernel(row_stage, *shared, mine, theirs, k, GROUPS[n], parts[k])
        for p, piece in enumerate(pieces):
            for s, value in zip(GROUPS[n], piece):
                outward[k][p][s] = flip(value, s * weights) if s else value

    pack(0), pack(1, row_table, *scale, *turns[0]), pack(2), pack(3)
    cross(0), cross(1), mixing(0), swapping(0), mixing(1), cross(2)
    for k in range(1, SLICES):
        finish(k - 1, 0), swapping(k), finish(k - 1, 1)
        if k + 1 < SLICES:
            if k + 2 < SLICES:
                cross(k + 2)
            mixing(k + 1)
    finish(SLICES - 1, 0), finish(SLICES - 1, 1)
    outs, start, last = None, 0, SLICES - 1
    for n, part in enumerate(parts[last]):
        sources = [(outward[k][0], 0) for k in range(last)] + [(outward[last][n], start)]
        outs = lane_stage(zs, sources, outs, start, part, rows, mid, inner, lane_table)
        start += part
    return tuple(values.reshape(local) for values in outs)


def solution(mesh):
    spec = P(AXES)
    return jax.shard_map(
        on_device, mesh=mesh, in_specs=(spec, spec), out_specs=(spec, spec, spec), check_vma=False
    )
```

time: 457 us -> 551 us (1.21)
  starting transfers between devices: 18.3 us -> 146 us
  waiting for transfers between devices: 338 us -> 246 us
  Pallas kernels: 77.7 us -> 128 us
  other arithmetic: 6.52 us -> 18.1 us
  local copies, waits for them, and re-layouts: 13.4 us -> 6.63 us
    all_to_all x4 -> x0, waiting for transfers between devices: 338 us -> none  [exchange(): return lax.all_to_all(x, AXES, split_axis=0, concat_axis=0, tiled=True)]
    ppermute x0 -> x69, waiting for transfers between devices: none -> 246 us  [flip(): lax.ppermute(values, AXES, [(i, i ^ distance) for i in range(devices)])]
    ppermute x0 -> x69, starting transfers between devices: none -> 146 us  [flip(): lax.ppermute(values, AXES, [(i, i ^ distance) for i in range(devices)])]
    pallas_call x5 -> x24, Pallas kernels: 77.7 us -> 128 us  [the longest x8 51.8 us: row_stage(): pl.pallas_call(functools.partial(row_kernel, c, slots, sizes), in_specs=[...]
    all_to_all x4 -> x0, starting transfers between devices: 18.3 us -> none  [exchange(): return lax.all_to_all(x, AXES, split_axis=0, concat_axis=0, tiled=True)]
    reshape x2 -> x0, local copies, waits for them, and re-layouts: 13.3 us -> none  [outgoing(): return jnp.swapaxes(values.reshape(rows, devices, LANES), 0, 1)]
    sin x2 -> x4, other arithmetic: 2.49 us -> 9.52 us  [phases(): return (jnp.cos(angle), jnp.sin(angle))]
    unnamed x8 -> x110, local copies, waits for them, and re-layouts: 0.01 us -> 5.95 us
  transfers between devices with their start and end apart: 4 -> 69, of which waited for: 4 -> 26; matrix products, arithmetic and copies ran while one was open for 3% -> 3% of each run, Pallas kernels for 7% -> 18%
where the time goes in v2:
time: 551 us; the launch traced here: 549 us
  waiting for transfers between devices  246 us (45%)
  starting transfers between devices  146 us (26%)
  Pallas kernels  128 us (23%)
  other arithmetic  18.1 us (3%)
  local copies, waits for them, and re-layouts  6.63 us (1%)
    ppermute x69, waiting for transfers between devices, flip(): lax.ppermute(values, AXES, [(i, i ^ distance) for i in range(devices)])  246 us
    ppermute x69, starting transfers between devices, flip(): lax.ppermute(values, AXES, [(i, i ^ distance) for i in range(devices)])  146 us
    pallas_call x8, Pallas kernels, row_stage(): pl.pallas_call(functools.partial(row_kernel, c, slots, sizes), in_specs=[...  51.8 us
    pallas_call x4, Pallas kernels, lane_stage(): pl.pallas_call(kernel, grid=(part // block,), in_specs=specs, out_specs=[...  22 us
    pallas_call x4, Pallas kernels, swap_stage(): pl.pallas_call(swap_kernel, grid=(rows // block,), in_specs=[SCALAR, SCAL...  18.8 us
    pallas_call x4, Pallas kernels, mix_stage(): pl.pallas_call(functools.partial(mix_kernel, len(mine)), grid=(rows // bl...  17.7 us
    pallas_call x4, Pallas kernels, pack_stage(): pl.pallas_call(functools.partial(pack_kernel, c * SWAP % tile), grid=(row...  17.5 us
  transfers between devices with their start and end apart: 69, of which 26 were waited for; matrix products, arithmetic and copies ran while one was open for 3% of the time, Pallas kernels for 18%

profile of v2, /device:TPU:0, one launch (start us, length us, event | category | flops | bytes accessed | tf_op | source)
XLA Modules:
  0.0 548.5 jit_solution(3667011831279320794)
XLA Ops:
  22.8 7.8 %collective-permute-done.refs_1_ = f32[2,512,128]{2,1,0:T(8,128)S(1)} collective-permute-done((f32[2,512,128]{2,1,0:T(8,128)}, f32[2,512,128]{2,1,0:T(8,128)S(1)}, u32[]{:S(2)}, u32[]{:S(2)}) %collective-permute-start) | collective-permute-done | bytes 524320 | tf_op jit(solution)/shard_map/ppermute | solution.py:312
  32.3 14.1 %collective-permute-done.1.refs_2_ = f32[2,512,128]{2,1,0:T(8,128)S(1)} collective-permute-done((f32[2,512,128]{2,1,0:T(8,128)}, f32[2,512,128]{2,1,0:T(8,128)S(1)}, u32[]{:S(2)}, u32[]{:S(2)}) %collective-permute-start.1) | collective-permute-done | bytes 524320 | tf_op jit(solution)/shard_map/ppermute | solution.py:312
  49.1 5.6 %fusion.28 = (f32[512,4]{1,0:T(8,128)}, f32[512,4]{1,0:T(8,128)}, f32[512,4]{1,0:T(8,128)}, f32[512,4]{1,0:T(8,128)}, f32[512,4]{1,0:T(8,128)}, /*index=5*/f32[512,4]{1,0:T(8,128)}, f32[512,4]{1,0:T(8,128)}, f32[512,4]{1,0:T(8,128)}) fusion(s32[4]{0:T(128)S(1)} %get-tuple-element.177, s32[512]{0:T(512)S(1)} %fusion.40, s32[512]{0:T(512)S(1)} %fusion.43, ...), kind=kLoop, calls=%fused_computation.66 | loop fusion | flops 114688 | bytes 73744 | tf_op jit(solution)/shard_map/sin | solution.py:36
  54.7 4.4 pack_stage.5
  59.1 4.4 pack_stage.6
  63.5 4.4 pack_stage.7
  69.7 4.4 mix_stage.4.after_ref.mine_ref
  74.1 10.0 %collective-permute-start.8 = (f32[2,512,128]{2,1,0:T(8,128)}, f32[2,512,128]{2,1,0:T(8,128)S(1)}, u32[]{:S(2)}, u32[]{:S(2)}) collective-permute-start(f32[2,512,128]{2,1,0:T(8,128)} %get-tuple-element.83), channel_id=1, source_target_pairs={{0,2},{1,3},{2,0},{3,1},{4,6},{5,7},{6,4},{7,5},{8,10},{9,11},{10,... | collective-permute-start | bytes 1572872 | tf_op jit(solution)/shard_map/ppermute | solution.py:312
  87.0 20.5 %collective-permute-done.8.refs_1_ = f32[2,512,128]{2,1,0:T(8,128)S(1)} collective-permute-done((f32[2,512,128]{2,1,0:T(8,128)}, f32[2,512,128]{2,1,0:T(8,128)S(1)}, u32[]{:S(2)}, u32[]{:S(2)}) %collective-permute-start.8) | collective-permute-done | bytes 524320 | tf_op jit(solution)/shard_map/ppermute | solution.py:312
  108.1 14.5 %collective-permute-done.9.refs_2_ = f32[2,512,128]{2,1,0:T(8,128)} collective-permute-done((f32[2,512,128]{2,1,0:T(8,128)}, f32[2,512,128]{2,1,0:T(8,128)}, u32[]{:S(2)}, u32[]{:S(2)}) %collective-permute-start.9) | collective-permute-done | bytes 524320 | tf_op jit(solution)/shard_map/ppermute | solution.py:312
  127.2 4.7 swap_stage.4
  131.9 5.7 %collective-permute-done.13.refs_6_ = f32[2,512,128]{2,1,0:T(8,128)} collective-permute-done((f32[2,512,128]{2,1,0:T(8,128)}, f32[2,512,128]{2,1,0:T(8,128)}, u32[]{:S(2)}, u32[]{:S(2)}) %collective-permute-start.13) | collective-permute-done | bytes 524320 | tf_op jit(solution)/shard_map/ppermute | solution.py:312
  137.7 6.2 %collective-permute-done.14.refs_7_ = f32[2,512,128]{2,1,0:T(8,128)} collective-permute-done((f32[2,512,128]{2,1,0:T(8,128)}, f32[2,512,128]{2,1,0:T(8,128)}, u32[]{:S(2)}, u32[]{:S(2)}) %collective-permute-start.14) | collective-permute-done | bytes 524320 | tf_op jit(solution)/shard_map/ppermute | solution.py:312
  143.9 4.4 mix_stage.5.after_ref.mine_ref
  155.5 19.6 %collective-permute-done.23.refs_1_ = f32[2,512,128]{2,1,0:T(8,128)} collective-permute-done((f32[2,512,128]{2,1,0:T(8,128)}, f32[2,512,128]{2,1,0:T(8,128)}, u32[]{:S(2)}, u32[]{:S(2)}) %collective-permute-start.23) | collective-permute-done | bytes 524320 | tf_op jit(solution)/shard_map/ppermute | solution.py:312
  176.6 13.4 %collective-permute-done.24.refs_2_ = f32[2,512,128]{2,1,0:T(8,128)} collective-permute-done((f32[2,512,128]{2,1,0:T(8,128)}, f32[2,512,128]{2,1,0:T(8,128)}, u32[]{:S(2)}, u32[]{:S(2)}) %collective-permute-start.24) | collective-permute-done | bytes 524320 | tf_op jit(solution)/shard_map/ppermute | solution.py:312
  194.2 10.9 %collective-permute-done.18.refs_2_ = f32[2,512,128]{2,1,0:T(8,128)S(1)} collective-permute-done((f32[2,512,128]{2,1,0:T(8,128)}, f32[2,512,128]{2,1,0:T(8,128)S(1)}, u32[]{:S(2)}, u32[]{:S(2)}) %collective-permute-start.18) | collective-permute-done | bytes 524320 | tf_op jit(solution)/shard_map/ppermute | solution.py:312
  207.8 6.8 %row_stage.8 = (f32[2,512,128]{2,1,0:T(8,128)}, f32[2,512,128]{2,1,0:T(8,128)}) custom-call(f32[9]{0:T(128)} %pad_maximum_fusion.2.coef_ref, f32[4,2,512,128]{3,2,1,0:T(8,128)} %mix_stage.5.after_ref.mine_ref, f32[512,4]{1,0:T(8,128)} %get-tuple-element.167.refs_4_.tc_ref, f32[512,4]{1,0:T(8,128)} %get-tuple-element.168.refs_5_.ts_ref, ...), custom_call_target="tpu_custom_call" | custom-call | flops 209715200 | bytes 8388608 | tf_op jit(solution)/shard_map/row_stage/pallas_call | solution.py:218
  214.6 4.7 swap_stage.5
  219.3 6.8 %row_stage.9 = (f32[2,512,128]{2,1,0:T(8,128)}, f32[2,512,128]{2,1,0:T(8,128)}) custom-call(f32[9]{0:T(128)} %pad_maximum_fusion.2.coef_ref, f32[2,512,128]{2,1,0:T(8,128)} %get-tuple-element.89.after_ref.refs_1_, f32[512,4]{1,0:T(8,128)} %get-tuple-element.167.refs_4_.tc_ref, f32[512,4]{1,0:T(8,128)} %get-tuple-element.168.refs_5_.ts_ref, ...), custom_call_target="tpu_custom_call" | custom-call | flops 209715200 | bytes 8388608 | tf_op jit(solution)/shard_map/row_stage/pallas_call | solution.py:218
  229.5 8.1 %collective-permute-done.29.refs_7_ = f32[2,512,128]{2,1,0:T(8,128)} collective-permute-done((f32[2,512,128]{2,1,0:T(8,128)}, f32[2,512,128]{2,1,0:T(8,128)}, u32[]{:S(2)}, u32[]{:S(2)}) %collective-permute-start.29) | collective-permute-done | bytes 524320 | tf_op jit(solution)/shard_map/ppermute | solution.py:312
  237.6 4.4 mix_stage.6.after_ref.mine_ref
  242.0 11.8 %collective-permute-start.38 = (f32[2,512,128]{2,1,0:T(8,128)}, f32[2,512,128]{2,1,0:T(8,128)}, u32[]{:S(2)}, u32[]{:S(2)}) collective-permute-start(f32[2,512,128]{2,1,0:T(8,128)} %get-tuple-element.105), channel_id=1, source_target_pairs={{0,2},{1,3},{2,0},{3,1},{4,6},{5,7},{6,4},{7,5},{8,10},{9,11},{10,... | collective-permute-start | bytes 1572872 | tf_op jit(solution)/shard_map/ppermute | solution.py:312
  256.8 20.6 %collective-permute-done.38.refs_1_ = f32[2,512,128]{2,1,0:T(8,128)} collective-permute-done((f32[2,512,128]{2,1,0:T(8,128)}, f32[2,512,128]{2,1,0:T(8,128)}, u32[]{:S(2)}, u32[]{:S(2)}) %collective-permute-start.38) | collective-permute-done | bytes 524320 | tf_op jit(solution)/shard_map/ppermute | solution.py:312
  277.9 14.4 %collective-permute-done.39.refs_2_ = f32[2,512,128]{2,1,0:T(8,128)} collective-permute-done((f32[2,512,128]{2,1,0:T(8,128)}, f32[2,512,128]{2,1,0:T(8,128)}, u32[]{:S(2)}, u32[]{:S(2)}) %collective-permute-start.39) | collective-permute-done | bytes 524320 | tf_op jit(solution)/shard_map/ppermute | solution.py:312
  296.4 10.9 %collective-permute-done.33.refs_2_ = f32[2,512,128]{2,1,0:T(8,128)S(1)} collective-permute-done((f32[2,512,128]{2,1,0:T(8,128)}, f32[2,512,128]{2,1,0:T(8,128)S(1)}, u32[]{:S(2)}, u32[]{:S(2)}) %collective-permute-start.33) | collective-permute-done | bytes 524320 | tf_op jit(solution)/shard_map/ppermute | solution.py:312
  309.4 6.8 %row_stage.10 = (f32[2,512,128]{2,1,0:T(8,128)}, f32[2,512,128]{2,1,0:T(8,128)}) custom-call(f32[9]{0:T(128)} %pad_maximum_fusion.2.coef_ref, f32[4,2,512,128]{3,2,1,0:T(8,128)} %mix_stage.6.after_ref.mine_ref, f32[512,4]{1,0:T(8,128)} %get-tuple-element.169.tc_ref, f32[512,4]{1,0:T(8,128)} %get-tuple-element.170.ts_ref, ...), custom_call_target="tpu_custom_call" | custom-call | flops 209715200 | bytes 8388608 | tf_op jit(solution)/shard_map/row_stage/pallas_call | solution.py:218
  316.2 4.7 swap_stage.6
  320.9 6.8 %row_stage.11 = (f32[2,512,128]{2,1,0:T(8,128)}, f32[2,512,128]{2,1,0:T(8,128)}) custom-call(f32[9]{0:T(128)} %pad_maximum_fusion.2.coef_ref, f32[2,512,128]{2,1,0:T(8,128)} %get-tuple-element.100.after_ref.refs_1_, f32[512,4]{1,0:T(8,128)} %get-tuple-element.169.tc_ref, f32[512,4]{1,0:T(8,128)} %get-tuple-element.170.ts_ref, ...), custom_call_target="tpu_custom_call" | custom-call | flops 209715200 | bytes 8388608 | tf_op jit(solution)/shard_map/row_stage/pallas_call | solution.py:218
  331.8 7.1 %collective-permute-done.44.refs_7_ = f32[2,512,128]{2,1,0:T(8,128)} collective-permute-done((f32[2,512,128]{2,1,0:T(8,128)}, f32[2,512,128]{2,1,0:T(8,128)}, u32[]{:S(2)}, u32[]{:S(2)}) %collective-permute-start.44) | collective-permute-done | bytes 524320 | tf_op jit(solution)/shard_map/ppermute | solution.py:312
  338.8 4.5 mix_stage.7.after_ref.mine_ref
  349.0 9.5 %collective-permute-start.21 = (f32[2,512,128]{2,1,0:T(8,128)}, f32[2,512,128]{2,1,0:T(8,128)S(1)}, u32[]{:S(2)}, u32[]{:S(2)}) collective-permute-start(f32[2,512,128]{2,1,0:T(8,128)} %get-tuple-element.88.after_ref), channel_id=1, source_target_pairs={{0,4},{1,5},{2,6},{3,7},{4,0},{5,1},{6,2},{7,3},{8,12},{9,13},{10,... | collective-permute-start | bytes 1572872 | tf_op jit(solution)/shard_map/ppermute | solution.py:312
  359.6 23.1 %collective-permute-start.20 = (f32[2,512,128]{2,1,0:T(8,128)}, f32[2,512,128]{2,1,0:T(8,128)S(1)}, u32[]{:S(2)}, u32[]{:S(2)}) collective-permute-start(f32[2,512,128]{2,1,0:T(8,128)} %get-tuple-element.92.after_ref), channel_id=1, source_target_pairs={{0,2},{1,3},{2,0},{3,1},{4,6},{5,7},{6,4},{7,5},{8,10},{9,11},{10,... | collective-permute-start | bytes 1572872 | tf_op jit(solution)/shard_map/ppermute | solution.py:312
  387.0 6.9 %row_stage.12 = (f32[2,512,128]{2,1,0:T(8,128)}, f32[2,512,128]{2,1,0:T(8,128)}) custom-call(f32[9]{0:T(128)} %pad_maximum_fusion.2.coef_ref, f32[4,2,512,128]{3,2,1,0:T(8,128)} %mix_stage.7.after_ref.mine_ref, f32[512,4]{1,0:T(8,128)} %get-tuple-element.171.tc_ref, f32[512,4]{1,0:T(8,128)} %get-tuple-element.172.ts_ref, ...), custom_call_target="tpu_custom_call" | custom-call | flops 209715200 | bytes 8388608 | tf_op jit(solution)/shard_map/row_stage/pallas_call | solution.py:218
  394.4 4.7 swap_stage.7
  400.2 15.6 %collective-permute-done.20.refs_1_ = f32[2,512,128]{2,1,0:T(8,128)S(1)} collective-permute-done((f32[2,512,128]{2,1,0:T(8,128)}, f32[2,512,128]{2,1,0:T(8,128)S(1)}, u32[]{:S(2)}, u32[]{:S(2)}) %collective-permute-start.20) | collective-permute-done | bytes 524320 | tf_op jit(solution)/shard_map/ppermute | solution.py:312
  417.8 20.4 %collective-permute-done.36.refs_6_ = f32[2,512,128]{2,1,0:T(8,128)S(1)} collective-permute-done((f32[2,512,128]{2,1,0:T(8,128)}, f32[2,512,128]{2,1,0:T(8,128)S(1)}, u32[]{:S(2)}, u32[]{:S(2)}) %collective-permute-start.36) | collective-permute-done | bytes 524320 | tf_op jit(solution)/shard_map/ppermute | solution.py:312
  444.4 7.0 %row_stage.13 = (f32[2,512,128]{2,1,0:T(8,128)}, f32[2,512,128]{2,1,0:T(8,128)}) custom-call(f32[9]{0:T(128)} %pad_maximum_fusion.2.coef_ref, f32[2,512,128]{2,1,0:T(8,128)} %get-tuple-element.111.after_ref.refs_1_, f32[512,4]{1,0:T(8,128)} %get-tuple-element.171.tc_ref, f32[512,4]{1,0:T(8,128)} %get-tuple-element.172.ts_ref, ...), custom_call_target="tpu_custom_call" | custom-call | flops 209715200 | bytes 8388608 | tf_op jit(solution)/shard_map/row_stage/pallas_call | solution.py:218
  454.2 5.3 row_stage.14
  459.5 17.3 %collective-permute-start.61 = (f32[2,128,128]{2,1,0:T(8,128)}, f32[2,128,128]{2,1,0:T(8,128)S(1)}, u32[]{:S(2)}, u32[]{:S(2)}) collective-permute-start(f32[2,128,128]{2,1,0:T(8,128)} %get-tuple-element.126), channel_id=1, source_target_pairs={{0,4},{1,5},{2,6},{3,7},{4,0},{5,1},{6,2},{7,3},{8,12},{9,13},{10,... | collective-permute-start | bytes 393224 | tf_op jit(solution)/shard_map/ppermute | solution.py:312
  476.8 13.8 %collective-permute-done.51.refs_10_ = f32[2,512,128]{2,1,0:T(8,128)} collective-permute-done((f32[2,512,128]{2,1,0:T(8,128)}, f32[2,512,128]{2,1,0:T(8,128)}, u32[]{:S(2)}, u32[]{:S(2)}) %collective-permute-start.51) | collective-permute-done | bytes 524320 | tf_op jit(solution)/shard_map/ppermute | solution.py:312
  494.5 5.4 row_stage.15
  501.1 4.9 collective-permute-done.61.refs_14_
  508.8 4.8 collective-permute-start.63
  524.8 5.5 lane_stage.4
  530.3 5.5 %lane_stage.5 = (f32[512,16,128]{2,1,0:T(8,128)}, f32[512,16,128]{2,1,0:T(8,128)}, f32[512,16,128]{2,1,0:T(8,128)}) custom-call(s32[1]{0:T(128)} %bitcast.z_ref.refs_0_, f32[512,128]{1,0:T(8,128)} %get-tuple-element.166.mc_ref, f32[512,128]{1,0:T(8,128)} %get-tuple-element.165.ms_ref, ...), custom_call_target="tpu_custom_call", output_to_operand_aliasing={{0}: (22, {}), {1}: (23, {}), {2}: (24, {})} | custom-call | flops 671088640 | bytes 5242880 | tf_op jit(solution)/shard_map/lane_stage/pallas_call | solution.py:277
  536.6 5.5 %lane_stage.6 = (f32[512,16,128]{2,1,0:T(8,128)}, f32[512,16,128]{2,1,0:T(8,128)}, f32[512,16,128]{2,1,0:T(8,128)}) custom-call(s32[1]{0:T(128)} %bitcast.z_ref.refs_0_, f32[512,128]{1,0:T(8,128)} %get-tuple-element.166.mc_ref, f32[512,128]{1,0:T(8,128)} %get-tuple-element.165.ms_ref, ...), custom_call_target="tpu_custom_call", output_to_operand_aliasing={{0}: (22, {}), {1}: (23, {}), {2}: (24, {})} | custom-call | flops 671088640 | bytes 5242880 | tf_op jit(solution)/shard_map/lane_stage/pallas_call | solution.py:277
  542.9 5.5 %lane_stage.7 = (f32[512,16,128]{2,1,0:T(8,128)}, f32[512,16,128]{2,1,0:T(8,128)}, f32[512,16,128]{2,1,0:T(8,128)}) custom-call(s32[1]{0:T(128)} %bitcast.z_ref.refs_0_, f32[512,128]{1,0:T(8,128)} %get-tuple-element.166.mc_ref, f32[512,128]{1,0:T(8,128)} %get-tuple-element.165.ms_ref, ...), custom_call_target="tpu_custom_call", output_to_operand_aliasing={{0}: (22, {}), {1}: (23, {}), {2}: (24, {})} | custom-call | flops 671088640 | bytes 5242880 | tf_op jit(solution)/shard_map/lane_stage/pallas_call | solution.py:277
  (247 shorter events, 110.8 us)
Async XLA Ops:
  5.0 25.7 %collective-permute-start = (f32[2,512,128]{2,1,0:T(8,128)}, f32[2,512,128]{2,1,0:T(8,128)S(1)}, u32[]{:S(2)}, u32[]{:S(2)}) collective-permute-start(f32[2,512,128]{2,1,0:T(8,128)} %get-tuple-element.79), channel_id=1, source_target_pairs={{0,2},{1,3},{2,0},{3,1},{4,6},{5,7},{6,4},{7,5},{8,10},{9,11},{10,... | collective-permute-start | bytes 1572872 | tf_op jit(solution)/shard_map/ppermute | solution.py:312
  8.0 38.4 %collective-permute-start.1 = (f32[2,512,128]{2,1,0:T(8,128)}, f32[2,512,128]{2,1,0:T(8,128)S(1)}, u32[]{:S(2)}, u32[]{:S(2)}) collective-permute-start(f32[2,512,128]{2,1,0:T(8,128)} %get-tuple-element.80), channel_id=1, source_target_pairs={{0,4},{1,5},{2,6},{3,7},{4,0},{5,1},{6,2},{7,3},{8,12},{9,13},{10,... | collective-permute-start | bytes 1572872 | tf_op jit(solution)/shard_map/ppermute | solution.py:312
  10.6 37.3 %collective-permute-start.2 = (f32[2,512,128]{2,1,0:T(8,128)}, f32[2,512,128]{2,1,0:T(8,128)S(1)}, u32[]{:S(2)}, u32[]{:S(2)}) collective-permute-start(f32[2,512,128]{2,1,0:T(8,128)} %get-tuple-element.81), channel_id=1, source_target_pairs={{0,6},{1,7},{2,4},{3,5},{4,2},{5,3},{6,0},{7,1},{8,14},{9,15},{10,... | collective-permute-start | bytes 1572872 | tf_op jit(solution)/shard_map/ppermute | solution.py:312
  10.6 57.9 %collective-permute-start.3 = (f32[2,512,128]{2,1,0:T(8,128)}, f32[2,512,128]{2,1,0:T(8,128)S(1)}, u32[]{:S(2)}, u32[]{:S(2)}) collective-permute-start(f32[2,512,128]{2,1,0:T(8,128)} %get-tuple-element.75.refs_0_), channel_id=1, source_target_pairs={{0,16},{1,17},{2,18},{3,19},{4,20},{5,21},{6,22},{7,23},{8,24},{9,... | collective-permute-start | bytes 1572872 | tf_op jit(solution)/shard_map/ppermute | solution.py:312
  30.7 37.9 %collective-permute-start.4 = (f32[2,512,128]{2,1,0:T(8,128)S(1)}, f32[2,512,128]{2,1,0:T(8,128)S(1)}, u32[]{:S(2)}, u32[]{:S(2)}) collective-permute-start(f32[2,512,128]{2,1,0:T(8,128)S(1)} %collective-permute-done.refs_1_), channel_id=1, source_target_pairs={{0,16},{1,17},{2,18},{3,19},{4,20},{5,21},{6,22},{7,23},{8,24},{9,... | collective-permute-start | bytes 1572872 | tf_op jit(solution)/shard_map/ppermute | solution.py:312
  74.1 51.8 %collective-permute-start.7 = (f32[4,2,512,128]{3,2,1,0:T(8,128)}, f32[4,2,512,128]{3,2,1,0:T(8,128)S(1)}, u32[]{:S(2)}, u32[]{:S(2)}) collective-permute-start(f32[4,2,512,128]{3,2,1,0:T(8,128)} %mix_stage.4.after_ref.mine_ref), channel_id=1, source_target_pairs={{0,8},{1,9},{2,10},{3,11},{4,12},{5,13},{6,14},{7,15},{8,0},{9,1},... | collective-permute-start | bytes 6291464 | tf_op jit(solution)/shard_map/ppermute | solution.py:312
  74.1 33.5 %collective-permute-start.8 = (f32[2,512,128]{2,1,0:T(8,128)}, f32[2,512,128]{2,1,0:T(8,128)S(1)}, u32[]{:S(2)}, u32[]{:S(2)}) collective-permute-start(f32[2,512,128]{2,1,0:T(8,128)} %get-tuple-element.83), channel_id=1, source_target_pairs={{0,2},{1,3},{2,0},{3,1},{4,6},{5,7},{6,4},{7,5},{8,10},{9,11},{10,... | collective-permute-start | bytes 1572872 | tf_op jit(solution)/shard_map/ppermute | solution.py:312
  84.0 38.5 %collective-permute-start.9 = (f32[2,512,128]{2,1,0:T(8,128)}, f32[2,512,128]{2,1,0:T(8,128)}, u32[]{:S(2)}, u32[]{:S(2)}) collective-permute-start(f32[2,512,128]{2,1,0:T(8,128)} %get-tuple-element.84), channel_id=1, source_target_pairs={{0,4},{1,5},{2,6},{3,7},{4,0},{5,1},{6,2},{7,3},{8,12},{9,13},{10,... | collective-permute-start | bytes 1572872 | tf_op jit(solution)/shard_map/ppermute | solution.py:312
  85.1 38.0 %collective-permute-start.10 = (f32[2,512,128]{2,1,0:T(8,128)}, f32[2,512,128]{2,1,0:T(8,128)}, u32[]{:S(2)}, u32[]{:S(2)}) collective-permute-start(f32[2,512,128]{2,1,0:T(8,128)} %get-tuple-element.85), channel_id=1, source_target_pairs={{0,6},{1,7},{2,4},{3,5},{4,2},{5,3},{6,0},{7,1},{8,14},{9,15},{10,... | collective-permute-start | bytes 1572872 | tf_op jit(solution)/shard_map/ppermute | solution.py:312
  86.5 45.4 %collective-permute-start.11 = (f32[2,512,128]{2,1,0:T(8,128)S(1)}, f32[2,512,128]{2,1,0:T(8,128)}, u32[]{:S(2)}, u32[]{:S(2)}) collective-permute-start(f32[2,512,128]{2,1,0:T(8,128)S(1)} %copy-done.14), channel_id=1, source_target_pairs={{0,16},{1,17},{2,18},{3,19},{4,20},{5,21},{6,22},{7,23},{8,24},{9,... | collective-permute-start | bytes 1572872 | tf_op jit(solution)/shard_map/ppermute | solution.py:312
  148.3 57.2 %collective-permute-start.17 = (f32[4,2,512,128]{3,2,1,0:T(8,128)}, f32[4,2,512,128]{3,2,1,0:T(8,128)S(1)}, u32[]{:S(2)}, u32[]{:S(2)}) collective-permute-start(f32[4,2,512,128]{3,2,1,0:T(8,128)} %mix_stage.5.after_ref.mine_ref), channel_id=1, source_target_pairs={{0,8},{1,9},{2,10},{3,11},{4,12},{5,13},{6,14},{7,15},{8,0},{9,1},... | collective-permute-start | bytes 6291464 | tf_op jit(solution)/shard_map/ppermute | solution.py:312
  148.4 26.8 %collective-permute-start.23 = (f32[2,512,128]{2,1,0:T(8,128)}, f32[2,512,128]{2,1,0:T(8,128)}, u32[]{:S(2)}, u32[]{:S(2)}) collective-permute-start(f32[2,512,128]{2,1,0:T(8,128)} %get-tuple-element.94), channel_id=1, source_target_pairs={{0,2},{1,3},{2,0},{3,1},{4,6},{5,7},{6,4},{7,5},{8,10},{9,11},{10,... | collective-permute-start | bytes 1572872 | tf_op jit(solution)/shard_map/ppermute | solution.py:312
  151.5 38.5 %collective-permute-start.24 = (f32[2,512,128]{2,1,0:T(8,128)}, f32[2,512,128]{2,1,0:T(8,128)}, u32[]{:S(2)}, u32[]{:S(2)}) collective-permute-start(f32[2,512,128]{2,1,0:T(8,128)} %get-tuple-element.95), channel_id=1, source_target_pairs={{0,4},{1,5},{2,6},{3,7},{4,0},{5,1},{6,2},{7,3},{8,12},{9,13},{10,... | collective-permute-start | bytes 1572872 | tf_op jit(solution)/shard_map/ppermute | solution.py:312
  154.0 37.6 %collective-permute-start.25 = (f32[2,512,128]{2,1,0:T(8,128)}, f32[2,512,128]{2,1,0:T(8,128)}, u32[]{:S(2)}, u32[]{:S(2)}) collective-permute-start(f32[2,512,128]{2,1,0:T(8,128)} %get-tuple-element.96), channel_id=1, source_target_pairs={{0,6},{1,7},{2,4},{3,5},{4,2},{5,3},{6,0},{7,1},{8,14},{9,15},{10,... | collective-permute-start | bytes 1572872 | tf_op jit(solution)/shard_map/ppermute | solution.py:312
  154.0 38.1 %collective-permute-start.15 = (f32[2,512,128]{2,1,0:T(8,128)}, f32[2,512,128]{2,1,0:T(8,128)S(1)}, u32[]{:S(2)}, u32[]{:S(2)}) collective-permute-start(f32[2,512,128]{2,1,0:T(8,128)} %get-tuple-element.86.refs_0_), channel_id=1, source_target_pairs={{0,1},{1,0},{2,3},{3,2},{4,5},{5,4},{6,7},{7,6},{8,9},{9,8},{10,11... | collective-permute-start | bytes 1572872 | tf_op jit(solution)/shard_map/ppermute | solution.py:312
  191.6 27.8 %collective-permute-start.19 = (f32[2,512,128]{2,1,0:T(8,128)S(1)}, f32[2,512,128]{2,1,0:T(8,128)}, u32[]{:S(2)}, u32[]{:S(2)}) collective-permute-start(f32[2,512,128]{2,1,0:T(8,128)S(1)} %copy-done.13), channel_id=1, source_target_pairs={{0,1},{1,0},{2,3},{3,2},{4,5},{5,4},{6,7},{7,6},{8,9},{9,8},{10,11... | collective-permute-start | bytes 1572872 | tf_op jit(solution)/shard_map/ppermute | solution.py:312
  192.1 34.1 %collective-permute-start.26 = (f32[2,512,128]{2,1,0:T(8,128)S(1)}, f32[2,512,128]{2,1,0:T(8,128)}, u32[]{:S(2)}, u32[]{:S(2)}) collective-permute-start(f32[2,512,128]{2,1,0:T(8,128)S(1)} %copy-done.12), channel_id=1, source_target_pairs={{0,16},{1,17},{2,18},{3,19},{4,20},{5,21},{6,22},{7,23},{8,24},{9,... | collective-permute-start | bytes 1572872 | tf_op jit(solution)/shard_map/ppermute | solution.py:312
  192.7 33.5 %collective-permute-start.27 = (f32[2,512,128]{2,1,0:T(8,128)}, f32[2,512,128]{2,1,0:T(8,128)}, u32[]{:S(2)}, u32[]{:S(2)}) collective-permute-start(f32[2,512,128]{2,1,0:T(8,128)} %collective-permute-done.23.refs_1_), channel_id=1, source_target_pairs={{0,16},{1,17},{2,18},{3,19},{4,20},{5,21},{6,22},{7,23},{8,24},{9,... | collective-permute-start | bytes 1572872 | tf_op jit(solution)/shard_map/ppermute | solution.py:312
  205.0 24.5 %collective-permute-start.28 = (f32[2,512,128]{2,1,0:T(8,128)}, f32[2,512,128]{2,1,0:T(8,128)}, u32[]{:S(2)}, u32[]{:S(2)}) collective-permute-start(f32[2,512,128]{2,1,0:T(8,128)} %collective-permute-done.24.refs_2_), channel_id=1, source_target_pairs={{0,16},{1,17},{2,18},{3,19},{4,20},{5,21},{6,22},{7,23},{8,24},{9,... | collective-permute-start | bytes 1572872 | tf_op jit(solution)/shard_map/ppermute | solution.py:312
  205.9 31.7 %collective-permute-start.29 = (f32[2,512,128]{2,1,0:T(8,128)}, f32[2,512,128]{2,1,0:T(8,128)}, u32[]{:S(2)}, u32[]{:S(2)}) collective-permute-start(f32[2,512,128]{2,1,0:T(8,128)} %collective-permute-done.25.refs_3_), channel_id=1, source_target_pairs={{0,16},{1,17},{2,18},{3,19},{4,20},{5,21},{6,22},{7,23},{8,24},{9,... | collective-permute-start | bytes 1572872 | tf_op jit(solution)/shard_map/ppermute | solution.py:312
  242.0 65.8 %collective-permute-start.32 = (f32[4,2,512,128]{3,2,1,0:T(8,128)}, f32[4,2,512,128]{3,2,1,0:T(8,128)S(1)}, u32[]{:S(2)}, u32[]{:S(2)}) collective-permute-start(f32[4,2,512,128]{3,2,1,0:T(8,128)} %mix_stage.6.after_ref.mine_ref), channel_id=1, source_target_pairs={{0,8},{1,9},{2,10},{3,11},{4,12},{5,13},{6,14},{7,15},{8,0},{9,1},... | collective-permute-start | bytes 6291464 | tf_op jit(solution)/shard_map/ppermute | solution.py:312
  242.0 35.4 %collective-permute-start.38 = (f32[2,512,128]{2,1,0:T(8,128)}, f32[2,512,128]{2,1,0:T(8,128)}, u32[]{:S(2)}, u32[]{:S(2)}) collective-permute-start(f32[2,512,128]{2,1,0:T(8,128)} %get-tuple-element.105), channel_id=1, source_target_pairs={{0,2},{1,3},{2,0},{3,1},{4,6},{5,7},{6,4},{7,5},{8,10},{9,11},{10,... | collective-permute-start | bytes 1572872 | tf_op jit(solution)/shard_map/ppermute | solution.py:312
  253.8 38.5 %collective-permute-start.39 = (f32[2,512,128]{2,1,0:T(8,128)}, f32[2,512,128]{2,1,0:T(8,128)}, u32[]{:S(2)}, u32[]{:S(2)}) collective-permute-start(f32[2,512,128]{2,1,0:T(8,128)} %get-tuple-element.106), channel_id=1, source_target_pairs={{0,4},{1,5},{2,6},{3,7},{4,0},{5,1},{6,2},{7,3},{8,12},{9,13},{10,... | collective-permute-start | bytes 1572872 | tf_op jit(solution)/shard_map/ppermute | solution.py:312
  254.9 38.0 %collective-permute-start.40 = (f32[2,512,128]{2,1,0:T(8,128)}, f32[2,512,128]{2,1,0:T(8,128)}, u32[]{:S(2)}, u32[]{:S(2)}) collective-permute-start(f32[2,512,128]{2,1,0:T(8,128)} %get-tuple-element.107), channel_id=1, source_target_pairs={{0,6},{1,7},{2,4},{3,5},{4,2},{5,3},{6,0},{7,1},{8,14},{9,15},{10,... | collective-permute-start | bytes 1572872 | tf_op jit(solution)/shard_map/ppermute | solution.py:312
  256.3 38.1 %collective-permute-start.30 = (f32[2,512,128]{2,1,0:T(8,128)}, f32[2,512,128]{2,1,0:T(8,128)S(1)}, u32[]{:S(2)}, u32[]{:S(2)}) collective-permute-start(f32[2,512,128]{2,1,0:T(8,128)} %get-tuple-element.97.refs_0_), channel_id=1, source_target_pairs={{0,1},{1,0},{2,3},{3,2},{4,5},{5,4},{6,7},{7,6},{8,9},{9,8},{10,11... | collective-permute-start | bytes 1572872 | tf_op jit(solution)/shard_map/ppermute | solution.py:312
  292.8 28.1 %collective-permute-start.34 = (f32[2,512,128]{2,1,0:T(8,128)S(1)}, f32[2,512,128]{2,1,0:T(8,128)}, u32[]{:S(2)}, u32[]{:S(2)}) collective-permute-start(f32[2,512,128]{2,1,0:T(8,128)S(1)} %copy-done.8), channel_id=1, source_target_pairs={{0,1},{1,0},{2,3},{3,2},{4,5},{5,4},{6,7},{7,6},{8,9},{9,8},{10,11... | collective-permute-start | bytes 1572872 | tf_op jit(solution)/shard_map/ppermute | solution.py:312
  294.4 33.4 %collective-permute-start.41 = (f32[2,512,128]{2,1,0:T(8,128)S(1)}, f32[2,512,128]{2,1,0:T(8,128)}, u32[]{:S(2)}, u32[]{:S(2)}) collective-permute-start(f32[2,512,128]{2,1,0:T(8,128)S(1)} %copy-done.15), channel_id=1, source_target_pairs={{0,16},{1,17},{2,18},{3,19},{4,20},{5,21},{6,22},{7,23},{8,24},{9,... | collective-permute-start | bytes 1572872 | tf_op jit(solution)/shard_map/ppermute | solution.py:312
  295.0 32.8 %collective-permute-start.42 = (f32[2,512,128]{2,1,0:T(8,128)}, f32[2,512,128]{2,1,0:T(8,128)}, u32[]{:S(2)}, u32[]{:S(2)}) collective-permute-start(f32[2,512,128]{2,1,0:T(8,128)} %collective-permute-done.38.refs_1_), channel_id=1, source_target_pairs={{0,16},{1,17},{2,18},{3,19},{4,20},{5,21},{6,22},{7,23},{8,24},{9,... | collective-permute-start | bytes 1572872 | tf_op jit(solution)/shard_map/ppermute | solution.py:312
  307.3 24.5 %collective-permute-start.43 = (f32[2,512,128]{2,1,0:T(8,128)}, f32[2,512,128]{2,1,0:T(8,128)}, u32[]{:S(2)}, u32[]{:S(2)}) collective-permute-start(f32[2,512,128]{2,1,0:T(8,128)} %collective-permute-done.39.refs_2_), channel_id=1, source_target_pairs={{0,16},{1,17},{2,18},{3,19},{4,20},{5,21},{6,22},{7,23},{8,24},{9,... | collective-permute-start | bytes 1572872 | tf_op jit(solution)/shard_map/ppermute | solution.py:312
  308.1 30.7 %collective-permute-start.44 = (f32[2,512,128]{2,1,0:T(8,128)}, f32[2,512,128]{2,1,0:T(8,128)}, u32[]{:S(2)}, u32[]{:S(2)}) collective-permute-start(f32[2,512,128]{2,1,0:T(8,128)} %collective-permute-done.40.refs_3_), channel_id=1, source_target_pairs={{0,16},{1,17},{2,18},{3,19},{4,20},{5,21},{6,22},{7,23},{8,24},{9,... | collective-permute-start | bytes 1572872 | tf_op jit(solution)/shard_map/ppermute | solution.py:312
  343.3 50.5 %collective-permute-start.47 = (f32[4,2,512,128]{3,2,1,0:T(8,128)}, f32[4,2,512,128]{3,2,1,0:T(8,128)}, u32[]{:S(2)}, u32[]{:S(2)}) collective-permute-start(f32[4,2,512,128]{3,2,1,0:T(8,128)} %mix_stage.7.after_ref.mine_ref), channel_id=1, source_target_pairs={{0,8},{1,9},{2,10},{3,11},{4,12},{5,13},{6,14},{7,15},{8,0},{9,1},... | collective-permute-start | bytes 6291464 | tf_op jit(solution)/shard_map/ppermute | solution.py:312
  347.0 35.8 %collective-permute-start.45 = (f32[2,512,128]{2,1,0:T(8,128)S(1)}, f32[2,512,128]{2,1,0:T(8,128)S(1)}, u32[]{:S(2)}, u32[]{:S(2)}) collective-permute-start(f32[2,512,128]{2,1,0:T(8,128)S(1)} %copy-done.23), channel_id=1, source_target_pairs={{0,1},{1,0},{2,3},{3,2},{4,5},{5,4},{6,7},{7,6},{8,9},{9,8},{10,11... | collective-permute-start | bytes 1572872 | tf_op jit(solution)/shard_map/ppermute | solution.py:312
  347.5 38.6 %collective-permute-start.46 = (f32[2,512,128]{2,1,0:T(8,128)S(1)}, f32[2,512,128]{2,1,0:T(8,128)S(1)}, u32[]{:S(2)}, u32[]{:S(2)}) collective-permute-start(f32[2,512,128]{2,1,0:T(8,128)S(1)} %copy-done.24), channel_id=1, source_target_pairs={{0,1},{1,0},{2,3},{3,2},{4,5},{5,4},{6,7},{7,6},{8,9},{9,8},{10,11... | collective-permute-start | bytes 1572872 | tf_op jit(solution)/shard_map/ppermute | solution.py:312
  349.0 50.1 %collective-permute-start.21 = (f32[2,512,128]{2,1,0:T(8,128)}, f32[2,512,128]{2,1,0:T(8,128)S(1)}, u32[]{:S(2)}, u32[]{:S(2)}) collective-permute-start(f32[2,512,128]{2,1,0:T(8,128)} %get-tuple-element.88.after_ref), channel_id=1, source_target_pairs={{0,4},{1,5},{2,6},{3,7},{4,0},{5,1},{6,2},{7,3},{8,12},{9,13},{10,... | collective-permute-start | bytes 1572872 | tf_op jit(solution)/shard_map/ppermute | solution.py:312
  359.6 56.1 %collective-permute-start.20 = (f32[2,512,128]{2,1,0:T(8,128)}, f32[2,512,128]{2,1,0:T(8,128)S(1)}, u32[]{:S(2)}, u32[]{:S(2)}) collective-permute-start(f32[2,512,128]{2,1,0:T(8,128)} %get-tuple-element.92.after_ref), channel_id=1, source_target_pairs={{0,2},{1,3},{2,0},{3,1},{4,6},{5,7},{6,4},{7,5},{8,10},{9,11},{10,... | collective-permute-start | bytes 1572872 | tf_op jit(solution)/shard_map/ppermute | solution.py:312
  382.8 34.4 %collective-permute-start.37 = (f32[2,512,128]{2,1,0:T(8,128)}, f32[2,512,128]{2,1,0:T(8,128)S(1)}, u32[]{:S(2)}, u32[]{:S(2)}) collective-permute-start(f32[2,512,128]{2,1,0:T(8,128)} %get-tuple-element.104), channel_id=1, source_target_pairs={{0,6},{1,7},{2,4},{3,5},{4,2},{5,3},{6,0},{7,1},{8,14},{9,15},{10,... | collective-permute-start | bytes 1572872 | tf_op jit(solution)/shard_map/ppermute | solution.py:312
  386.2 52.1 %collective-permute-start.36 = (f32[2,512,128]{2,1,0:T(8,128)}, f32[2,512,128]{2,1,0:T(8,128)S(1)}, u32[]{:S(2)}, u32[]{:S(2)}) collective-permute-start(f32[2,512,128]{2,1,0:T(8,128)} %get-tuple-element.99.after_ref), channel_id=1, source_target_pairs={{0,4},{1,5},{2,6},{3,7},{4,0},{5,1},{6,2},{7,3},{8,12},{9,13},{10,... | collective-permute-start | bytes 1572872 | tf_op jit(solution)/shard_map/ppermute | solution.py:312
  393.8 45.8 %collective-permute-start.48 = (f32[2,512,128]{2,1,0:T(8,128)S(1)}, f32[2,512,128]{2,1,0:T(8,128)}, u32[]{:S(2)}, u32[]{:S(2)}) collective-permute-start(f32[2,512,128]{2,1,0:T(8,128)S(1)} %copy-done.16), channel_id=1, source_target_pairs={{0,1},{1,0},{2,3},{3,2},{4,5},{5,4},{6,7},{7,6},{8,9},{9,8},{10,11... | collective-permute-start | bytes 1572872 | tf_op jit(solution)/shard_map/ppermute | solution.py:312
  399.1 43.1 %collective-permute-start.35 = (f32[2,512,128]{2,1,0:T(8,128)}, f32[2,512,128]{2,1,0:T(8,128)S(1)}, u32[]{:S(2)}, u32[]{:S(2)}) collective-permute-start(f32[2,512,128]{2,1,0:T(8,128)} %get-tuple-element.103.after_ref), channel_id=1, source_target_pairs={{0,2},{1,3},{2,0},{3,1},{4,6},{5,7},{6,4},{7,5},{8,10},{9,11},{10,... | collective-permute-start | bytes 1572872 | tf_op jit(solution)/shard_map/ppermute | solution.py:312
  415.8 26.5 %collective-permute-start.49 = (f32[2,512,128]{2,1,0:T(8,128)}, f32[2,512,128]{2,1,0:T(8,128)}, u32[]{:S(2)}, u32[]{:S(2)}) collective-permute-start(f32[2,512,128]{2,1,0:T(8,128)} %get-tuple-element.100.after_ref.refs_1_), channel_id=1, source_target_pairs={{0,1},{1,0},{2,3},{3,2},{4,5},{5,4},{6,7},{7,6},{8,9},{9,8},{10,11... | collective-permute-start | bytes 1572872 | tf_op jit(solution)/shard_map/ppermute | solution.py:312
  417.2 26.7 %collective-permute-start.53 = (f32[2,512,128]{2,1,0:T(8,128)}, f32[2,512,128]{2,1,0:T(8,128)}, u32[]{:S(2)}, u32[]{:S(2)}) collective-permute-start(f32[2,512,128]{2,1,0:T(8,128)} %get-tuple-element.116.refs_0_), channel_id=1, source_target_pairs={{0,1},{1,0},{2,3},{3,2},{4,5},{5,4},{6,7},{7,6},{8,9},{9,8},{10,11... | collective-permute-start | bytes 1572872 | tf_op jit(solution)/shard_map/ppermute | solution.py:312
  442.3 48.3 %collective-permute-start.51 = (f32[2,512,128]{2,1,0:T(8,128)}, f32[2,512,128]{2,1,0:T(8,128)}, u32[]{:S(2)}, u32[]{:S(2)}) collective-permute-start(f32[2,512,128]{2,1,0:T(8,128)} %get-tuple-element.110.after_ref), channel_id=1, source_target_pairs={{0,4},{1,5},{2,6},{3,7},{4,0},{5,1},{6,2},{7,3},{8,12},{9,13},{10,... | collective-permute-start | bytes 1572872 | tf_op jit(solution)/shard_map/ppermute | solution.py:312
  442.3 48.3 %collective-permute-start.55 = (f32[2,512,128]{2,1,0:T(8,128)}, f32[2,512,128]{2,1,0:T(8,128)}, u32[]{:S(2)}, u32[]{:S(2)}) collective-permute-start(f32[2,512,128]{2,1,0:T(8,128)} %get-tuple-element.119.refs_0_), channel_id=1, source_target_pairs={{0,1},{1,0},{2,3},{3,2},{4,5},{5,4},{6,7},{7,6},{8,9},{9,8},{10,11... | collective-permute-start | bytes 1572872 | tf_op jit(solution)/shard_map/ppermute | solution.py:312
  443.9 48.0 %collective-permute-start.56 = (f32[2,512,128]{2,1,0:T(8,128)}, f32[2,512,128]{2,1,0:T(8,128)}, u32[]{:S(2)}, u32[]{:S(2)}) collective-permute-start(f32[2,512,128]{2,1,0:T(8,128)} %get-tuple-element.111.after_ref.refs_1_), channel_id=1, source_target_pairs={{0,1},{1,0},{2,3},{3,2},{4,5},{5,4},{6,7},{7,6},{8,9},{9,8},{10,11... | collective-permute-start | bytes 1572872 | tf_op jit(solution)/shard_map/ppermute | solution.py:312
  453.3 46.5 %collective-permute-start.50 = (f32[2,512,128]{2,1,0:T(8,128)}, f32[2,512,128]{2,1,0:T(8,128)S(1)}, u32[]{:S(2)}, u32[]{:S(2)}) collective-permute-start(f32[2,512,128]{2,1,0:T(8,128)} %get-tuple-element.114.after_ref), channel_id=1, source_target_pairs={{0,2},{1,3},{2,0},{3,1},{4,6},{5,7},{6,4},{7,5},{8,10},{9,11},{10,... | collective-permute-start | bytes 1572872 | tf_op jit(solution)/shard_map/ppermute | solution.py:312
  459.5 46.5 %collective-permute-start.61 = (f32[2,128,128]{2,1,0:T(8,128)}, f32[2,128,128]{2,1,0:T(8,128)S(1)}, u32[]{:S(2)}, u32[]{:S(2)}) collective-permute-start(f32[2,128,128]{2,1,0:T(8,128)} %get-tuple-element.126), channel_id=1, source_target_pairs={{0,4},{1,5},{2,6},{3,7},{4,0},{5,1},{6,2},{7,3},{8,12},{9,13},{10,... | collective-permute-start | bytes 393224 | tf_op jit(solution)/shard_map/ppermute | solution.py:312
  506.0 29.9 %collective-permute-start.62 = (f32[2,128,128]{2,1,0:T(8,128)S(1)}, f32[2,128,128]{2,1,0:T(8,128)S(1)}, u32[]{:S(2)}, u32[]{:S(2)}) collective-permute-start(f32[2,128,128]{2,1,0:T(8,128)S(1)} %copy-done.54), channel_id=1, source_target_pairs={{0,6},{1,7},{2,4},{3,5},{4,2},{5,3},{6,0},{7,1},{8,14},{9,15},{10,... | collective-permute-start | bytes 393224 | tf_op jit(solution)/shard_map/ppermute | solution.py:312
  508.8 27.1 %collective-permute-start.60 = (f32[2,128,128]{2,1,0:T(8,128)}, f32[2,128,128]{2,1,0:T(8,128)S(1)}, u32[]{:S(2)}, u32[]{:S(2)}) collective-permute-start(f32[2,128,128]{2,1,0:T(8,128)} %get-tuple-element.125), channel_id=1, source_target_pairs={{0,2},{1,3},{2,0},{3,1},{4,6},{5,7},{6,4},{7,5},{8,10},{9,11},{10,... | collective-permute-start | bytes 393224 | tf_op jit(solution)/shard_map/ppermute | solution.py:312
  (76 other events, 1271.3 us)

commit v3 on v2

--- a/solution.py
+++ b/solution.py
@@ -87,7 +87,7 @@
 
 def pack_stage(z, re, im, c, after):
     rows, _, lanes = re.shape
-    block, tile = 128, 8
+    block, tile = 256, 8
     spec = pl.BlockSpec((block, tile, lanes), lambda i: (i, c * SWAP // tile, 0))
     out = pl.BlockSpec((2, block, lanes), lambda i: (0, i, 0))
     return pl.pallas_call(
@@ -179,7 +179,7 @@
     )(z, coef, turn, after, mine, theirs)
 
 
-def row_kernel(c, slots, sizes, coef_ref, after_ref, tc_ref, ts_ref, rc_ref, rs_ref, table_ref, *refs):
+def row_kernel(slots, sizes, coef_ref, after_ref, tc_ref, ts_ref, rc_ref, rs_ref, table_ref, *refs):
     refs, (high_ref, low_ref) = refs[:-2], refs[-2:]
     inputs = len(slots) if len(slots) < SWAP else 1
     mine, theirs, outs = refs[:inputs], refs[inputs : 2 * inputs], refs[2 * inputs :]
@@ -202,7 +202,7 @@
                 yr = mixed[:TILE, :LANES] - mixed[TILE:, LANES:]
                 yi = mixed[TILE:, :LANES] + mixed[:TILE, LANES:]
                 here = pl.ds(pl.multiple_of((base + m) * TILE, TILE), TILE)
-                cosine, sine = rc_ref[here, c : c + 1], rs_ref[here, c : c + 1]
+                cosine, sine = rc_ref[here, :], rs_ref[here, :]
                 there = pl.ds(pl.multiple_of(m * TILE, TILE), TILE)
                 out_ref[0, there, :] = yr * cosine - yi * sine
                 out_ref[1, there, :] = yr * sine + yi * cosine
@@ -212,11 +212,11 @@
             base += size // TILE
 
 
-def row_stage(coef, turn, scale, table, mine, theirs, c, slots, sizes, after):
+def row_stage(coef, turn, scale, table, mine, theirs, slots, sizes, after):
     rows = mine[0].shape[-2]
     shapes = [jax.ShapeDtypeStruct((2, size, LANES), jnp.float32) for size in sizes for _ in slots]
     outs = pl.pallas_call(
-        functools.partial(row_kernel, c, slots, sizes),
+        functools.partial(row_kernel, slots, sizes),
         in_specs=[SCALAR, ANYWHERE] + [WHOLE] * (5 + 2 * len(mine)),
         out_specs=[WHOLE] * len(shapes),
         out_shape=shapes,
@@ -227,19 +227,16 @@
     return [outs[k * len(slots) : (k + 1) * len(slots)] for k in range(len(sizes))]
 
 
-def lane_kernel(block, z_ref, mc_ref, ms_ref, jc_ref, js_ref, table_ref, *refs):
+def lane_kernel(block, z_ref, jc_ref, js_ref, table_ref, *refs):
     count = jc_ref.shape[0]
     scratch = refs[-1]
     re_ref, im_ref, prob_ref = refs[-4:-1]
     for n in range(count):
         scratch[(n // SWAP) * SWAP + jnp.bitwise_xor(z_ref[0], n % SWAP)] = refs[n][...]
     reals, imags = fourier([scratch[n, 0] for n in range(count)], [scratch[n, 1] for n in range(count)])
-    mc, ms = mc_ref[...], ms_ref[...]
     highs, lows = [], []
     for j in range(count):
-        jc, js = jc_ref[j : j + 1, :], js_ref[j : j + 1, :]
-        c = mc * jc - ms * js
-        s = mc * js + ms * jc
+        c, s = jc_ref[j : j + 1, :], js_ref[j : j + 1, :]
         rh, rl = halves(reals[j] * c - imags[j] * s)
         ih, il = halves(reals[j] * s + imags[j] * c)
         highs.append(jnp.concatenate([rh, ih], axis=1))
@@ -254,16 +251,15 @@
     prob_ref[...] = re * re + im * im
 
 
-def lane_stage(z, sources, previous, start, part, rows, mid, inner, table):
+def lane_stage(z, sources, previous, start, part, rows, inner, table):
     count = inner[0].shape[0]
-    block = 32
+    block = 64
     first = start // block
-    mspec = pl.BlockSpec((block, LANES), lambda i: (first + i, 0))
     jspec = pl.BlockSpec((count, LANES), lambda i: (0, 0))
     out = pl.BlockSpec((block, count, LANES), lambda i: (first + i, 0, 0))
     shape = jax.ShapeDtypeStruct((rows, count, LANES), jnp.float32)
-    arguments = [z, *mid, *inner, table]
-    specs = [SCALAR, mspec, mspec, jspec, jspec, pl.BlockSpec((2, 2 * LANES, 2 * LANES), lambda i: (0, 0, 0))]
+    arguments = [z, *inner, table]
+    specs = [SCALAR, jspec, jspec, pl.BlockSpec((2, 2 * LANES, 2 * LANES), lambda i: (0, 0, 0))]
     for source, base in sources:
         offset = (start - base) // block
         arguments += source
@@ -329,16 +325,17 @@
     table = jnp.concatenate([cosine.reshape(tiles), sine.reshape(tiles)], axis=1)
     row_table = jnp.stack(table_halves(table), axis=1)
     offsets = jnp.arange(SLICES, dtype=jnp.int32) * SWAP + z
-    scale = phases(rev_a[:, None] * offsets[None, :], rows * inside)
     turns = [
         phases((a_index[:, None] * (inside * LANES) + offsets[c] * LANES) * k_slot[None, :], total)
         for c in range(SLICES)
     ]
 
     lane = np.arange(LANES, dtype=np.int32)
-    mid = phases((k_here + devices * rev_a)[:, None] * lane[None, :], total)
-    angle = (reversed_bits(inside)[:, None] * lane[None, :] % (inside * LANES)) * (2.0 * math.pi / (inside * LANES))
-    inner = (jnp.asarray(np.cos(angle), jnp.float32), jnp.asarray(np.sin(angle), jnp.float32))
+    scales = [
+        phases(rev_a[:, None] * (offsets[c] * LANES + lane[None, :]), rows * inside * LANES) for c in range(SLICES)
+    ]
+    k_inner = reversed_bits(inside)[:, None] * (devices * rows)
+    inner = phases((k_here + k_inner) * lane[None, :], total)
     angle = (lane[:, None] * rev_l[None, :] % LANES) * (2.0 * math.pi / LANES)
     c, s = np.cos(angle) / math.sqrt(total), np.sin(angle) / math.sqrt(total)
     lane_table = jnp.stack(table_halves(jnp.asarray(np.block([[c, s], [-s, c]]), jnp.float32)))
@@ -357,7 +354,7 @@
 
     packed, inward, across, mixed, spread = {}, {}, {}, {}, {}
     parts = {k: (rows,) for k in range(SLICES)}
-    parts[SLICES - 1] = (TILE,) * (rows // TILE)
+    parts[SLICES - 1] = (rows // 2, rows // 4, rows // 4)
     outward = {k: [[None] * SWAP for _ in sizes] for k, sizes in parts.items()}
 
     def pack(k, *after):
@@ -384,25 +381,20 @@
 
     def finish(k, n):
         mine, theirs = ([v[k][s] for s in GROUPS[n]] for v in (mixed, spread))
-        shared = (w_coef[0], turns[k], scale, row_table)
-        pieces = kernel(row_stage, *shared, mine, theirs, k, GROUPS[n], parts[k])
+        shared = (w_coef[0], turns[k], scales[k], row_table)
+        pieces = kernel(row_stage, *shared, mine, theirs, GROUPS[n], parts[k])
         for p, piece in enumerate(pieces):
             for s, value in zip(GROUPS[n], piece):
                 outward[k][p][s] = flip(value, s * weights) if s else value
 
-    pack(0), pack(1, row_table, *scale, *turns[0]), pack(2), pack(3)
-    cross(0), cross(1), mixing(0), swapping(0), mixing(1), cross(2)
-    for k in range(1, SLICES):
-        finish(k - 1, 0), swapping(k), finish(k - 1, 1)
-        if k + 1 < SLICES:
-            if k + 2 < SLICES:
-                cross(k + 2)
-            mixing(k + 1)
-    finish(SLICES - 1, 0), finish(SLICES - 1, 1)
+    pack(0), pack(1, row_table, *scales[0], *turns[0]), pack(2), pack(3)
+    cross(0), cross(1), mixing(0), swapping(0), mixing(1), swapping(1)
+    finish(0, 0), cross(2), finish(0, 1), cross(3), finish(1, 0), mixing(2), swapping(2), finish(1, 1)
+    mixing(3), finish(2, 0), swapping(3), finish(2, 1), finish(3, 0), finish(3, 1)
     outs, start, last = None, 0, SLICES - 1
     for n, part in enumerate(parts[last]):
         sources = [(outward[k][0], 0) for k in range(last)] + [(outward[last][n], start)]
-        outs = lane_stage(zs, sources, outs, start, part, rows, mid, inner, lane_table)
+        outs = lane_stage(zs, sources, outs, start, part, rows, inner, lane_table)
         start += part
     return tuple(values.reshape(local) for values in outs)
 

time: 551 us -> 539 us (0.978)
  starting transfers between devices: 146 us -> 121 us
  waiting for transfers between devices: 246 us -> 263 us
  Pallas kernels: 128 us -> 121 us
    ppermute x69 -> x66, starting transfers between devices: 146 us -> 121 us  [flip(): lax.ppermute(values, AXES, [(i, i ^ distance) for i in range(devices)])]
    ppermute x69 -> x66, waiting for transfers between devices: 246 us -> 263 us  [flip(): lax.ppermute(values, AXES, [(i, i ^ distance) for i in range(devices)])]
    pallas_call x4 -> x3, Pallas kernels: 22 us -> 16.9 us  [lane_stage(): pl.pallas_call(kernel, grid=(part // block,), in_specs=specs, out_specs=[...]
  transfers between devices with their start and end apart: 69 -> 66, of which waited for: 26 -> 24; matrix products, arithmetic and copies ran while one was open for 3% -> 4% of each run, Pallas kernels for 18% -> 18%
where the time goes in v3:
time: 539 us; the launch traced here: 538 us
  waiting for transfers between devices  263 us (49%)
  Pallas kernels  121 us (22%)
  starting transfers between devices  121 us (22%)
  other arithmetic  20.7 us (4%)
  local copies, waits for them, and re-layouts  7.67 us (1%)
    ppermute x66, waiting for transfers between devices, flip(): lax.ppermute(values, AXES, [(i, i ^ distance) for i in range(devices)])  263 us
    ppermute x66, starting transfers between devices, flip(): lax.ppermute(values, AXES, [(i, i ^ distance) for i in range(devices)])  121 us
    pallas_call x8, Pallas kernels, row_stage(): pl.pallas_call(functools.partial(row_kernel, slots, sizes), in_specs=[SCA...  53.7 us
    pallas_call x4, Pallas kernels, swap_stage(): pl.pallas_call(swap_kernel, grid=(rows // block,), in_specs=[SCALAR, SCAL...  18.8 us
    pallas_call x4, Pallas kernels, mix_stage(): pl.pallas_call(functools.partial(mix_kernel, len(mine)), grid=(rows // bl...  17.7 us
    pallas_call x3, Pallas kernels, lane_stage(): pl.pallas_call(kernel, grid=(part // block,), in_specs=specs, out_specs=[...  16.9 us
    pallas_call x4, Pallas kernels, pack_stage(): pl.pallas_call(functools.partial(pack_kernel, c * SWAP % tile), grid=(row...  13.8 us
    sin x4, other arithmetic, phases(): return (jnp.cos(angle), jnp.sin(angle))  12.1 us
  transfers between devices with their start and end apart: 66, of which 24 were waited for; matrix products, arithmetic and copies ran while one was open for 4% of the time, Pallas kernels for 18%

profile of v3, /device:TPU:0, one launch (start us, length us, event | category | flops | bytes accessed | tf_op | source)
XLA Modules:
  0.0 537.5 jit_solution(5970566264680160892)
XLA Ops:
  13.4 4.2 cosine_bitcast_fusion
  20.9 5.7 %fusion.39 = (f32[512,128]{1,0:T(8,128)}, f32[512,128]{1,0:T(8,128)}, f32[512,128]{1,0:T(8,128)}, f32[512,128]{1,0:T(8,128)}, f32[512,128]{1,0:T(8,128)}, /*inde...) fusion(s32[128]{0:T(128)S(1)} %get-tuple-element.163, s32[512]{0:T(512)S(1)} %copy-done.45, ...), kind=kLoop, calls=%fused_computation.88 | loop fusion | flops 3670016 | bytes 2101248 | tf_op jit(solution)/shard_map/sin | solution.py:36
  31.5 14.1 %collective-permute-done.1.refs_2_ = f32[2,512,128]{2,1,0:T(8,128)S(1)} collective-permute-done((f32[2,512,128]{2,1,0:T(8,128)}, f32[2,512,128]{2,1,0:T(8,128)S(1)}, u32[]{:S(2)}, u32[]{:S(2)}) %collective-permute-start.1) | collective-permute-done | bytes 524320 | tf_op jit(solution)/shard_map/ppermute | solution.py:308
  47.6 5.6 %fusion.31 = (f32[512,4]{1,0:T(8,128)}, f32[512,4]{1,0:T(8,128)}, f32[512,4]{1,0:T(8,128)}, f32[512,4]{1,0:T(8,128)}, f32[512,4]{1,0:T(8,128)}, /*index=5*/f32[512,4]{1,0:T(8,128)}, f32[512,4]{1,0:T(8,128)}, f32[512,4]{1,0:T(8,128)}) fusion(s32[4]{0:T(128)S(1)} %get-tuple-element.179, s32[512]{0:T(512)S(1)} %fusion.55, s32[512]{0:T(512)S(1)} %fusion.58, ...), kind=kLoop, calls=%fused_computation.80 | loop fusion | flops 114688 | bytes 73744 | tf_op jit(solution)/shard_map/sin | solution.py:36
  65.5 4.4 mix_stage.4.after_ref.mine_ref
  69.9 9.8 %collective-permute-start.8 = (f32[2,512,128]{2,1,0:T(8,128)}, f32[2,512,128]{2,1,0:T(8,128)S(1)}, u32[]{:S(2)}, u32[]{:S(2)}) collective-permute-start(f32[2,512,128]{2,1,0:T(8,128)} %get-tuple-element.76), channel_id=1, source_target_pairs={{0,2},{1,3},{2,0},{3,1},{4,6},{5,7},{6,4},{7,5},{8,10},{9,11},{10,... | collective-permute-start | bytes 1572872 | tf_op jit(solution)/shard_map/ppermute | solution.py:308
  82.7 20.5 %collective-permute-done.8.refs_1_ = f32[2,512,128]{2,1,0:T(8,128)S(1)} collective-permute-done((f32[2,512,128]{2,1,0:T(8,128)}, f32[2,512,128]{2,1,0:T(8,128)S(1)}, u32[]{:S(2)}, u32[]{:S(2)}) %collective-permute-start.8) | collective-permute-done | bytes 524320 | tf_op jit(solution)/shard_map/ppermute | solution.py:308
  103.8 14.5 %collective-permute-done.9.refs_2_ = f32[2,512,128]{2,1,0:T(8,128)} collective-permute-done((f32[2,512,128]{2,1,0:T(8,128)}, f32[2,512,128]{2,1,0:T(8,128)}, u32[]{:S(2)}, u32[]{:S(2)}) %collective-permute-start.9) | collective-permute-done | bytes 524320 | tf_op jit(solution)/shard_map/ppermute | solution.py:308
  122.9 4.7 swap_stage.4
  127.6 5.7 %collective-permute-done.13.refs_6_ = f32[2,512,128]{2,1,0:T(8,128)} collective-permute-done((f32[2,512,128]{2,1,0:T(8,128)}, f32[2,512,128]{2,1,0:T(8,128)}, u32[]{:S(2)}, u32[]{:S(2)}) %collective-permute-start.13) | collective-permute-done | bytes 524320 | tf_op jit(solution)/shard_map/ppermute | solution.py:308
  133.4 6.2 %collective-permute-done.14.refs_7_ = f32[2,512,128]{2,1,0:T(8,128)} collective-permute-done((f32[2,512,128]{2,1,0:T(8,128)}, f32[2,512,128]{2,1,0:T(8,128)}, u32[]{:S(2)}, u32[]{:S(2)}) %collective-permute-start.14) | collective-permute-done | bytes 524320 | tf_op jit(solution)/shard_map/ppermute | solution.py:308
  139.6 4.4 mix_stage.5.after_ref.mine_ref
  152.4 4.7 swap_stage.5
  157.1 13.6 %collective-permute-done.25.refs_1_ = f32[2,512,128]{2,1,0:T(8,128)} collective-permute-done((f32[2,512,128]{2,1,0:T(8,128)}, f32[2,512,128]{2,1,0:T(8,128)}, u32[]{:S(2)}, u32[]{:S(2)}) %collective-permute-start.25) | collective-permute-done | bytes 524320 | tf_op jit(solution)/shard_map/ppermute | solution.py:308
  172.2 13.4 %collective-permute-done.26.refs_2_ = f32[2,512,128]{2,1,0:T(8,128)} collective-permute-done((f32[2,512,128]{2,1,0:T(8,128)}, f32[2,512,128]{2,1,0:T(8,128)}, u32[]{:S(2)}, u32[]{:S(2)}) %collective-permute-start.26) | collective-permute-done | bytes 524320 | tf_op jit(solution)/shard_map/ppermute | solution.py:308
  191.2 9.2 %collective-permute-done.19.refs_3_ = f32[2,512,128]{2,1,0:T(8,128)S(1)} collective-permute-done((f32[2,512,128]{2,1,0:T(8,128)S(1)}, f32[2,512,128]{2,1,0:T(8,128)S(1)}, u32[]{:S(2)}, u32[]{:S(2)}) %collective-permute-start.19) | collective-permute-done | bytes 524320 | tf_op jit(solution)/shard_map/ppermute | solution.py:308
  201.0 10.7 %collective-permute-done.23.refs_2_ = f32[2,512,128]{2,1,0:T(8,128)S(1)} collective-permute-done((f32[2,512,128]{2,1,0:T(8,128)}, f32[2,512,128]{2,1,0:T(8,128)S(1)}, u32[]{:S(2)}, u32[]{:S(2)}) %collective-permute-start.23) | collective-permute-done | bytes 524320 | tf_op jit(solution)/shard_map/ppermute | solution.py:308
  212.9 7.0 %row_stage.8 = (f32[2,512,128]{2,1,0:T(8,128)}, f32[2,512,128]{2,1,0:T(8,128)}) custom-call(f32[9]{0:T(128)} %pad_maximum_fusion.2.coef_ref, f32[2,512,128]{2,1,0:T(8,128)} %get-tuple-element.79.after_ref.refs_1_, f32[512,4]{1,0:T(8,128)} %get-tuple-element.167.refs_4_.tc_ref, f32[512,4]{1,0:T(8,128)} %get-tuple-element.168.refs_5_.ts_ref, ...), custom_call_target="tpu_custom_call" | custom-call | flops 209715200 | bytes 8388608 | tf_op jit(solution)/shard_map/row_stage/pallas_call | solution.py:218
  219.9 6.8 %row_stage.9 = (f32[2,512,128]{2,1,0:T(8,128)}, f32[2,512,128]{2,1,0:T(8,128)}) custom-call(f32[9]{0:T(128)} %pad_maximum_fusion.2.coef_ref, f32[2,512,128]{2,1,0:T(8,128)} %get-tuple-element.82.after_ref, f32[512,4]{1,0:T(8,128)} %get-tuple-element.167.refs_4_.tc_ref, f32[512,4]{1,0:T(8,128)} %get-tuple-element.168.refs_5_.ts_ref, ...), custom_call_target="tpu_custom_call" | custom-call | flops 209715200 | bytes 8388608 | tf_op jit(solution)/shard_map/row_stage/pallas_call | solution.py:218
  227.5 6.8 %row_stage.10 = (f32[2,512,128]{2,1,0:T(8,128)}, f32[2,512,128]{2,1,0:T(8,128)}) custom-call(f32[9]{0:T(128)} %pad_maximum_fusion.2.coef_ref, f32[2,512,128]{2,1,0:T(8,128)} %get-tuple-element.85.after_ref, f32[512,4]{1,0:T(8,128)} %get-tuple-element.169.tc_ref, f32[512,4]{1,0:T(8,128)} %get-tuple-element.170.ts_ref, f32[512,128]{1,0:T(8,128)} %get-tuple-element.157.rc_ref, ...), custom_call_target="tpu_custom_call" | custom-call | flops 209715200 | bytes 8388608 | tf_op jit(solution)/shard_map/row_stage/pallas_call | solution.py:218
  235.1 4.4 mix_stage.6.after_ref.mine_ref
  239.6 10.0 %collective-permute-start.38 = (f32[2,512,128]{2,1,0:T(8,128)}, f32[2,512,128]{2,1,0:T(8,128)}, u32[]{:S(2)}, u32[]{:S(2)}) collective-permute-start(f32[2,512,128]{2,1,0:T(8,128)} %get-tuple-element.98), channel_id=1, source_target_pairs={{0,2},{1,3},{2,0},{3,1},{4,6},{5,7},{6,4},{7,5},{8,10},{9,11},{10,... | collective-permute-start | bytes 1572872 | tf_op jit(solution)/shard_map/ppermute | solution.py:308
  253.6 19.6 %collective-permute-done.38.refs_1_ = f32[2,512,128]{2,1,0:T(8,128)} collective-permute-done((f32[2,512,128]{2,1,0:T(8,128)}, f32[2,512,128]{2,1,0:T(8,128)}, u32[]{:S(2)}, u32[]{:S(2)}) %collective-permute-start.38) | collective-permute-done | bytes 524320 | tf_op jit(solution)/shard_map/ppermute | solution.py:308
  274.7 13.4 %collective-permute-done.39.refs_2_ = f32[2,512,128]{2,1,0:T(8,128)} collective-permute-done((f32[2,512,128]{2,1,0:T(8,128)}, f32[2,512,128]{2,1,0:T(8,128)}, u32[]{:S(2)}, u32[]{:S(2)}) %collective-permute-start.39) | collective-permute-done | bytes 524320 | tf_op jit(solution)/shard_map/ppermute | solution.py:308
  292.3 4.7 swap_stage.6
  297.0 6.8 %row_stage.11 = (f32[2,512,128]{2,1,0:T(8,128)}, f32[2,512,128]{2,1,0:T(8,128)}) custom-call(f32[9]{0:T(128)} %pad_maximum_fusion.2.coef_ref, f32[2,512,128]{2,1,0:T(8,128)} %get-tuple-element.93.after_ref.refs_1_, f32[512,4]{1,0:T(8,128)} %get-tuple-element.169.tc_ref, f32[512,4]{1,0:T(8,128)} %get-tuple-element.170.ts_ref, ...), custom_call_target="tpu_custom_call" | custom-call | flops 209715200 | bytes 8388608 | tf_op jit(solution)/shard_map/row_stage/pallas_call | solution.py:218
  303.8 10.4 %collective-permute-done.42.refs_5_ = f32[2,512,128]{2,1,0:T(8,128)} collective-permute-done((f32[2,512,128]{2,1,0:T(8,128)}, f32[2,512,128]{2,1,0:T(8,128)}, u32[]{:S(2)}, u32[]{:S(2)}) %collective-permute-start.42) | collective-permute-done | bytes 524320 | tf_op jit(solution)/shard_map/ppermute | solution.py:308
  314.2 9.1 %collective-permute-done.43.refs_6_ = f32[2,512,128]{2,1,0:T(8,128)} collective-permute-done((f32[2,512,128]{2,1,0:T(8,128)}, f32[2,512,128]{2,1,0:T(8,128)}, u32[]{:S(2)}, u32[]{:S(2)}) %collective-permute-start.43) | collective-permute-done | bytes 524320 | tf_op jit(solution)/shard_map/ppermute | solution.py:308
  323.3 5.6 %collective-permute-done.44.refs_7_ = f32[2,512,128]{2,1,0:T(8,128)} collective-permute-done((f32[2,512,128]{2,1,0:T(8,128)}, f32[2,512,128]{2,1,0:T(8,128)}, u32[]{:S(2)}, u32[]{:S(2)}) %collective-permute-start.44) | collective-permute-done | bytes 524320 | tf_op jit(solution)/shard_map/ppermute | solution.py:308
  328.9 4.5 mix_stage.7.after_ref.mine_ref
  335.5 6.1 %collective-permute-start.20 = (f32[2,512,128]{2,1,0:T(8,128)}, f32[2,512,128]{2,1,0:T(8,128)S(1)}, u32[]{:S(2)}, u32[]{:S(2)}) collective-permute-start(f32[2,512,128]{2,1,0:T(8,128)} %get-tuple-element.85.after_ref), channel_id=1, source_target_pairs={{0,2},{1,3},{2,0},{3,1},{4,6},{5,7},{6,4},{7,5},{8,10},{9,11},{10,... | collective-permute-start | bytes 1572872 | tf_op jit(solution)/shard_map/ppermute | solution.py:308
  344.0 4.3 collective-permute-done.45.refs_2_
  348.4 7.1 %collective-permute-start.21 = (f32[2,512,128]{2,1,0:T(8,128)S(1)}, f32[2,512,128]{2,1,0:T(8,128)S(1)}, u32[]{:S(2)}, u32[]{:S(2)}) collective-permute-start(f32[2,512,128]{2,1,0:T(8,128)S(1)} %copy-done.16), channel_id=1, source_target_pairs={{0,4},{1,5},{2,6},{3,7},{4,0},{5,1},{6,2},{7,3},{8,12},{9,13},{10,... | collective-permute-start | bytes 1572872 | tf_op jit(solution)/shard_map/ppermute | solution.py:308
  359.8 7.8 %collective-permute-start.37 = (f32[2,512,128]{2,1,0:T(8,128)}, f32[2,512,128]{2,1,0:T(8,128)S(1)}, u32[]{:S(2)}, u32[]{:S(2)}) collective-permute-start(f32[2,512,128]{2,1,0:T(8,128)} %get-tuple-element.97), channel_id=1, source_target_pairs={{0,6},{1,7},{2,4},{3,5},{4,2},{5,3},{6,0},{7,1},{8,14},{9,15},{10,... | collective-permute-start | bytes 1572872 | tf_op jit(solution)/shard_map/ppermute | solution.py:308
  369.1 6.9 %row_stage.12 = (f32[2,512,128]{2,1,0:T(8,128)}, f32[2,512,128]{2,1,0:T(8,128)}) custom-call(f32[9]{0:T(128)} %pad_maximum_fusion.2.coef_ref, f32[4,2,512,128]{3,2,1,0:T(8,128)} %mix_stage.7.after_ref.mine_ref, f32[512,4]{1,0:T(8,128)} %get-tuple-element.171.tc_ref, f32[512,4]{1,0:T(8,128)} %get-tuple-element.172.ts_ref, ...), custom_call_target="tpu_custom_call" | custom-call | flops 209715200 | bytes 8388608 | tf_op jit(solution)/shard_map/row_stage/pallas_call | solution.py:218
  375.9 4.8 swap_stage.7
  382.8 18.5 %collective-permute-done.21.refs_2_ = f32[2,512,128]{2,1,0:T(8,128)S(1)} collective-permute-done((f32[2,512,128]{2,1,0:T(8,128)S(1)}, f32[2,512,128]{2,1,0:T(8,128)S(1)}, u32[]{:S(2)}, u32[]{:S(2)}) %collective-permute-start.21) | collective-permute-done | bytes 524320 | tf_op jit(solution)/shard_map/ppermute | solution.py:308
  404.9 10.8 %collective-permute-start.36 = (f32[2,512,128]{2,1,0:T(8,128)}, f32[2,512,128]{2,1,0:T(8,128)S(1)}, u32[]{:S(2)}, u32[]{:S(2)}) collective-permute-start(f32[2,512,128]{2,1,0:T(8,128)} %get-tuple-element.89.after_ref), channel_id=1, source_target_pairs={{0,4},{1,5},{2,6},{3,7},{4,0},{5,1},{6,2},{7,3},{8,12},{9,13},{10,... | collective-permute-start | bytes 1572872 | tf_op jit(solution)/shard_map/ppermute | solution.py:308
  419.4 9.9 %collective-permute-done.55.refs_2_ = f32[2,512,128]{2,1,0:T(8,128)} collective-permute-done((f32[2,512,128]{2,1,0:T(8,128)}, f32[2,512,128]{2,1,0:T(8,128)}, u32[]{:S(2)}, u32[]{:S(2)}) %collective-permute-start.55) | collective-permute-done | bytes 524320 | tf_op jit(solution)/shard_map/ppermute | solution.py:308
  429.3 6.8 %row_stage.13 = (f32[2,512,128]{2,1,0:T(8,128)}, f32[2,512,128]{2,1,0:T(8,128)}) custom-call(f32[9]{0:T(128)} %pad_maximum_fusion.2.coef_ref, f32[2,512,128]{2,1,0:T(8,128)} %get-tuple-element.104.after_ref.refs_1_, f32[512,4]{1,0:T(8,128)} %get-tuple-element.171.tc_ref, f32[512,4]{1,0:T(8,128)} %get-tuple-element.172.ts_ref, ...), custom_call_target="tpu_custom_call" | custom-call | flops 209715200 | bytes 8388608 | tf_op jit(solution)/shard_map/row_stage/pallas_call | solution.py:218
  438.7 6.2 %row_stage.14 = (f32[2,256,128]{2,1,0:T(8,128)}, f32[2,256,128]{2,1,0:T(8,128)}, f32[2,128,128]{2,1,0:T(8,128)}, f32[2,128,128]{2,1,0:T(8,128)}, f32[2,128,128]{2,1,0:T(8,128)}, /*index=5*/f32[2,128,128]{2,1,0:T(8,128)}) custom-call(f32[9]{0:T(128)} %pad_maximum_fusion.2.coef_ref, f32[2,512,128]{2,1,0:T(8,128)} %get-tuple-element.107.after_ref, ...), custom_call_target="tpu_custom_call" | custom-call | flops 209715200 | bytes 8388608 | tf_op jit(solution)/shard_map/row_stage/pallas_call | solution.py:218
  444.9 6.5 %row_stage.15 = (f32[2,256,128]{2,1,0:T(8,128)}, f32[2,256,128]{2,1,0:T(8,128)}, f32[2,128,128]{2,1,0:T(8,128)}, f32[2,128,128]{2,1,0:T(8,128)}, f32[2,128,128]{2,1,0:T(8,128)}, /*index=5*/f32[2,128,128]{2,1,0:T(8,128)}) custom-call(f32[9]{0:T(128)} %pad_maximum_fusion.2.coef_ref, f32[2,256,128]{2,1,0:T(8,128)} %get-tuple-element.111.after_ref, ...), custom_call_target="tpu_custom_call" | custom-call | flops 209715200 | bytes 8388608 | tf_op jit(solution)/shard_map/row_stage/pallas_call | solution.py:218
  456.3 42.0 %collective-permute-done.51.refs_10_ = f32[2,512,128]{2,1,0:T(8,128)} collective-permute-done((f32[2,512,128]{2,1,0:T(8,128)}, f32[2,512,128]{2,1,0:T(8,128)}, u32[]{:S(2)}, u32[]{:S(2)}) %collective-permute-start.51) | collective-permute-done | bytes 524320 | tf_op jit(solution)/shard_map/ppermute | solution.py:308
  500.3 9.2 %collective-permute-done.61.refs_14_ = f32[2,128,128]{2,1,0:T(8,128)S(1)} collective-permute-done((f32[2,128,128]{2,1,0:T(8,128)S(1)}, f32[2,128,128]{2,1,0:T(8,128)S(1)}, u32[]{:S(2)}, u32[]{:S(2)}) %collective-permute-start.61) | collective-permute-done | bytes 131104 | tf_op jit(solution)/shard_map/ppermute | solution.py:308
  510.3 5.6 %collective-permute-start.58 = (f32[2,128,128]{2,1,0:T(8,128)}, f32[2,128,128]{2,1,0:T(8,128)S(1)}, u32[]{:S(2)}, u32[]{:S(2)}) collective-permute-start(f32[2,128,128]{2,1,0:T(8,128)} %get-tuple-element.115), channel_id=1, source_target_pairs={{0,4},{1,5},{2,6},{3,7},{4,0},{5,1},{6,2},{7,3},{8,12},{9,13},{10,... | collective-permute-start | bytes 393224 | tf_op jit(solution)/shard_map/ppermute | solution.py:308
  518.9 7.6 %lane_stage.3 = (f32[512,16,128]{2,1,0:T(8,128)}, f32[512,16,128]{2,1,0:T(8,128)}, f32[512,16,128]{2,1,0:T(8,128)}) custom-call(s32[1]{0:T(128)} %bitcast.z_ref.refs_0_, f32[16,128]{1,0:T(8,128)} %get-tuple-element.178.jc_ref, f32[16,128]{1,0:T(8,128)} %get-tuple-element.177.js_ref, bf16[2,256,256]{2,1,0:T(8,128)(2,1)} %constant.226.table_ref, ...), custom_call_target="tpu_custom_call" | custom-call | flops 1342177280 | bytes 10485760 | tf_op jit(solution)/shard_map/lane_stage/pallas_call | solution.py:273
  527.2 4.7 lane_stage.4
  532.7 4.7 lane_stage.5
  (235 shorter events, 103.7 us)
Async XLA Ops:
  4.1 25.7 %collective-permute-start = (f32[2,512,128]{2,1,0:T(8,128)}, f32[2,512,128]{2,1,0:T(8,128)S(1)}, u32[]{:S(2)}, u32[]{:S(2)}) collective-permute-start(f32[2,512,128]{2,1,0:T(8,128)} %get-tuple-element.72), channel_id=1, source_target_pairs={{0,2},{1,3},{2,0},{3,1},{4,6},{5,7},{6,4},{7,5},{8,10},{9,11},{10,... | collective-permute-start | bytes 1572872 | tf_op jit(solution)/shard_map/ppermute | solution.py:308
  7.2 38.4 %collective-permute-start.1 = (f32[2,512,128]{2,1,0:T(8,128)}, f32[2,512,128]{2,1,0:T(8,128)S(1)}, u32[]{:S(2)}, u32[]{:S(2)}) collective-permute-start(f32[2,512,128]{2,1,0:T(8,128)} %get-tuple-element.73), channel_id=1, source_target_pairs={{0,4},{1,5},{2,6},{3,7},{4,0},{5,1},{6,2},{7,3},{8,12},{9,13},{10,... | collective-permute-start | bytes 1572872 | tf_op jit(solution)/shard_map/ppermute | solution.py:308
  9.8 37.3 %collective-permute-start.2 = (f32[2,512,128]{2,1,0:T(8,128)}, f32[2,512,128]{2,1,0:T(8,128)S(1)}, u32[]{:S(2)}, u32[]{:S(2)}) collective-permute-start(f32[2,512,128]{2,1,0:T(8,128)} %get-tuple-element.74), channel_id=1, source_target_pairs={{0,6},{1,7},{2,4},{3,5},{4,2},{5,3},{6,0},{7,1},{8,14},{9,15},{10,... | collective-permute-start | bytes 1572872 | tf_op jit(solution)/shard_map/ppermute | solution.py:308
  9.8 54.4 %collective-permute-start.3 = (f32[2,512,128]{2,1,0:T(8,128)}, f32[2,512,128]{2,1,0:T(8,128)S(1)}, u32[]{:S(2)}, u32[]{:S(2)}) collective-permute-start(f32[2,512,128]{2,1,0:T(8,128)} %get-tuple-element.68.refs_0_), channel_id=1, source_target_pairs={{0,16},{1,17},{2,18},{3,19},{4,20},{5,21},{6,22},{7,23},{8,24},{9,... | collective-permute-start | bytes 1572872 | tf_op jit(solution)/shard_map/ppermute | solution.py:308
  29.8 34.4 %collective-permute-start.4 = (f32[2,512,128]{2,1,0:T(8,128)S(1)}, f32[2,512,128]{2,1,0:T(8,128)S(1)}, u32[]{:S(2)}, u32[]{:S(2)}) collective-permute-start(f32[2,512,128]{2,1,0:T(8,128)S(1)} %collective-permute-done.refs_1_), channel_id=1, source_target_pairs={{0,16},{1,17},{2,18},{3,19},{4,20},{5,21},{6,22},{7,23},{8,24},{9,... | collective-permute-start | bytes 1572872 | tf_op jit(solution)/shard_map/ppermute | solution.py:308
  69.9 51.7 %collective-permute-start.7 = (f32[4,2,512,128]{3,2,1,0:T(8,128)}, f32[4,2,512,128]{3,2,1,0:T(8,128)S(1)}, u32[]{:S(2)}, u32[]{:S(2)}) collective-permute-start(f32[4,2,512,128]{3,2,1,0:T(8,128)} %mix_stage.4.after_ref.mine_ref), channel_id=1, source_target_pairs={{0,8},{1,9},{2,10},{3,11},{4,12},{5,13},{6,14},{7,15},{8,0},{9,1},... | collective-permute-start | bytes 6291464 | tf_op jit(solution)/shard_map/ppermute | solution.py:308
  69.9 33.3 %collective-permute-start.8 = (f32[2,512,128]{2,1,0:T(8,128)}, f32[2,512,128]{2,1,0:T(8,128)S(1)}, u32[]{:S(2)}, u32[]{:S(2)}) collective-permute-start(f32[2,512,128]{2,1,0:T(8,128)} %get-tuple-element.76), channel_id=1, source_target_pairs={{0,2},{1,3},{2,0},{3,1},{4,6},{5,7},{6,4},{7,5},{8,10},{9,11},{10,... | collective-permute-start | bytes 1572872 | tf_op jit(solution)/shard_map/ppermute | solution.py:308
  79.7 38.5 %collective-permute-start.9 = (f32[2,512,128]{2,1,0:T(8,128)}, f32[2,512,128]{2,1,0:T(8,128)}, u32[]{:S(2)}, u32[]{:S(2)}) collective-permute-start(f32[2,512,128]{2,1,0:T(8,128)} %get-tuple-element.77), channel_id=1, source_target_pairs={{0,4},{1,5},{2,6},{3,7},{4,0},{5,1},{6,2},{7,3},{8,12},{9,13},{10,... | collective-permute-start | bytes 1572872 | tf_op jit(solution)/shard_map/ppermute | solution.py:308
  80.8 38.0 %collective-permute-start.10 = (f32[2,512,128]{2,1,0:T(8,128)}, f32[2,512,128]{2,1,0:T(8,128)}, u32[]{:S(2)}, u32[]{:S(2)}) collective-permute-start(f32[2,512,128]{2,1,0:T(8,128)} %get-tuple-element.78), channel_id=1, source_target_pairs={{0,6},{1,7},{2,4},{3,5},{4,2},{5,3},{6,0},{7,1},{8,14},{9,15},{10,... | collective-permute-start | bytes 1572872 | tf_op jit(solution)/shard_map/ppermute | solution.py:308
  82.2 45.4 %collective-permute-start.11 = (f32[2,512,128]{2,1,0:T(8,128)S(1)}, f32[2,512,128]{2,1,0:T(8,128)}, u32[]{:S(2)}, u32[]{:S(2)}) collective-permute-start(f32[2,512,128]{2,1,0:T(8,128)S(1)} %copy-done.14), channel_id=1, source_target_pairs={{0,16},{1,17},{2,18},{3,19},{4,20},{5,21},{6,22},{7,23},{8,24},{9,... | collective-permute-start | bytes 1572872 | tf_op jit(solution)/shard_map/ppermute | solution.py:308
  103.2 24.4 %collective-permute-start.12 = (f32[2,512,128]{2,1,0:T(8,128)S(1)}, f32[2,512,128]{2,1,0:T(8,128)}, u32[]{:S(2)}, u32[]{:S(2)}) collective-permute-start(f32[2,512,128]{2,1,0:T(8,128)S(1)} %collective-permute-done.8.refs_1_), channel_id=1, source_target_pairs={{0,16},{1,17},{2,18},{3,19},{4,20},{5,21},{6,22},{7,23},{8,24},{9,... | collective-permute-start | bytes 1572872 | tf_op jit(solution)/shard_map/ppermute | solution.py:308
  144.0 26.8 %collective-permute-start.25 = (f32[2,512,128]{2,1,0:T(8,128)}, f32[2,512,128]{2,1,0:T(8,128)}, u32[]{:S(2)}, u32[]{:S(2)}) collective-permute-start(f32[2,512,128]{2,1,0:T(8,128)} %get-tuple-element.90), channel_id=1, source_target_pairs={{0,2},{1,3},{2,0},{3,1},{4,6},{5,7},{6,4},{7,5},{8,10},{9,11},{10,... | collective-permute-start | bytes 1572872 | tf_op jit(solution)/shard_map/ppermute | solution.py:308
  147.1 38.5 %collective-permute-start.26 = (f32[2,512,128]{2,1,0:T(8,128)}, f32[2,512,128]{2,1,0:T(8,128)}, u32[]{:S(2)}, u32[]{:S(2)}) collective-permute-start(f32[2,512,128]{2,1,0:T(8,128)} %get-tuple-element.91), channel_id=1, source_target_pairs={{0,4},{1,5},{2,6},{3,7},{4,0},{5,1},{6,2},{7,3},{8,12},{9,13},{10,... | collective-permute-start | bytes 1572872 | tf_op jit(solution)/shard_map/ppermute | solution.py:308
  149.6 37.6 %collective-permute-start.27 = (f32[2,512,128]{2,1,0:T(8,128)}, f32[2,512,128]{2,1,0:T(8,128)}, u32[]{:S(2)}, u32[]{:S(2)}) collective-permute-start(f32[2,512,128]{2,1,0:T(8,128)} %get-tuple-element.92), channel_id=1, source_target_pairs={{0,6},{1,7},{2,4},{3,5},{4,2},{5,3},{6,0},{7,1},{8,14},{9,15},{10,... | collective-permute-start | bytes 1572872 | tf_op jit(solution)/shard_map/ppermute | solution.py:308
  149.6 38.1 %collective-permute-start.16 = (f32[2,512,128]{2,1,0:T(8,128)}, f32[2,512,128]{2,1,0:T(8,128)}, u32[]{:S(2)}, u32[]{:S(2)}) collective-permute-start(f32[2,512,128]{2,1,0:T(8,128)} %get-tuple-element.80.refs_0_), channel_id=1, source_target_pairs={{0,1},{1,0},{2,3},{3,2},{4,5},{5,4},{6,7},{7,6},{8,9},{9,8},{10,11... | collective-permute-start | bytes 1572872 | tf_op jit(solution)/shard_map/ppermute | solution.py:308
  151.1 38.1 %collective-permute-start.17 = (f32[2,512,128]{2,1,0:T(8,128)}, f32[2,512,128]{2,1,0:T(8,128)}, u32[]{:S(2)}, u32[]{:S(2)}) collective-permute-start(f32[2,512,128]{2,1,0:T(8,128)} %get-tuple-element.81.refs_1_), channel_id=1, source_target_pairs={{0,1},{1,0},{2,3},{3,2},{4,5},{5,4},{6,7},{7,6},{8,9},{9,8},{10,11... | collective-permute-start | bytes 1572872 | tf_op jit(solution)/shard_map/ppermute | solution.py:308
  187.2 24.5 %collective-permute-start.23 = (f32[2,512,128]{2,1,0:T(8,128)}, f32[2,512,128]{2,1,0:T(8,128)S(1)}, u32[]{:S(2)}, u32[]{:S(2)}) collective-permute-start(f32[2,512,128]{2,1,0:T(8,128)} %get-tuple-element.87.refs_0_), channel_id=1, source_target_pairs={{0,1},{1,0},{2,3},{3,2},{4,5},{5,4},{6,7},{7,6},{8,9},{9,8},{10,11... | collective-permute-start | bytes 1572872 | tf_op jit(solution)/shard_map/ppermute | solution.py:308
  187.7 39.0 %collective-permute-start.24 = (f32[2,512,128]{2,1,0:T(8,128)}, f32[2,512,128]{2,1,0:T(8,128)S(1)}, u32[]{:S(2)}, u32[]{:S(2)}) collective-permute-start(f32[2,512,128]{2,1,0:T(8,128)} %get-tuple-element.88.refs_1_), channel_id=1, source_target_pairs={{0,1},{1,0},{2,3},{3,2},{4,5},{5,4},{6,7},{7,6},{8,9},{9,8},{10,11... | collective-permute-start | bytes 1572872 | tf_op jit(solution)/shard_map/ppermute | solution.py:308
  189.2 45.1 %collective-permute-start.28 = (f32[2,512,128]{2,1,0:T(8,128)S(1)}, f32[2,512,128]{2,1,0:T(8,128)}, u32[]{:S(2)}, u32[]{:S(2)}) collective-permute-start(f32[2,512,128]{2,1,0:T(8,128)S(1)} %copy-done.12), channel_id=1, source_target_pairs={{0,16},{1,17},{2,18},{3,19},{4,20},{5,21},{6,22},{7,23},{8,24},{9,... | collective-permute-start | bytes 1572872 | tf_op jit(solution)/shard_map/ppermute | solution.py:308
  189.7 44.6 %collective-permute-start.29 = (f32[2,512,128]{2,1,0:T(8,128)}, f32[2,512,128]{2,1,0:T(8,128)}, u32[]{:S(2)}, u32[]{:S(2)}) collective-permute-start(f32[2,512,128]{2,1,0:T(8,128)} %collective-permute-done.25.refs_1_), channel_id=1, source_target_pairs={{0,16},{1,17},{2,18},{3,19},{4,20},{5,21},{6,22},{7,23},{8,24},{9,... | collective-permute-start | bytes 1572872 | tf_op jit(solution)/shard_map/ppermute | solution.py:308
  200.4 33.9 %collective-permute-start.30 = (f32[2,512,128]{2,1,0:T(8,128)}, f32[2,512,128]{2,1,0:T(8,128)S(1)}, u32[]{:S(2)}, u32[]{:S(2)}) collective-permute-start(f32[2,512,128]{2,1,0:T(8,128)} %collective-permute-done.26.refs_2_), channel_id=1, source_target_pairs={{0,16},{1,17},{2,18},{3,19},{4,20},{5,21},{6,22},{7,23},{8,24},{9,... | collective-permute-start | bytes 1572872 | tf_op jit(solution)/shard_map/ppermute | solution.py:308
  239.6 51.1 %collective-permute-start.32 = (f32[4,2,512,128]{3,2,1,0:T(8,128)}, f32[4,2,512,128]{3,2,1,0:T(8,128)S(1)}, u32[]{:S(2)}, u32[]{:S(2)}) collective-permute-start(f32[4,2,512,128]{3,2,1,0:T(8,128)} %mix_stage.6.after_ref.mine_ref), channel_id=1, source_target_pairs={{0,8},{1,9},{2,10},{3,11},{4,12},{5,13},{6,14},{7,15},{8,0},{9,1},... | collective-permute-start | bytes 6291464 | tf_op jit(solution)/shard_map/ppermute | solution.py:308
  239.6 33.6 %collective-permute-start.38 = (f32[2,512,128]{2,1,0:T(8,128)}, f32[2,512,128]{2,1,0:T(8,128)}, u32[]{:S(2)}, u32[]{:S(2)}) collective-permute-start(f32[2,512,128]{2,1,0:T(8,128)} %get-tuple-element.98), channel_id=1, source_target_pairs={{0,2},{1,3},{2,0},{3,1},{4,6},{5,7},{6,4},{7,5},{8,10},{9,11},{10,... | collective-permute-start | bytes 1572872 | tf_op jit(solution)/shard_map/ppermute | solution.py:308
  249.6 38.5 %collective-permute-start.39 = (f32[2,512,128]{2,1,0:T(8,128)}, f32[2,512,128]{2,1,0:T(8,128)}, u32[]{:S(2)}, u32[]{:S(2)}) collective-permute-start(f32[2,512,128]{2,1,0:T(8,128)} %get-tuple-element.99), channel_id=1, source_target_pairs={{0,4},{1,5},{2,6},{3,7},{4,0},{5,1},{6,2},{7,3},{8,12},{9,13},{10,... | collective-permute-start | bytes 1572872 | tf_op jit(solution)/shard_map/ppermute | solution.py:308
  250.6 38.0 %collective-permute-start.40 = (f32[2,512,128]{2,1,0:T(8,128)}, f32[2,512,128]{2,1,0:T(8,128)}, u32[]{:S(2)}, u32[]{:S(2)}) collective-permute-start(f32[2,512,128]{2,1,0:T(8,128)} %get-tuple-element.100), channel_id=1, source_target_pairs={{0,6},{1,7},{2,4},{3,5},{4,2},{5,3},{6,0},{7,1},{8,14},{9,15},{10,... | collective-permute-start | bytes 1572872 | tf_op jit(solution)/shard_map/ppermute | solution.py:308
  252.0 38.1 %collective-permute-start.33 = (f32[2,512,128]{2,1,0:T(8,128)}, f32[2,512,128]{2,1,0:T(8,128)S(1)}, u32[]{:S(2)}, u32[]{:S(2)}) collective-permute-start(f32[2,512,128]{2,1,0:T(8,128)} %get-tuple-element.94.refs_0_), channel_id=1, source_target_pairs={{0,1},{1,0},{2,3},{3,2},{4,5},{5,4},{6,7},{7,6},{8,9},{9,8},{10,11... | collective-permute-start | bytes 1572872 | tf_op jit(solution)/shard_map/ppermute | solution.py:308
  288.6 25.6 %collective-permute-start.42 = (f32[2,512,128]{2,1,0:T(8,128)}, f32[2,512,128]{2,1,0:T(8,128)}, u32[]{:S(2)}, u32[]{:S(2)}) collective-permute-start(f32[2,512,128]{2,1,0:T(8,128)} %collective-permute-done.38.refs_1_), channel_id=1, source_target_pairs={{0,16},{1,17},{2,18},{3,19},{4,20},{5,21},{6,22},{7,23},{8,24},{9,... | collective-permute-start | bytes 1572872 | tf_op jit(solution)/shard_map/ppermute | solution.py:308
  290.1 33.2 %collective-permute-start.43 = (f32[2,512,128]{2,1,0:T(8,128)}, f32[2,512,128]{2,1,0:T(8,128)}, u32[]{:S(2)}, u32[]{:S(2)}) collective-permute-start(f32[2,512,128]{2,1,0:T(8,128)} %collective-permute-done.39.refs_2_), channel_id=1, source_target_pairs={{0,16},{1,17},{2,18},{3,19},{4,20},{5,21},{6,22},{7,23},{8,24},{9,... | collective-permute-start | bytes 1572872 | tf_op jit(solution)/shard_map/ppermute | solution.py:308
  290.9 38.0 %collective-permute-start.44 = (f32[2,512,128]{2,1,0:T(8,128)}, f32[2,512,128]{2,1,0:T(8,128)}, u32[]{:S(2)}, u32[]{:S(2)}) collective-permute-start(f32[2,512,128]{2,1,0:T(8,128)} %collective-permute-done.40.refs_3_), channel_id=1, source_target_pairs={{0,16},{1,17},{2,18},{3,19},{4,20},{5,21},{6,22},{7,23},{8,24},{9,... | collective-permute-start | bytes 1572872 | tf_op jit(solution)/shard_map/ppermute | solution.py:308
  333.4 34.2 %collective-permute-start.47 = (f32[4,2,512,128]{3,2,1,0:T(8,128)}, f32[4,2,512,128]{3,2,1,0:T(8,128)}, u32[]{:S(2)}, u32[]{:S(2)}) collective-permute-start(f32[4,2,512,128]{3,2,1,0:T(8,128)} %mix_stage.7.after_ref.mine_ref), channel_id=1, source_target_pairs={{0,8},{1,9},{2,10},{3,11},{4,12},{5,13},{6,14},{7,15},{8,0},{9,1},... | collective-permute-start | bytes 6291464 | tf_op jit(solution)/shard_map/ppermute | solution.py:308
  335.5 45.2 %collective-permute-start.20 = (f32[2,512,128]{2,1,0:T(8,128)}, f32[2,512,128]{2,1,0:T(8,128)S(1)}, u32[]{:S(2)}, u32[]{:S(2)}) collective-permute-start(f32[2,512,128]{2,1,0:T(8,128)} %get-tuple-element.85.after_ref), channel_id=1, source_target_pairs={{0,2},{1,3},{2,0},{3,1},{4,6},{5,7},{6,4},{7,5},{8,10},{9,11},{10,... | collective-permute-start | bytes 1572872 | tf_op jit(solution)/shard_map/ppermute | solution.py:308
  341.6 39.7 %collective-permute-start.22 = (f32[2,512,128]{2,1,0:T(8,128)}, f32[2,512,128]{2,1,0:T(8,128)S(1)}, u32[]{:S(2)}, u32[]{:S(2)}) collective-permute-start(f32[2,512,128]{2,1,0:T(8,128)} %get-tuple-element.86), channel_id=1, source_target_pairs={{0,6},{1,7},{2,4},{3,5},{4,2},{5,3},{6,0},{7,1},{8,14},{9,15},{10,... | collective-permute-start | bytes 1572872 | tf_op jit(solution)/shard_map/ppermute | solution.py:308
  348.4 52.9 %collective-permute-start.21 = (f32[2,512,128]{2,1,0:T(8,128)S(1)}, f32[2,512,128]{2,1,0:T(8,128)S(1)}, u32[]{:S(2)}, u32[]{:S(2)}) collective-permute-start(f32[2,512,128]{2,1,0:T(8,128)S(1)} %copy-done.16), channel_id=1, source_target_pairs={{0,4},{1,5},{2,6},{3,7},{4,0},{5,1},{6,2},{7,3},{8,12},{9,13},{10,... | collective-permute-start | bytes 1572872 | tf_op jit(solution)/shard_map/ppermute | solution.py:308
  359.8 43.1 %collective-permute-start.37 = (f32[2,512,128]{2,1,0:T(8,128)}, f32[2,512,128]{2,1,0:T(8,128)S(1)}, u32[]{:S(2)}, u32[]{:S(2)}) collective-permute-start(f32[2,512,128]{2,1,0:T(8,128)} %get-tuple-element.97), channel_id=1, source_target_pairs={{0,6},{1,7},{2,4},{3,5},{4,2},{5,3},{6,0},{7,1},{8,14},{9,15},{10,... | collective-permute-start | bytes 1572872 | tf_op jit(solution)/shard_map/ppermute | solution.py:308
  367.5 35.8 %collective-permute-start.48 = (f32[2,512,128]{2,1,0:T(8,128)}, f32[2,512,128]{2,1,0:T(8,128)}, u32[]{:S(2)}, u32[]{:S(2)}) collective-permute-start(f32[2,512,128]{2,1,0:T(8,128)} %get-tuple-element.105.refs_0_), channel_id=1, source_target_pairs={{0,1},{1,0},{2,3},{3,2},{4,5},{5,4},{6,7},{7,6},{8,9},{9,8},{10,11... | collective-permute-start | bytes 1572872 | tf_op jit(solution)/shard_map/ppermute | solution.py:308
  380.7 24.2 %collective-permute-start.49 = (f32[2,512,128]{2,1,0:T(8,128)S(1)}, f32[2,512,128]{2,1,0:T(8,128)S(1)}, u32[]{:S(2)}, u32[]{:S(2)}) collective-permute-start(f32[2,512,128]{2,1,0:T(8,128)S(1)} %copy-done.8), channel_id=1, source_target_pairs={{0,1},{1,0},{2,3},{3,2},{4,5},{5,4},{6,7},{7,6},{8,9},{9,8},{10,11... | collective-permute-start | bytes 1572872 | tf_op jit(solution)/shard_map/ppermute | solution.py:308
  381.3 34.4 %collective-permute-start.53 = (f32[2,512,128]{2,1,0:T(8,128)}, f32[2,512,128]{2,1,0:T(8,128)}, u32[]{:S(2)}, u32[]{:S(2)}) collective-permute-start(f32[2,512,128]{2,1,0:T(8,128)} %get-tuple-element.109.refs_0_), channel_id=1, source_target_pairs={{0,1},{1,0},{2,3},{3,2},{4,5},{5,4},{6,7},{7,6},{8,9},{9,8},{10,11... | collective-permute-start | bytes 1572872 | tf_op jit(solution)/shard_map/ppermute | solution.py:308
  402.8 26.5 %collective-permute-start.55 = (f32[2,512,128]{2,1,0:T(8,128)}, f32[2,512,128]{2,1,0:T(8,128)}, u32[]{:S(2)}, u32[]{:S(2)}) collective-permute-start(f32[2,512,128]{2,1,0:T(8,128)} %get-tuple-element.112.refs_0_), channel_id=1, source_target_pairs={{0,1},{1,0},{2,3},{3,2},{4,5},{5,4},{6,7},{7,6},{8,9},{9,8},{10,11... | collective-permute-start | bytes 1572872 | tf_op jit(solution)/shard_map/ppermute | solution.py:308
  403.3 35.3 %collective-permute-start.56 = (f32[2,512,128]{2,1,0:T(8,128)}, f32[2,512,128]{2,1,0:T(8,128)}, u32[]{:S(2)}, u32[]{:S(2)}) collective-permute-start(f32[2,512,128]{2,1,0:T(8,128)} %get-tuple-element.104.after_ref.refs_1_), channel_id=1, source_target_pairs={{0,1},{1,0},{2,3},{3,2},{4,5},{5,4},{6,7},{7,6},{8,9},{9,8},{10,11... | collective-permute-start | bytes 1572872 | tf_op jit(solution)/shard_map/ppermute | solution.py:308
  404.9 46.4 %collective-permute-start.36 = (f32[2,512,128]{2,1,0:T(8,128)}, f32[2,512,128]{2,1,0:T(8,128)S(1)}, u32[]{:S(2)}, u32[]{:S(2)}) collective-permute-start(f32[2,512,128]{2,1,0:T(8,128)} %get-tuple-element.89.after_ref), channel_id=1, source_target_pairs={{0,4},{1,5},{2,6},{3,7},{4,0},{5,1},{6,2},{7,3},{8,12},{9,13},{10,... | collective-permute-start | bytes 1572872 | tf_op jit(solution)/shard_map/ppermute | solution.py:308
  415.7 36.7 %collective-permute-start.35 = (f32[2,512,128]{2,1,0:T(8,128)}, f32[2,512,128]{2,1,0:T(8,128)S(1)}, u32[]{:S(2)}, u32[]{:S(2)}) collective-permute-start(f32[2,512,128]{2,1,0:T(8,128)} %get-tuple-element.96.after_ref), channel_id=1, source_target_pairs={{0,2},{1,3},{2,0},{3,1},{4,6},{5,7},{6,4},{7,5},{8,10},{9,11},{10,... | collective-permute-start | bytes 1572872 | tf_op jit(solution)/shard_map/ppermute | solution.py:308
  418.1 36.3 %collective-permute-start.52 = (f32[2,512,128]{2,1,0:T(8,128)}, f32[2,512,128]{2,1,0:T(8,128)}, u32[]{:S(2)}, u32[]{:S(2)}) collective-permute-start(f32[2,512,128]{2,1,0:T(8,128)} %get-tuple-element.108), channel_id=1, source_target_pairs={{0,6},{1,7},{2,4},{3,5},{4,2},{5,3},{6,0},{7,1},{8,14},{9,15},{10,... | collective-permute-start | bytes 1572872 | tf_op jit(solution)/shard_map/ppermute | solution.py:308
  429.3 69.0 %collective-permute-start.51 = (f32[2,512,128]{2,1,0:T(8,128)}, f32[2,512,128]{2,1,0:T(8,128)}, u32[]{:S(2)}, u32[]{:S(2)}) collective-permute-start(f32[2,512,128]{2,1,0:T(8,128)} %get-tuple-element.103.after_ref), channel_id=1, source_target_pairs={{0,4},{1,5},{2,6},{3,7},{4,0},{5,1},{6,2},{7,3},{8,12},{9,13},{10,... | collective-permute-start | bytes 1572872 | tf_op jit(solution)/shard_map/ppermute | solution.py:308
  438.7 59.7 %collective-permute-start.50 = (f32[2,512,128]{2,1,0:T(8,128)}, f32[2,512,128]{2,1,0:T(8,128)S(1)}, u32[]{:S(2)}, u32[]{:S(2)}) collective-permute-start(f32[2,512,128]{2,1,0:T(8,128)} %get-tuple-element.107.after_ref), channel_id=1, source_target_pairs={{0,2},{1,3},{2,0},{3,1},{4,6},{5,7},{6,4},{7,5},{8,10},{9,11},{10,... | collective-permute-start | bytes 1572872 | tf_op jit(solution)/shard_map/ppermute | solution.py:308
  451.3 64.6 %collective-permute-start.64 = (f32[2,256,128]{2,1,0:T(8,128)S(1)}, f32[2,256,128]{2,1,0:T(8,128)S(1)}, u32[]{:S(2)}, u32[]{:S(2)}) collective-permute-start(f32[2,256,128]{2,1,0:T(8,128)S(1)} %copy-done.34), channel_id=1, source_target_pairs={{0,4},{1,5},{2,6},{3,7},{4,0},{5,1},{6,2},{7,3},{8,12},{9,13},{10,... | collective-permute-start | bytes 786440 | tf_op jit(solution)/shard_map/ppermute | solution.py:308
  452.4 57.2 %collective-permute-start.61 = (f32[2,128,128]{2,1,0:T(8,128)S(1)}, f32[2,128,128]{2,1,0:T(8,128)S(1)}, u32[]{:S(2)}, u32[]{:S(2)}) collective-permute-start(f32[2,128,128]{2,1,0:T(8,128)S(1)} %copy-done.50), channel_id=1, source_target_pairs={{0,4},{1,5},{2,6},{3,7},{4,0},{5,1},{6,2},{7,3},{8,12},{9,13},{10,... | collective-permute-start | bytes 393224 | tf_op jit(solution)/shard_map/ppermute | solution.py:308
  454.4 55.9 %collective-permute-start.65 = (f32[2,256,128]{2,1,0:T(8,128)S(1)}, f32[2,256,128]{2,1,0:T(8,128)S(1)}, u32[]{:S(2)}, u32[]{:S(2)}) collective-permute-start(f32[2,256,128]{2,1,0:T(8,128)S(1)} %copy-done.48), channel_id=1, source_target_pairs={{0,6},{1,7},{2,4},{3,5},{4,2},{5,3},{6,0},{7,1},{8,14},{9,15},{10,... | collective-permute-start | bytes 786440 | tf_op jit(solution)/shard_map/ppermute | solution.py:308
  498.4 28.1 %collective-permute-start.62 = (f32[2,128,128]{2,1,0:T(8,128)}, f32[2,128,128]{2,1,0:T(8,128)S(1)}, u32[]{:S(2)}, u32[]{:S(2)}) collective-permute-start(f32[2,128,128]{2,1,0:T(8,128)} %get-tuple-element.120), channel_id=1, source_target_pairs={{0,6},{1,7},{2,4},{3,5},{4,2},{5,3},{6,0},{7,1},{8,14},{9,15},{10,... | collective-permute-start | bytes 393224 | tf_op jit(solution)/shard_map/ppermute | solution.py:308
  (70 other events, 1240.9 us)

commit v4 on v3

--- a/solution.py
+++ b/solution.py
@@ -17,6 +17,7 @@
 TILE = 128
 GROUPS = ((2, 3), (1, 0))
 
+FULL = pltpu.CompilerParams(vmem_limit_bytes=67043328)
 SCALAR = pl.BlockSpec(memory_space=pltpu.SMEM)
 ANYWHERE = pl.BlockSpec(memory_space=pl.ANY)
 WHOLE = pl.BlockSpec(memory_space=pltpu.VMEM)
@@ -75,27 +76,27 @@
     return reals, imags
 
 
-def pack_kernel(first, z_ref, re_ref, im_ref, *refs):
-    outs = refs[-SWAP:]
+def pack_kernel(first, slots, z_ref, re_ref, im_ref, *refs):
+    outs = refs[-len(slots) :]
     block, tile, lanes = re_ref.shape
     for side, ref in enumerate((re_ref, im_ref)):
         flat = ref.reshape(block * tile, lanes)
-        for slot, out_ref in enumerate(outs):
+        for slot, out_ref in zip(slots, outs):
             place = first + jnp.bitwise_xor(z_ref[0], slot)
             out_ref[side] = flat[pl.ds(place, block, stride=tile), :]
 
 
-def pack_stage(z, re, im, c, after):
+def pack_stage(z, re, im, c, slots, after):
     rows, _, lanes = re.shape
     block, tile = 256, 8
     spec = pl.BlockSpec((block, tile, lanes), lambda i: (i, c * SWAP // tile, 0))
     out = pl.BlockSpec((2, block, lanes), lambda i: (0, i, 0))
     return pl.pallas_call(
-        functools.partial(pack_kernel, c * SWAP % tile),
+        functools.partial(pack_kernel, c * SWAP % tile, slots),
         grid=(rows // block,),
         in_specs=[SCALAR, spec, spec] + [ANYWHERE] * len(after),
-        out_specs=[out] * SWAP,
-        out_shape=[jax.ShapeDtypeStruct((2, rows, lanes), jnp.float32)] * SWAP,
+        out_specs=[out] * len(slots),
+        out_shape=[jax.ShapeDtypeStruct((2, rows, lanes), jnp.float32)] * len(slots),
         cost_estimate=pl.CostEstimate(flops=40 << 20, bytes_accessed=8 << 20, transcendentals=0),
         name="pack_stage",
     )(z, re, im, *after)
@@ -132,7 +133,7 @@
 
 def mix_stage(coef, mine, theirs, listed, after):
     rows = mine[0].shape[-2]
-    block = 128
+    block = 256
     return pl.pallas_call(
         functools.partial(mix_kernel, len(mine)),
         grid=(rows // block,),
@@ -140,6 +141,7 @@
         out_specs=slot_spec(listed, block),
         out_shape=slot_shape(listed, rows),
         cost_estimate=pl.CostEstimate(flops=20 << 20, bytes_accessed=6 << 20, transcendentals=0),
+        compiler_params=FULL,
         name="mix_stage",
     )(coef, after, *mine, *theirs)
 
@@ -165,7 +167,7 @@
 
 def swap_stage(z, coef, turn, mine, theirs, listed, after):
     rows = mine.shape[-2]
-    block = 128
+    block = 256
     full = slot_spec(False, block)
     return pl.pallas_call(
         swap_kernel,
@@ -175,6 +177,7 @@
         out_shape=slot_shape(listed, rows),
         scratch_shapes=[pltpu.VMEM((SWAP, 2, block, LANES), jnp.float32)],
         cost_estimate=pl.CostEstimate(flops=30 << 20, bytes_accessed=6 << 20, transcendentals=0),
+        compiler_params=FULL,
         name="swap_stage",
     )(z, coef, turn, after, mine, theirs)
 
@@ -222,6 +225,7 @@
         out_shape=shapes,
         scratch_shapes=[pltpu.VMEM((rows, 2 * LANES), jnp.bfloat16)] * 2,
         cost_estimate=pl.CostEstimate(flops=len(slots) * (100 << 20), bytes_accessed=8 << 20, transcendentals=0),
+        compiler_params=FULL,
         name="row_stage",
     )(coef, after, *turn, *scale, table, *mine, *theirs)
     return [outs[k * len(slots) : (k + 1) * len(slots)] for k in range(len(sizes))]
@@ -281,6 +285,7 @@
         cost_estimate=pl.CostEstimate(
             flops=20 * count * part * LANES * LANES, bytes_accessed=20 * count * part * LANES, transcendentals=0
         ),
+        compiler_params=FULL,
         name="lane_stage",
     )(*arguments)
 
@@ -349,18 +354,19 @@
         chain[0] = leaf
         return result
 
-    def swap_out(arrays):
-        return [arrays[0]] + [flip(arrays[s], s * weights) for s in range(1, SWAP)]
-
     packed, inward, across, mixed, spread = {}, {}, {}, {}, {}
     parts = {k: (rows,) for k in range(SLICES)}
     parts[SLICES - 1] = (rows // 2, rows // 4, rows // 4)
     outward = {k: [[None] * SWAP for _ in sizes] for k, sizes in parts.items()}
 
     def pack(k, *after):
-        packed[k] = pack_stage(zs, re, im, k, [chain[0], *after])
-        chain[0] = packed[k][0]
-        inward[k] = swap_out(packed[k])
+        packed[k], inward[k] = [None] * SWAP, [None] * SWAP
+        for group in GROUPS if k == 0 else (sum(GROUPS, ()),):
+            pieces = pack_stage(zs, re, im, k, group, [chain[0], *after])
+            chain[0] = pieces[0]
+            for s, piece in zip(group, pieces):
+                packed[k][s] = piece
+                inward[k][s] = flip(piece, s * weights) if s else piece
         across[k] = [flip(packed[k][0], devices // 2)]
 
     def cross(k):

time: 539 us -> 535 us (level)
  waiting for transfers between devices: 263 us -> 300 us
  starting transfers between devices: 121 us -> 91.3 us
  local copies, waits for them, and re-layouts: 7.67 us -> 1.36 us
    ppermute x66, waiting for transfers between devices: 263 us -> 300 us  [flip(): lax.ppermute(values, AXES, [(i, i ^ distance) for i in range(devices)])]
    ppermute x66, starting transfers between devices: 121 us -> 91.3 us  [flip(): lax.ppermute(values, AXES, [(i, i ^ distance) for i in range(devices)])]
    unnamed x104 -> x20, local copies, waits for them, and re-layouts: 6.98 us -> 0.04 us
    pallas_call x4 -> x5, Pallas kernels: 13.8 us -> 16.6 us  [pack_stage(): pl.pallas_call(functools.partial(pack_kernel, c * SWAP % tile, slots), gr...]
  transfers between devices with their start and end apart: 66 -> 66, of which waited for: 24 -> 26; matrix products, arithmetic and copies ran while one was open for 4% -> 4% of each run, Pallas kernels for 18% -> 18%
where the time goes in v4:
time: 535 us; the launch traced here: 534 us
  waiting for transfers between devices  300 us (56%)
  Pallas kernels  116 us (22%)
  starting transfers between devices  91.3 us (17%)
  other arithmetic  22.5 us (4%)
    ppermute x66, waiting for transfers between devices, flip(): lax.ppermute(values, AXES, [(i, i ^ distance) for i in range(devices)])  300 us
    ppermute x66, starting transfers between devices, flip(): lax.ppermute(values, AXES, [(i, i ^ distance) for i in range(devices)])  91.3 us
    pallas_call x8, Pallas kernels, row_stage(): pl.pallas_call(functools.partial(row_kernel, slots, sizes), in_specs=[SCA...  53.4 us
    pallas_call x3, Pallas kernels, lane_stage(): pl.pallas_call(kernel, grid=(part // block,), in_specs=specs, out_specs=[...  17 us
    pallas_call x5, Pallas kernels, pack_stage(): pl.pallas_call(functools.partial(pack_kernel, c * SWAP % tile, slots), gr...  16.6 us
    pallas_call x4, Pallas kernels, swap_stage(): pl.pallas_call(swap_kernel, grid=(rows // block,), in_specs=[SCALAR, SCAL...  15.6 us
    pallas_call x4, Pallas kernels, mix_stage(): pl.pallas_call(functools.partial(mix_kernel, len(mine)), grid=(rows // bl...  13.4 us
    sin x4, other arithmetic, phases(): return (jnp.cos(angle), jnp.sin(angle))  12 us
  transfers between devices with their start and end apart: 66, of which 26 were waited for; matrix products, arithmetic and copies ran while one was open for 4% of the time, Pallas kernels for 18%

profile of v4, /device:TPU:0, one launch (start us, length us, event | category | flops | bytes accessed | tf_op | source)
XLA Modules:
  0.0 534.4 jit_solution(3218072172875288176)
XLA Ops:
  3.8 5.1 collective-permute-start.2
  16.2 4.2 cosine_bitcast_fusion
  24.2 5.7 %fusion.39 = (f32[512,128]{1,0:T(8,128)}, f32[512,128]{1,0:T(8,128)}, f32[512,128]{1,0:T(8,128)}, f32[512,128]{1,0:T(8,128)}, f32[512,128]{1,0:T(8,128)}, /*inde...) fusion(s32[128]{0:T(128)S(1)} %get-tuple-element.163, s32[512]{0:T(512)S(1)} %copy-done.7, ...), kind=kLoop, calls=%fused_computation.88 | loop fusion | flops 3670016 | bytes 2101248 | tf_op jit(solution)/shard_map/sin | solution.py:37
  30.3 23.5 %collective-permute-done.1.refs_2_ = f32[2,512,128]{2,1,0:T(8,128)S(1)} collective-permute-done((f32[2,512,128]{2,1,0:T(8,128)}, f32[2,512,128]{2,1,0:T(8,128)S(1)}, u32[]{:S(2)}, u32[]{:S(2)}) %collective-permute-start.1) | collective-permute-done | bytes 524320 | tf_op jit(solution)/shard_map/ppermute | solution.py:313
  55.9 5.6 %fusion.31 = (f32[512,4]{1,0:T(8,128)}, f32[512,4]{1,0:T(8,128)}, f32[512,4]{1,0:T(8,128)}, f32[512,4]{1,0:T(8,128)}, f32[512,4]{1,0:T(8,128)}, /*index=5*/f32[512,4]{1,0:T(8,128)}, f32[512,4]{1,0:T(8,128)}, f32[512,4]{1,0:T(8,128)}) fusion(s32[4]{0:T(128)S(1)} %get-tuple-element.179, s32[512]{0:T(512)S(1)} %fusion.55, s32[512]{0:T(512)S(1)} %fusion.58, ...), kind=kLoop, calls=%fused_computation.80 | loop fusion | flops 114688 | bytes 73744 | tf_op jit(solution)/shard_map/sin | solution.py:37
  61.5 3.4 pack_stage.7
  64.9 3.5 pack_stage.8
  68.4 3.4 pack_stage.9
  72.5 5.7 %collective-permute-done.4.refs_5_ = f32[2,512,128]{2,1,0:T(8,128)} collective-permute-done((f32[2,512,128]{2,1,0:T(8,128)S(1)}, f32[2,512,128]{2,1,0:T(8,128)}, u32[]{:S(2)}, u32[]{:S(2)}) %collective-permute-start.4) | collective-permute-done | bytes 524320 | tf_op jit(solution)/shard_map/ppermute | solution.py:313
  78.2 3.4 mix_stage.4.after_ref.mine_ref
  86.6 9.6 %collective-permute-done.8.refs_1_ = f32[2,512,128]{2,1,0:T(8,128)} collective-permute-done((f32[2,512,128]{2,1,0:T(8,128)}, f32[2,512,128]{2,1,0:T(8,128)}, u32[]{:S(2)}, u32[]{:S(2)}) %collective-permute-start.8) | collective-permute-done | bytes 524320 | tf_op jit(solution)/shard_map/ppermute | solution.py:313
  97.7 11.2 %collective-permute-done.10.refs_3_ = f32[2,512,128]{2,1,0:T(8,128)} collective-permute-done((f32[2,512,128]{2,1,0:T(8,128)}, f32[2,512,128]{2,1,0:T(8,128)}, u32[]{:S(2)}, u32[]{:S(2)}) %collective-permute-start.10) | collective-permute-done | bytes 524320 | tf_op jit(solution)/shard_map/ppermute | solution.py:313
  110.4 20.7 %collective-permute-done.9.refs_2_ = f32[2,512,128]{2,1,0:T(8,128)} collective-permute-done((f32[2,512,128]{2,1,0:T(8,128)}, f32[2,512,128]{2,1,0:T(8,128)}, u32[]{:S(2)}, u32[]{:S(2)}) %collective-permute-start.9) | collective-permute-done | bytes 524320 | tf_op jit(solution)/shard_map/ppermute | solution.py:313
  135.1 3.9 swap_stage.4
  139.0 5.5 %collective-permute-done.13.refs_6_ = f32[2,512,128]{2,1,0:T(8,128)} collective-permute-done((f32[2,512,128]{2,1,0:T(8,128)}, f32[2,512,128]{2,1,0:T(8,128)}, u32[]{:S(2)}, u32[]{:S(2)}) %collective-permute-start.13) | collective-permute-done | bytes 524320 | tf_op jit(solution)/shard_map/ppermute | solution.py:313
  153.9 3.9 swap_stage.5
  157.8 4.7 collective-permute-done.25.refs_1_
  164.0 11.2 %collective-permute-done.27.refs_3_ = f32[2,512,128]{2,1,0:T(8,128)} collective-permute-done((f32[2,512,128]{2,1,0:T(8,128)}, f32[2,512,128]{2,1,0:T(8,128)}, u32[]{:S(2)}, u32[]{:S(2)}) %collective-permute-start.27) | collective-permute-done | bytes 524320 | tf_op jit(solution)/shard_map/ppermute | solution.py:313
  176.7 20.7 %collective-permute-done.26.refs_2_ = f32[2,512,128]{2,1,0:T(8,128)} collective-permute-done((f32[2,512,128]{2,1,0:T(8,128)}, f32[2,512,128]{2,1,0:T(8,128)}, u32[]{:S(2)}, u32[]{:S(2)}) %collective-permute-start.26) | collective-permute-done | bytes 524320 | tf_op jit(solution)/shard_map/ppermute | solution.py:313
  203.0 9.6 %collective-permute-done.23.refs_2_ = f32[2,512,128]{2,1,0:T(8,128)} collective-permute-done((f32[2,512,128]{2,1,0:T(8,128)}, f32[2,512,128]{2,1,0:T(8,128)}, u32[]{:S(2)}, u32[]{:S(2)}) %collective-permute-start.23) | collective-permute-done | bytes 524320 | tf_op jit(solution)/shard_map/ppermute | solution.py:313
  214.7 6.8 %row_stage.8 = (f32[2,512,128]{2,1,0:T(8,128)}, f32[2,512,128]{2,1,0:T(8,128)}) custom-call(f32[9]{0:T(128)} %pad_maximum_fusion.2.coef_ref, f32[2,512,128]{2,1,0:T(8,128)} %get-tuple-element.79.after_ref.refs_1_, f32[512,4]{1,0:T(8,128)} %get-tuple-element.167.refs_4_.tc_ref, f32[512,4]{1,0:T(8,128)} %get-tuple-element.168.refs_5_.ts_ref, ...), custom_call_target="tpu_custom_call" | custom-call | flops 209715200 | bytes 8388608 | tf_op jit(solution)/shard_map/row_stage/pallas_call | solution.py:221
  221.5 6.8 %row_stage.9 = (f32[2,512,128]{2,1,0:T(8,128)}, f32[2,512,128]{2,1,0:T(8,128)}) custom-call(f32[9]{0:T(128)} %pad_maximum_fusion.2.coef_ref, f32[2,512,128]{2,1,0:T(8,128)} %get-tuple-element.82.after_ref, f32[512,4]{1,0:T(8,128)} %get-tuple-element.167.refs_4_.tc_ref, f32[512,4]{1,0:T(8,128)} %get-tuple-element.168.refs_5_.ts_ref, ...), custom_call_target="tpu_custom_call" | custom-call | flops 209715200 | bytes 8388608 | tf_op jit(solution)/shard_map/row_stage/pallas_call | solution.py:221
  228.3 6.8 %row_stage.10 = (f32[2,512,128]{2,1,0:T(8,128)}, f32[2,512,128]{2,1,0:T(8,128)}) custom-call(f32[9]{0:T(128)} %pad_maximum_fusion.2.coef_ref, f32[2,512,128]{2,1,0:T(8,128)} %get-tuple-element.85.after_ref, f32[512,4]{1,0:T(8,128)} %get-tuple-element.169.tc_ref, f32[512,4]{1,0:T(8,128)} %get-tuple-element.170.ts_ref, f32[512,128]{1,0:T(8,128)} %get-tuple-element.157.rc_ref, ...), custom_call_target="tpu_custom_call" | custom-call | flops 209715200 | bytes 8388608 | tf_op jit(solution)/shard_map/row_stage/pallas_call | solution.py:221
  237.0 9.0 %collective-permute-done.30.refs_6_ = f32[2,512,128]{2,1,0:T(8,128)} collective-permute-done((f32[2,512,128]{2,1,0:T(8,128)}, f32[2,512,128]{2,1,0:T(8,128)}, u32[]{:S(2)}, u32[]{:S(2)}) %collective-permute-start.30) | collective-permute-done | bytes 524320 | tf_op jit(solution)/shard_map/ppermute | solution.py:313
  246.0 3.3 mix_stage.6.after_ref.mine_ref
  254.5 9.6 %collective-permute-done.38.refs_1_ = f32[2,512,128]{2,1,0:T(8,128)} collective-permute-done((f32[2,512,128]{2,1,0:T(8,128)}, f32[2,512,128]{2,1,0:T(8,128)}, u32[]{:S(2)}, u32[]{:S(2)}) %collective-permute-start.38) | collective-permute-done | bytes 524320 | tf_op jit(solution)/shard_map/ppermute | solution.py:313
  265.6 10.6 %collective-permute-done.40.refs_3_ = f32[2,512,128]{2,1,0:T(8,128)} collective-permute-done((f32[2,512,128]{2,1,0:T(8,128)}, f32[2,512,128]{2,1,0:T(8,128)}, u32[]{:S(2)}, u32[]{:S(2)}) %collective-permute-start.40) | collective-permute-done | bytes 524320 | tf_op jit(solution)/shard_map/ppermute | solution.py:313
  277.7 21.3 %collective-permute-done.39.refs_2_ = f32[2,512,128]{2,1,0:T(8,128)} collective-permute-done((f32[2,512,128]{2,1,0:T(8,128)}, f32[2,512,128]{2,1,0:T(8,128)}, u32[]{:S(2)}, u32[]{:S(2)}) %collective-permute-start.39) | collective-permute-done | bytes 524320 | tf_op jit(solution)/shard_map/ppermute | solution.py:313
  302.4 3.9 swap_stage.6
  306.3 6.8 %row_stage.11 = (f32[2,512,128]{2,1,0:T(8,128)}, f32[2,512,128]{2,1,0:T(8,128)}) custom-call(f32[9]{0:T(128)} %pad_maximum_fusion.2.coef_ref, f32[2,512,128]{2,1,0:T(8,128)} %get-tuple-element.93.after_ref.refs_1_, f32[512,4]{1,0:T(8,128)} %get-tuple-element.169.tc_ref, f32[512,4]{1,0:T(8,128)} %get-tuple-element.170.ts_ref, ...), custom_call_target="tpu_custom_call" | custom-call | flops 209715200 | bytes 8388608 | tf_op jit(solution)/shard_map/row_stage/pallas_call | solution.py:221
  314.0 11.2 %collective-permute-done.44.refs_7_ = f32[2,512,128]{2,1,0:T(8,128)} collective-permute-done((f32[2,512,128]{2,1,0:T(8,128)}, f32[2,512,128]{2,1,0:T(8,128)}, u32[]{:S(2)}, u32[]{:S(2)}) %collective-permute-start.44) | collective-permute-done | bytes 524320 | tf_op jit(solution)/shard_map/ppermute | solution.py:313
  325.3 9.6 %collective-permute-done.43.refs_6_ = f32[2,512,128]{2,1,0:T(8,128)} collective-permute-done((f32[2,512,128]{2,1,0:T(8,128)}, f32[2,512,128]{2,1,0:T(8,128)}, u32[]{:S(2)}, u32[]{:S(2)}) %collective-permute-start.43) | collective-permute-done | bytes 524320 | tf_op jit(solution)/shard_map/ppermute | solution.py:313
  343.1 10.2 %collective-permute-done.45.refs_2_ = f32[2,512,128]{2,1,0:T(8,128)} collective-permute-done((f32[2,512,128]{2,1,0:T(8,128)}, f32[2,512,128]{2,1,0:T(8,128)}, u32[]{:S(2)}, u32[]{:S(2)}) %collective-permute-start.45) | collective-permute-done | bytes 524320 | tf_op jit(solution)/shard_map/ppermute | solution.py:313
  354.8 9.3 %collective-permute-done.46.refs_3_ = f32[2,512,128]{2,1,0:T(8,128)} collective-permute-done((f32[2,512,128]{2,1,0:T(8,128)}, f32[2,512,128]{2,1,0:T(8,128)}, u32[]{:S(2)}, u32[]{:S(2)}) %collective-permute-start.46) | collective-permute-done | bytes 524320 | tf_op jit(solution)/shard_map/ppermute | solution.py:313
  367.9 6.8 %row_stage.12 = (f32[2,512,128]{2,1,0:T(8,128)}, f32[2,512,128]{2,1,0:T(8,128)}) custom-call(f32[9]{0:T(128)} %pad_maximum_fusion.2.coef_ref, f32[4,2,512,128]{3,2,1,0:T(8,128)} %mix_stage.7.after_ref.mine_ref, f32[512,4]{1,0:T(8,128)} %get-tuple-element.171.tc_ref, f32[512,4]{1,0:T(8,128)} %get-tuple-element.172.ts_ref, ...), custom_call_target="tpu_custom_call" | custom-call | flops 209715200 | bytes 8388608 | tf_op jit(solution)/shard_map/row_stage/pallas_call | solution.py:221
  374.7 3.9 swap_stage.7
  380.7 20.1 %collective-permute-done.21.refs_2_ = f32[2,512,128]{2,1,0:T(8,128)} collective-permute-done((f32[2,512,128]{2,1,0:T(8,128)}, f32[2,512,128]{2,1,0:T(8,128)}, u32[]{:S(2)}, u32[]{:S(2)}) %collective-permute-start.21) | collective-permute-done | bytes 524320 | tf_op jit(solution)/shard_map/ppermute | solution.py:313
  404.3 10.8 %collective-permute-start.36 = (f32[2,512,128]{2,1,0:T(8,128)}, f32[2,512,128]{2,1,0:T(8,128)}, u32[]{:S(2)}, u32[]{:S(2)}) collective-permute-start(f32[2,512,128]{2,1,0:T(8,128)} %get-tuple-element.89.after_ref), channel_id=1, source_target_pairs={{0,4},{1,5},{2,6},{3,7},{4,0},{5,1},{6,2},{7,3},{8,12},{9,13},{10,... | collective-permute-start | bytes 1572872 | tf_op jit(solution)/shard_map/ppermute | solution.py:313
  419.1 8.0 %collective-permute-done.55.refs_2_ = f32[2,512,128]{2,1,0:T(8,128)} collective-permute-done((f32[2,512,128]{2,1,0:T(8,128)}, f32[2,512,128]{2,1,0:T(8,128)}, u32[]{:S(2)}, u32[]{:S(2)}) %collective-permute-start.55) | collective-permute-done | bytes 524320 | tf_op jit(solution)/shard_map/ppermute | solution.py:313
  428.2 6.8 %row_stage.13 = (f32[2,512,128]{2,1,0:T(8,128)}, f32[2,512,128]{2,1,0:T(8,128)}) custom-call(f32[9]{0:T(128)} %pad_maximum_fusion.2.coef_ref, f32[2,512,128]{2,1,0:T(8,128)} %get-tuple-element.104.after_ref.refs_1_, f32[512,4]{1,0:T(8,128)} %get-tuple-element.171.tc_ref, f32[512,4]{1,0:T(8,128)} %get-tuple-element.172.ts_ref, ...), custom_call_target="tpu_custom_call" | custom-call | flops 209715200 | bytes 8388608 | tf_op jit(solution)/shard_map/row_stage/pallas_call | solution.py:221
  437.7 6.4 %row_stage.14 = (f32[2,256,128]{2,1,0:T(8,128)}, f32[2,256,128]{2,1,0:T(8,128)}, f32[2,128,128]{2,1,0:T(8,128)}, f32[2,128,128]{2,1,0:T(8,128)}, f32[2,128,128]{2,1,0:T(8,128)}, /*index=5*/f32[2,128,128]{2,1,0:T(8,128)}) custom-call(f32[9]{0:T(128)} %pad_maximum_fusion.2.coef_ref, f32[2,512,128]{2,1,0:T(8,128)} %get-tuple-element.107.after_ref, ...), custom_call_target="tpu_custom_call" | custom-call | flops 209715200 | bytes 8388608 | tf_op jit(solution)/shard_map/row_stage/pallas_call | solution.py:221
  444.1 6.2 %row_stage.15 = (f32[2,256,128]{2,1,0:T(8,128)}, f32[2,256,128]{2,1,0:T(8,128)}, f32[2,128,128]{2,1,0:T(8,128)}, f32[2,128,128]{2,1,0:T(8,128)}, f32[2,128,128]{2,1,0:T(8,128)}, /*index=5*/f32[2,128,128]{2,1,0:T(8,128)}) custom-call(f32[9]{0:T(128)} %pad_maximum_fusion.2.coef_ref, f32[2,256,128]{2,1,0:T(8,128)} %get-tuple-element.111.after_ref, ...), custom_call_target="tpu_custom_call" | custom-call | flops 209715200 | bytes 8388608 | tf_op jit(solution)/shard_map/row_stage/pallas_call | solution.py:221
  454.6 43.8 %collective-permute-done.51.refs_10_ = f32[2,512,128]{2,1,0:T(8,128)} collective-permute-done((f32[2,512,128]{2,1,0:T(8,128)}, f32[2,512,128]{2,1,0:T(8,128)}, u32[]{:S(2)}, u32[]{:S(2)}) %collective-permute-start.51) | collective-permute-done | bytes 524320 | tf_op jit(solution)/shard_map/ppermute | solution.py:313
  500.3 9.2 %collective-permute-done.61.refs_14_ = f32[2,128,128]{2,1,0:T(8,128)} collective-permute-done((f32[2,128,128]{2,1,0:T(8,128)}, f32[2,128,128]{2,1,0:T(8,128)}, u32[]{:S(2)}, u32[]{:S(2)}) %collective-permute-start.61) | collective-permute-done | bytes 131104 | tf_op jit(solution)/shard_map/ppermute | solution.py:313
  510.3 5.4 %collective-permute-start.58 = (f32[2,128,128]{2,1,0:T(8,128)}, f32[2,128,128]{2,1,0:T(8,128)}, u32[]{:S(2)}, u32[]{:S(2)}) collective-permute-start(f32[2,128,128]{2,1,0:T(8,128)} %get-tuple-element.115), channel_id=1, source_target_pairs={{0,4},{1,5},{2,6},{3,7},{4,0},{5,1},{6,2},{7,3},{8,12},{9,13},{10,... | collective-permute-start | bytes 393224 | tf_op jit(solution)/shard_map/ppermute | solution.py:313
  517.2 7.6 %lane_stage.3 = (f32[512,16,128]{2,1,0:T(8,128)}, f32[512,16,128]{2,1,0:T(8,128)}, f32[512,16,128]{2,1,0:T(8,128)}) custom-call(s32[1]{0:T(128)} %bitcast.z_ref.refs_0_, f32[16,128]{1,0:T(8,128)} %get-tuple-element.178.jc_ref, f32[16,128]{1,0:T(8,128)} %get-tuple-element.177.js_ref, bf16[2,256,256]{2,1,0:T(8,128)(2,1)} %constant.226.table_ref, ...), custom_call_target="tpu_custom_call" | custom-call | flops 1342177280 | bytes 10485760 | tf_op jit(solution)/shard_map/lane_stage/pallas_call | solution.py:277
  524.8 4.7 lane_stage.4
  529.6 4.7 lane_stage.5
  (152 shorter events, 96.9 us)
Async XLA Ops:
  3.8 26.1 %collective-permute-start.2 = (f32[2,512,128]{2,1,0:T(8,128)}, f32[2,512,128]{2,1,0:T(8,128)S(1)}, u32[]{:S(2)}, u32[]{:S(2)}) collective-permute-start(f32[2,512,128]{2,1,0:T(8,128)} %get-tuple-element.74), channel_id=1, source_target_pairs={{0,6},{1,7},{2,4},{3,5},{4,2},{5,3},{6,0},{7,1},{8,14},{9,15},{10,... | collective-permute-start | bytes 1572872 | tf_op jit(solution)/shard_map/ppermute | solution.py:313
  8.8 45.0 %collective-permute-start.1 = (f32[2,512,128]{2,1,0:T(8,128)}, f32[2,512,128]{2,1,0:T(8,128)S(1)}, u32[]{:S(2)}, u32[]{:S(2)}) collective-permute-start(f32[2,512,128]{2,1,0:T(8,128)} %get-tuple-element.68.refs_0_), channel_id=1, source_target_pairs={{0,4},{1,5},{2,6},{3,7},{4,0},{5,1},{6,2},{7,3},{8,12},{9,13},{10,... | collective-permute-start | bytes 1572872 | tf_op jit(solution)/shard_map/ppermute | solution.py:313
  12.0 43.4 %collective-permute-start = (f32[2,512,128]{2,1,0:T(8,128)}, f32[2,512,128]{2,1,0:T(8,128)S(1)}, u32[]{:S(2)}, u32[]{:S(2)}) collective-permute-start(f32[2,512,128]{2,1,0:T(8,128)} %get-tuple-element.69.refs_0_), channel_id=1, source_target_pairs={{0,2},{1,3},{2,0},{3,1},{4,6},{5,7},{6,4},{7,5},{8,10},{9,11},{10,... | collective-permute-start | bytes 1572872 | tf_op jit(solution)/shard_map/ppermute | solution.py:313
  12.6 59.8 %collective-permute-start.3 = (f32[2,512,128]{2,1,0:T(8,128)}, f32[2,512,128]{2,1,0:T(8,128)S(1)}, u32[]{:S(2)}, u32[]{:S(2)}) collective-permute-start(f32[2,512,128]{2,1,0:T(8,128)} %get-tuple-element.73.refs_0_), channel_id=1, source_target_pairs={{0,16},{1,17},{2,18},{3,19},{4,20},{5,21},{6,22},{7,23},{8,24},{9,... | collective-permute-start | bytes 1572872 | tf_op jit(solution)/shard_map/ppermute | solution.py:313
  29.9 42.5 %collective-permute-start.6 = (f32[2,512,128]{2,1,0:T(8,128)S(1)}, f32[2,512,128]{2,1,0:T(8,128)S(1)}, u32[]{:S(2)}, u32[]{:S(2)}) collective-permute-start(f32[2,512,128]{2,1,0:T(8,128)S(1)} %collective-permute-done.2.refs_3_), channel_id=1, source_target_pairs={{0,16},{1,17},{2,18},{3,19},{4,20},{5,21},{6,22},{7,23},{8,24},{9,... | collective-permute-start | bytes 1572872 | tf_op jit(solution)/shard_map/ppermute | solution.py:313
  81.5 53.6 %collective-permute-start.7 = (f32[4,2,512,128]{3,2,1,0:T(8,128)}, f32[4,2,512,128]{3,2,1,0:T(8,128)}, u32[]{:S(2)}, u32[]{:S(2)}) collective-permute-start(f32[4,2,512,128]{3,2,1,0:T(8,128)} %mix_stage.4.after_ref.mine_ref), channel_id=1, source_target_pairs={{0,8},{1,9},{2,10},{3,11},{4,12},{5,13},{6,14},{7,15},{8,0},{9,1},... | collective-permute-start | bytes 6291464 | tf_op jit(solution)/shard_map/ppermute | solution.py:313
  82.2 26.7 %collective-permute-start.10 = (f32[2,512,128]{2,1,0:T(8,128)}, f32[2,512,128]{2,1,0:T(8,128)}, u32[]{:S(2)}, u32[]{:S(2)}) collective-permute-start(f32[2,512,128]{2,1,0:T(8,128)} %get-tuple-element.78), channel_id=1, source_target_pairs={{0,6},{1,7},{2,4},{3,5},{4,2},{5,3},{6,0},{7,1},{8,14},{9,15},{10,... | collective-permute-start | bytes 1572872 | tf_op jit(solution)/shard_map/ppermute | solution.py:313
  84.5 46.6 %collective-permute-start.9 = (f32[2,512,128]{2,1,0:T(8,128)}, f32[2,512,128]{2,1,0:T(8,128)}, u32[]{:S(2)}, u32[]{:S(2)}) collective-permute-start(f32[2,512,128]{2,1,0:T(8,128)} %get-tuple-element.70.refs_0_), channel_id=1, source_target_pairs={{0,4},{1,5},{2,6},{3,7},{4,0},{5,1},{6,2},{7,3},{8,12},{9,13},{10,... | collective-permute-start | bytes 1572872 | tf_op jit(solution)/shard_map/ppermute | solution.py:313
  85.1 53.9 %collective-permute-start.11 = (f32[2,512,128]{2,1,0:T(8,128)}, f32[2,512,128]{2,1,0:T(8,128)}, u32[]{:S(2)}, u32[]{:S(2)}) collective-permute-start(f32[2,512,128]{2,1,0:T(8,128)} %get-tuple-element.76.refs_0_), channel_id=1, source_target_pairs={{0,16},{1,17},{2,18},{3,19},{4,20},{5,21},{6,22},{7,23},{8,24},{9,... | collective-permute-start | bytes 1572872 | tf_op jit(solution)/shard_map/ppermute | solution.py:313
  96.2 42.8 %collective-permute-start.12 = (f32[2,512,128]{2,1,0:T(8,128)}, f32[2,512,128]{2,1,0:T(8,128)}, u32[]{:S(2)}, u32[]{:S(2)}) collective-permute-start(f32[2,512,128]{2,1,0:T(8,128)} %collective-permute-done.8.refs_1_), channel_id=1, source_target_pairs={{0,16},{1,17},{2,18},{3,19},{4,20},{5,21},{6,22},{7,23},{8,24},{9,... | collective-permute-start | bytes 1572872 | tf_op jit(solution)/shard_map/ppermute | solution.py:313
  108.9 30.1 %collective-permute-start.14 = (f32[2,512,128]{2,1,0:T(8,128)}, f32[2,512,128]{2,1,0:T(8,128)}, u32[]{:S(2)}, u32[]{:S(2)}) collective-permute-start(f32[2,512,128]{2,1,0:T(8,128)} %collective-permute-done.10.refs_3_), channel_id=1, source_target_pairs={{0,16},{1,17},{2,18},{3,19},{4,20},{5,21},{6,22},{7,23},{8,24},{9,... | collective-permute-start | bytes 1572872 | tf_op jit(solution)/shard_map/ppermute | solution.py:313
  148.0 27.3 %collective-permute-start.27 = (f32[2,512,128]{2,1,0:T(8,128)}, f32[2,512,128]{2,1,0:T(8,128)}, u32[]{:S(2)}, u32[]{:S(2)}) collective-permute-start(f32[2,512,128]{2,1,0:T(8,128)} %get-tuple-element.92), channel_id=1, source_target_pairs={{0,6},{1,7},{2,4},{3,5},{4,2},{5,3},{6,0},{7,1},{8,14},{9,15},{10,... | collective-permute-start | bytes 1572872 | tf_op jit(solution)/shard_map/ppermute | solution.py:313
  150.8 46.6 %collective-permute-start.26 = (f32[2,512,128]{2,1,0:T(8,128)}, f32[2,512,128]{2,1,0:T(8,128)}, u32[]{:S(2)}, u32[]{:S(2)}) collective-permute-start(f32[2,512,128]{2,1,0:T(8,128)} %get-tuple-element.71.refs_0_), channel_id=1, source_target_pairs={{0,4},{1,5},{2,6},{3,7},{4,0},{5,1},{6,2},{7,3},{8,12},{9,13},{10,... | collective-permute-start | bytes 1572872 | tf_op jit(solution)/shard_map/ppermute | solution.py:313
  151.4 47.5 %collective-permute-start.16 = (f32[2,512,128]{2,1,0:T(8,128)}, f32[2,512,128]{2,1,0:T(8,128)}, u32[]{:S(2)}, u32[]{:S(2)}) collective-permute-start(f32[2,512,128]{2,1,0:T(8,128)} %get-tuple-element.80.refs_0_), channel_id=1, source_target_pairs={{0,1},{1,0},{2,3},{3,2},{4,5},{5,4},{6,7},{7,6},{8,9},{9,8},{10,11... | collective-permute-start | bytes 1572872 | tf_op jit(solution)/shard_map/ppermute | solution.py:313
  153.0 46.5 %collective-permute-start.17 = (f32[2,512,128]{2,1,0:T(8,128)}, f32[2,512,128]{2,1,0:T(8,128)}, u32[]{:S(2)}, u32[]{:S(2)}) collective-permute-start(f32[2,512,128]{2,1,0:T(8,128)} %get-tuple-element.81.refs_1_), channel_id=1, source_target_pairs={{0,1},{1,0},{2,3},{3,2},{4,5},{5,4},{6,7},{7,6},{8,9},{9,8},{10,11... | collective-permute-start | bytes 1572872 | tf_op jit(solution)/shard_map/ppermute | solution.py:313
  162.5 38.4 %collective-permute-start.18 = (f32[2,512,128]{2,1,0:T(8,128)}, f32[2,512,128]{2,1,0:T(8,128)}, u32[]{:S(2)}, u32[]{:S(2)}) collective-permute-start(f32[2,512,128]{2,1,0:T(8,128)} %get-tuple-element.83.refs_0_), channel_id=1, source_target_pairs={{0,1},{1,0},{2,3},{3,2},{4,5},{5,4},{6,7},{7,6},{8,9},{9,8},{10,11... | collective-permute-start | bytes 1572872 | tf_op jit(solution)/shard_map/ppermute | solution.py:313
  175.2 26.3 %collective-permute-start.19 = (f32[2,512,128]{2,1,0:T(8,128)}, f32[2,512,128]{2,1,0:T(8,128)}, u32[]{:S(2)}, u32[]{:S(2)}) collective-permute-start(f32[2,512,128]{2,1,0:T(8,128)} %get-tuple-element.75.after_ref.refs_1_), channel_id=1, source_target_pairs={{0,1},{1,0},{2,3},{3,2},{4,5},{5,4},{6,7},{7,6},{8,9},{9,8},{10,11... | collective-permute-start | bytes 1572872 | tf_op jit(solution)/shard_map/ppermute | solution.py:313
  198.9 29.4 %collective-permute-start.24 = (f32[2,512,128]{2,1,0:T(8,128)}, f32[2,512,128]{2,1,0:T(8,128)}, u32[]{:S(2)}, u32[]{:S(2)}) collective-permute-start(f32[2,512,128]{2,1,0:T(8,128)} %get-tuple-element.88.refs_1_), channel_id=1, source_target_pairs={{0,1},{1,0},{2,3},{3,2},{4,5},{5,4},{6,7},{7,6},{8,9},{9,8},{10,11... | collective-permute-start | bytes 1572872 | tf_op jit(solution)/shard_map/ppermute | solution.py:313
  199.5 35.7 %collective-permute-start.28 = (f32[2,512,128]{2,1,0:T(8,128)}, f32[2,512,128]{2,1,0:T(8,128)}, u32[]{:S(2)}, u32[]{:S(2)}) collective-permute-start(f32[2,512,128]{2,1,0:T(8,128)} %get-tuple-element.90.refs_0_), channel_id=1, source_target_pairs={{0,16},{1,17},{2,18},{3,19},{4,20},{5,21},{6,22},{7,23},{8,24},{9,... | collective-permute-start | bytes 1572872 | tf_op jit(solution)/shard_map/ppermute | solution.py:313
  200.9 34.2 %collective-permute-start.29 = (f32[2,512,128]{2,1,0:T(8,128)}, f32[2,512,128]{2,1,0:T(8,128)}, u32[]{:S(2)}, u32[]{:S(2)}) collective-permute-start(f32[2,512,128]{2,1,0:T(8,128)} %collective-permute-done.25.refs_1_), channel_id=1, source_target_pairs={{0,16},{1,17},{2,18},{3,19},{4,20},{5,21},{6,22},{7,23},{8,24},{9,... | collective-permute-start | bytes 1572872 | tf_op jit(solution)/shard_map/ppermute | solution.py:313
  201.5 35.5 %collective-permute-start.31 = (f32[2,512,128]{2,1,0:T(8,128)}, f32[2,512,128]{2,1,0:T(8,128)}, u32[]{:S(2)}, u32[]{:S(2)}) collective-permute-start(f32[2,512,128]{2,1,0:T(8,128)} %collective-permute-done.27.refs_3_), channel_id=1, source_target_pairs={{0,16},{1,17},{2,18},{3,19},{4,20},{5,21},{6,22},{7,23},{8,24},{9,... | collective-permute-start | bytes 1572872 | tf_op jit(solution)/shard_map/ppermute | solution.py:313
  212.5 33.5 %collective-permute-start.30 = (f32[2,512,128]{2,1,0:T(8,128)}, f32[2,512,128]{2,1,0:T(8,128)}, u32[]{:S(2)}, u32[]{:S(2)}) collective-permute-start(f32[2,512,128]{2,1,0:T(8,128)} %collective-permute-done.26.refs_2_), channel_id=1, source_target_pairs={{0,16},{1,17},{2,18},{3,19},{4,20},{5,21},{6,22},{7,23},{8,24},{9,... | collective-permute-start | bytes 1572872 | tf_op jit(solution)/shard_map/ppermute | solution.py:313
  249.4 51.6 %collective-permute-start.32 = (f32[4,2,512,128]{3,2,1,0:T(8,128)}, f32[4,2,512,128]{3,2,1,0:T(8,128)}, u32[]{:S(2)}, u32[]{:S(2)}) collective-permute-start(f32[4,2,512,128]{3,2,1,0:T(8,128)} %mix_stage.6.after_ref.mine_ref), channel_id=1, source_target_pairs={{0,8},{1,9},{2,10},{3,11},{4,12},{5,13},{6,14},{7,15},{8,0},{9,1},... | collective-permute-start | bytes 6291464 | tf_op jit(solution)/shard_map/ppermute | solution.py:313
  249.5 26.7 %collective-permute-start.40 = (f32[2,512,128]{2,1,0:T(8,128)}, f32[2,512,128]{2,1,0:T(8,128)}, u32[]{:S(2)}, u32[]{:S(2)}) collective-permute-start(f32[2,512,128]{2,1,0:T(8,128)} %get-tuple-element.100), channel_id=1, source_target_pairs={{0,6},{1,7},{2,4},{3,5},{4,2},{5,3},{6,0},{7,1},{8,14},{9,15},{10,... | collective-permute-start | bytes 1572872 | tf_op jit(solution)/shard_map/ppermute | solution.py:313
  251.8 47.1 %collective-permute-start.39 = (f32[2,512,128]{2,1,0:T(8,128)}, f32[2,512,128]{2,1,0:T(8,128)}, u32[]{:S(2)}, u32[]{:S(2)}) collective-permute-start(f32[2,512,128]{2,1,0:T(8,128)} %get-tuple-element.72.after_ref), channel_id=1, source_target_pairs={{0,4},{1,5},{2,6},{3,7},{4,0},{5,1},{6,2},{7,3},{8,12},{9,13},{10,... | collective-permute-start | bytes 1572872 | tf_op jit(solution)/shard_map/ppermute | solution.py:313
  252.9 47.5 %collective-permute-start.33 = (f32[2,512,128]{2,1,0:T(8,128)}, f32[2,512,128]{2,1,0:T(8,128)}, u32[]{:S(2)}, u32[]{:S(2)}) collective-permute-start(f32[2,512,128]{2,1,0:T(8,128)} %get-tuple-element.94.refs_0_), channel_id=1, source_target_pairs={{0,1},{1,0},{2,3},{3,2},{4,5},{5,4},{6,7},{7,6},{8,9},{9,8},{10,11... | collective-permute-start | bytes 1572872 | tf_op jit(solution)/shard_map/ppermute | solution.py:313
  264.0 42.3 %collective-permute-start.34 = (f32[2,512,128]{2,1,0:T(8,128)}, f32[2,512,128]{2,1,0:T(8,128)}, u32[]{:S(2)}, u32[]{:S(2)}) collective-permute-start(f32[2,512,128]{2,1,0:T(8,128)} %get-tuple-element.79.after_ref.refs_1_), channel_id=1, source_target_pairs={{0,1},{1,0},{2,3},{3,2},{4,5},{5,4},{6,7},{7,6},{8,9},{9,8},{10,11... | collective-permute-start | bytes 1572872 | tf_op jit(solution)/shard_map/ppermute | solution.py:313
  276.2 37.0 %collective-permute-start.41 = (f32[2,512,128]{2,1,0:T(8,128)}, f32[2,512,128]{2,1,0:T(8,128)}, u32[]{:S(2)}, u32[]{:S(2)}) collective-permute-start(f32[2,512,128]{2,1,0:T(8,128)} %get-tuple-element.98.refs_0_), channel_id=1, source_target_pairs={{0,16},{1,17},{2,18},{3,19},{4,20},{5,21},{6,22},{7,23},{8,24},{9,... | collective-permute-start | bytes 1572872 | tf_op jit(solution)/shard_map/ppermute | solution.py:313
  300.4 24.9 %collective-permute-start.44 = (f32[2,512,128]{2,1,0:T(8,128)}, f32[2,512,128]{2,1,0:T(8,128)}, u32[]{:S(2)}, u32[]{:S(2)}) collective-permute-start(f32[2,512,128]{2,1,0:T(8,128)} %collective-permute-done.40.refs_3_), channel_id=1, source_target_pairs={{0,16},{1,17},{2,18},{3,19},{4,20},{5,21},{6,22},{7,23},{8,24},{9,... | collective-permute-start | bytes 1572872 | tf_op jit(solution)/shard_map/ppermute | solution.py:313
  301.0 33.9 %collective-permute-start.43 = (f32[2,512,128]{2,1,0:T(8,128)}, f32[2,512,128]{2,1,0:T(8,128)}, u32[]{:S(2)}, u32[]{:S(2)}) collective-permute-start(f32[2,512,128]{2,1,0:T(8,128)} %collective-permute-done.39.refs_2_), channel_id=1, source_target_pairs={{0,16},{1,17},{2,18},{3,19},{4,20},{5,21},{6,22},{7,23},{8,24},{9,... | collective-permute-start | bytes 1572872 | tf_op jit(solution)/shard_map/ppermute | solution.py:313
  338.2 28.2 %collective-permute-start.47 = (f32[4,2,512,128]{3,2,1,0:T(8,128)}, f32[4,2,512,128]{3,2,1,0:T(8,128)}, u32[]{:S(2)}, u32[]{:S(2)}) collective-permute-start(f32[4,2,512,128]{3,2,1,0:T(8,128)} %mix_stage.7.after_ref.mine_ref), channel_id=1, source_target_pairs={{0,8},{1,9},{2,10},{3,11},{4,12},{5,13},{6,14},{7,15},{8,0},{9,1},... | collective-permute-start | bytes 6291464 | tf_op jit(solution)/shard_map/ppermute | solution.py:313
  340.3 38.3 %collective-permute-start.20 = (f32[2,512,128]{2,1,0:T(8,128)}, f32[2,512,128]{2,1,0:T(8,128)}, u32[]{:S(2)}, u32[]{:S(2)}) collective-permute-start(f32[2,512,128]{2,1,0:T(8,128)} %get-tuple-element.85.after_ref), channel_id=1, source_target_pairs={{0,2},{1,3},{2,0},{3,1},{4,6},{5,7},{6,4},{7,5},{8,10},{9,11},{10,... | collective-permute-start | bytes 1572872 | tf_op jit(solution)/shard_map/ppermute | solution.py:313
  340.3 38.9 %collective-permute-start.22 = (f32[2,512,128]{2,1,0:T(8,128)}, f32[2,512,128]{2,1,0:T(8,128)}, u32[]{:S(2)}, u32[]{:S(2)}) collective-permute-start(f32[2,512,128]{2,1,0:T(8,128)} %get-tuple-element.86), channel_id=1, source_target_pairs={{0,6},{1,7},{2,4},{3,5},{4,2},{5,3},{6,0},{7,1},{8,14},{9,15},{10,... | collective-permute-start | bytes 1572872 | tf_op jit(solution)/shard_map/ppermute | solution.py:313
  353.4 47.4 %collective-permute-start.21 = (f32[2,512,128]{2,1,0:T(8,128)}, f32[2,512,128]{2,1,0:T(8,128)}, u32[]{:S(2)}, u32[]{:S(2)}) collective-permute-start(f32[2,512,128]{2,1,0:T(8,128)} %get-tuple-element.82.after_ref), channel_id=1, source_target_pairs={{0,4},{1,5},{2,6},{3,7},{4,0},{5,1},{6,2},{7,3},{8,12},{9,13},{10,... | collective-permute-start | bytes 1572872 | tf_op jit(solution)/shard_map/ppermute | solution.py:313
  364.1 38.2 %collective-permute-start.37 = (f32[2,512,128]{2,1,0:T(8,128)}, f32[2,512,128]{2,1,0:T(8,128)}, u32[]{:S(2)}, u32[]{:S(2)}) collective-permute-start(f32[2,512,128]{2,1,0:T(8,128)} %get-tuple-element.97), channel_id=1, source_target_pairs={{0,6},{1,7},{2,4},{3,5},{4,2},{5,3},{6,0},{7,1},{8,14},{9,15},{10,... | collective-permute-start | bytes 1572872 | tf_op jit(solution)/shard_map/ppermute | solution.py:313
  366.4 36.4 %collective-permute-start.48 = (f32[2,512,128]{2,1,0:T(8,128)}, f32[2,512,128]{2,1,0:T(8,128)}, u32[]{:S(2)}, u32[]{:S(2)}) collective-permute-start(f32[2,512,128]{2,1,0:T(8,128)} %get-tuple-element.105.refs_0_), channel_id=1, source_target_pairs={{0,1},{1,0},{2,3},{3,2},{4,5},{5,4},{6,7},{7,6},{8,9},{9,8},{10,11... | collective-permute-start | bytes 1572872 | tf_op jit(solution)/shard_map/ppermute | solution.py:313
  378.6 25.7 %collective-permute-start.49 = (f32[2,512,128]{2,1,0:T(8,128)}, f32[2,512,128]{2,1,0:T(8,128)}, u32[]{:S(2)}, u32[]{:S(2)}) collective-permute-start(f32[2,512,128]{2,1,0:T(8,128)} %get-tuple-element.93.after_ref.refs_1_), channel_id=1, source_target_pairs={{0,1},{1,0},{2,3},{3,2},{4,5},{5,4},{6,7},{7,6},{8,9},{9,8},{10,11... | collective-permute-start | bytes 1572872 | tf_op jit(solution)/shard_map/ppermute | solution.py:313
  379.2 35.9 %collective-permute-start.53 = (f32[2,512,128]{2,1,0:T(8,128)}, f32[2,512,128]{2,1,0:T(8,128)}, u32[]{:S(2)}, u32[]{:S(2)}) collective-permute-start(f32[2,512,128]{2,1,0:T(8,128)} %get-tuple-element.109.refs_0_), channel_id=1, source_target_pairs={{0,1},{1,0},{2,3},{3,2},{4,5},{5,4},{6,7},{7,6},{8,9},{9,8},{10,11... | collective-permute-start | bytes 1572872 | tf_op jit(solution)/shard_map/ppermute | solution.py:313
  402.8 34.0 %collective-permute-start.56 = (f32[2,512,128]{2,1,0:T(8,128)}, f32[2,512,128]{2,1,0:T(8,128)}, u32[]{:S(2)}, u32[]{:S(2)}) collective-permute-start(f32[2,512,128]{2,1,0:T(8,128)} %get-tuple-element.104.after_ref.refs_1_), channel_id=1, source_target_pairs={{0,1},{1,0},{2,3},{3,2},{4,5},{5,4},{6,7},{7,6},{8,9},{9,8},{10,11... | collective-permute-start | bytes 1572872 | tf_op jit(solution)/shard_map/ppermute | solution.py:313
  404.3 45.9 %collective-permute-start.36 = (f32[2,512,128]{2,1,0:T(8,128)}, f32[2,512,128]{2,1,0:T(8,128)}, u32[]{:S(2)}, u32[]{:S(2)}) collective-permute-start(f32[2,512,128]{2,1,0:T(8,128)} %get-tuple-element.89.after_ref), channel_id=1, source_target_pairs={{0,4},{1,5},{2,6},{3,7},{4,0},{5,1},{6,2},{7,3},{8,12},{9,13},{10,... | collective-permute-start | bytes 1572872 | tf_op jit(solution)/shard_map/ppermute | solution.py:313
  415.1 36.4 %collective-permute-start.35 = (f32[2,512,128]{2,1,0:T(8,128)}, f32[2,512,128]{2,1,0:T(8,128)}, u32[]{:S(2)}, u32[]{:S(2)}) collective-permute-start(f32[2,512,128]{2,1,0:T(8,128)} %get-tuple-element.96.after_ref), channel_id=1, source_target_pairs={{0,2},{1,3},{2,0},{3,1},{4,6},{5,7},{6,4},{7,5},{8,10},{9,11},{10,... | collective-permute-start | bytes 1572872 | tf_op jit(solution)/shard_map/ppermute | solution.py:313
  415.9 37.4 %collective-permute-start.52 = (f32[2,512,128]{2,1,0:T(8,128)}, f32[2,512,128]{2,1,0:T(8,128)}, u32[]{:S(2)}, u32[]{:S(2)}) collective-permute-start(f32[2,512,128]{2,1,0:T(8,128)} %get-tuple-element.108), channel_id=1, source_target_pairs={{0,6},{1,7},{2,4},{3,5},{4,2},{5,3},{6,0},{7,1},{8,14},{9,15},{10,... | collective-permute-start | bytes 1572872 | tf_op jit(solution)/shard_map/ppermute | solution.py:313
  427.1 71.2 %collective-permute-start.51 = (f32[2,512,128]{2,1,0:T(8,128)}, f32[2,512,128]{2,1,0:T(8,128)}, u32[]{:S(2)}, u32[]{:S(2)}) collective-permute-start(f32[2,512,128]{2,1,0:T(8,128)} %get-tuple-element.103.after_ref), channel_id=1, source_target_pairs={{0,4},{1,5},{2,6},{3,7},{4,0},{5,1},{6,2},{7,3},{8,12},{9,13},{10,... | collective-permute-start | bytes 1572872 | tf_op jit(solution)/shard_map/ppermute | solution.py:313
  436.8 62.2 %collective-permute-start.50 = (f32[2,512,128]{2,1,0:T(8,128)}, f32[2,512,128]{2,1,0:T(8,128)}, u32[]{:S(2)}, u32[]{:S(2)}) collective-permute-start(f32[2,512,128]{2,1,0:T(8,128)} %get-tuple-element.107.after_ref), channel_id=1, source_target_pairs={{0,2},{1,3},{2,0},{3,1},{4,6},{5,7},{6,4},{7,5},{8,10},{9,11},{10,... | collective-permute-start | bytes 1572872 | tf_op jit(solution)/shard_map/ppermute | solution.py:313
  450.3 65.4 %collective-permute-start.64 = (f32[2,256,128]{2,1,0:T(8,128)}, f32[2,256,128]{2,1,0:T(8,128)}, u32[]{:S(2)}, u32[]{:S(2)}) collective-permute-start(f32[2,256,128]{2,1,0:T(8,128)} %get-tuple-element.111.after_ref), channel_id=1, source_target_pairs={{0,4},{1,5},{2,6},{3,7},{4,0},{5,1},{6,2},{7,3},{8,12},{9,13},{10,... | collective-permute-start | bytes 786440 | tf_op jit(solution)/shard_map/ppermute | solution.py:313
  451.5 58.0 %collective-permute-start.61 = (f32[2,128,128]{2,1,0:T(8,128)}, f32[2,128,128]{2,1,0:T(8,128)}, u32[]{:S(2)}, u32[]{:S(2)}) collective-permute-start(f32[2,128,128]{2,1,0:T(8,128)} %get-tuple-element.119), channel_id=1, source_target_pairs={{0,4},{1,5},{2,6},{3,7},{4,0},{5,1},{6,2},{7,3},{8,12},{9,13},{10,... | collective-permute-start | bytes 393224 | tf_op jit(solution)/shard_map/ppermute | solution.py:313
  453.3 57.0 %collective-permute-start.65 = (f32[2,256,128]{2,1,0:T(8,128)}, f32[2,256,128]{2,1,0:T(8,128)}, u32[]{:S(2)}, u32[]{:S(2)}) collective-permute-start(f32[2,256,128]{2,1,0:T(8,128)} %get-tuple-element.123), channel_id=1, source_target_pairs={{0,6},{1,7},{2,4},{3,5},{4,2},{5,3},{6,0},{7,1},{8,14},{9,15},{10,... | collective-permute-start | bytes 786440 | tf_op jit(solution)/shard_map/ppermute | solution.py:313
  499.0 25.8 %collective-permute-start.62 = (f32[2,128,128]{2,1,0:T(8,128)}, f32[2,128,128]{2,1,0:T(8,128)}, u32[]{:S(2)}, u32[]{:S(2)}) collective-permute-start(f32[2,128,128]{2,1,0:T(8,128)} %get-tuple-element.120), channel_id=1, source_target_pairs={{0,6},{1,7},{2,4},{3,5},{4,2},{5,3},{6,0},{7,1},{8,14},{9,15},{10,... | collective-permute-start | bytes 393224 | tf_op jit(solution)/shard_map/ppermute | solution.py:313
  (28 other events, 387.3 us)
